TPU v7x, 32 devices: a whole 2x2x4 slice. The times are simulated.
32 devices in a mesh: shard: 16 (over z, x, core), task: 2 (over y).
Axes of the slice: x: 2, y: 2, z: 4, core: 2. Of those that a mesh axis runs over, the one named last changes fastest.
Arguments:
- task_deltas: bfloat16 [2, 4, 256, 16384], P('task', None, 'shard')
- rank_scores: int32 [2, 4, 256, 16384], P('task', None, 'shard'), may hold values from 0 to 1073741823
- keep_limits: int32 [2, 4, 8], P('task'), may hold values from 268435456 to 805306367
Outputs:
- merged: bfloat16 [4, 256, 16384], P(None, 'shard', 'task')
All inputs are finite; a program needn't handle non-finite values.
Results may differ from a plain program's by a relative error of at most 0.0051.
Values may be sent and summed in bfloat16 or wider, within the bound.
No kernel may reach another device: no remote copies, remote signals or barrier semaphores. Data moves between devices by JAX's collectives and lax.ppermute only.
A program may use at most 64 MiB of HBM per device.

v0:
```python
import jax
import jax.numpy as jnp
from jax import lax
from jax.sharding import PartitionSpec as P

EXPERTS = 8
FF = 16384


def swapped(value, axis, stride):
    mask = 2**stride
    pairs = [(source, source ^ mask) for source in range(lax.axis_size(axis))]
    return lax.ppermute(value, axis, pairs)


def keep_probability(column_sums, grand_sum, row_total):
    column_mean = column_sums / row_total
    grand_mean = grand_sum / (EXPERTS * row_total * FF)
    return (0.2 + 0.7 * column_mean / (column_mean + grand_mean)).astype(jnp.bfloat16)


def on_device(task_deltas, rank_scores, keep_limits):
    groups = lax.axis_size("shard") // EXPERTS
    expert = lax.axis_index("shard") // groups
    row_count = task_deltas.shape[2]
    rows_whole = row_count * groups
    width_all = task_deltas.shape[3]
    selector = jnp.arange(EXPERTS, dtype=jnp.int32) == expert
    results = []
    for layer_at in range(task_deltas.shape[1]):
        change = task_deltas[0, layer_at].astype(jnp.float32)
        magnitude = jnp.sum(jnp.abs(change), axis=0)
        group_total = magnitude
        for bit_at in range(groups.bit_length() - 1):
            group_total = group_total + swapped(group_total, "shard", bit_at)
        grand_sum = lax.psum(jnp.sum(magnitude), "shard")
        rounded = lax.optimization_barrier(keep_probability(group_total, grand_sum, rows_whole))
        probability = rounded.astype(jnp.float32)
        own_limit = jnp.sum(jnp.where(selector, keep_limits[0, layer_at], 0))
        retained = jnp.where(
            rank_scores[0, layer_at] < own_limit, change / probability[None, :], jnp.float32(0.0)
        )
        summed = lax.psum(retained, "task")
        columns = width_all // lax.axis_size("task")
        portion = lax.dynamic_slice_in_dim(summed, lax.axis_index("task") * columns, columns, 1)
        results.append(portion.astype(jnp.bfloat16))
    return jnp.stack(results)


def solution(mesh):
    return jax.shard_map(
        on_device,
        mesh=mesh,
        in_specs=(
            P("task", None, "shard", None),
            P("task", None, "shard", None),
            P("task", None, None),
        ),
        out_specs=P(None, "shard", "task"),
        check_vma=False,
    )
```

profile of v0, /device:TPU:0, one launch (start us, length us, event | category | flops | bytes accessed | tf_op | source)
XLA Modules:
  0.0 146.4 jit_solution(15803664491565942427)
XLA Ops:
  0.0 0.0 copy-start
  0.0 0.0 copy-start.1
  0.0 3.3 %fusion = (f32[]{:T(128)}, f32[]{:T(128)}, f32[]{:T(128)}, f32[]{:T(128)}, f32[16384]{0:T(1024)S(1)}, /*index=5*/f32[16384]{0:T(1024)S(1)}, f32[16384]{0:T(1024)S(1)}, f32[16384]{0:T(1024)S(1)}) fusion(bf16[1,4,16,16384]{3,2,1,0:T(8,128)(2,1)} %param.3), kind=kLoop, calls=%fused_computation.8 | loop fusion | flops 4128764 | bytes 2359312 | tf_op jit(solution)/shard_map/reduce_sum | solution.py:36
  3.3 0.5 collective-permute-start.1
  3.8 0.0 collective-permute-start
  3.8 0.5 collective-permute-start.3
  4.3 0.0 collective-permute-start.2
  4.3 35.8 %all-reduce = (f32[]{:T(128)}, f32[]{:T(128)}, f32[]{:T(128)}, f32[]{:T(128)}) all-reduce(f32[]{:T(128)} %get-tuple-element.8, f32[]{:T(128)} %get-tuple-element.7, f32[]{:T(128)} %get-tuple-element.6, f32[]{:T(128)} %get-tuple-element.5), channel_id=1, replica_groups=mesh['shard'=16,'task'=2] {'shard'}, use_global_device_ids=true, to_apply=%region_18.19 | all-reduce | flops 4 | bytes 32 | tf_op jit(solution)/shard_map/psum | solution.py:36
  42.6 0.0 copy-done.1
  42.6 0.7 fusion.23
  43.3 0.0 collective-permute-done.1
  43.4 0.0 collective-permute-done
  43.4 0.0 collective-permute-done.3
  43.5 0.0 collective-permute-done.2
  43.5 0.0 copy-done
  43.6 6.6 %fusion.8 = (f32[16,16384]{1,0:T(8,128)S(1)}, f32[16,16384]{1,0:T(8,128)}, f32[16,16384]{1,0:T(8,128)}, f32[16,16384]{1,0:T(8,128)}) fusion(s32[1,4,16,16384]{3,2,1,0:T(8,128)} %param.4, f32[16384]{0:T(1024)S(1)} %convert_element_type.63, s32[]{:T(128)} %get-tuple-element.13, bf16[1,4,16,16384]{3,2,1,0:T(8,128)(2,1)S(1)} %copy-done, ...), kind=kLoop, calls=%fused_computation.16 | loop fusion | flops 4194304 | bytes 10747920 | tf_op jit(solution)/shard_map/jit(_where)/select_n | solution.py:40
  50.2 95.0 %all-reduce.3 = (bf16[16,16384]{1,0:T(8,128)(2,1)S(1)}, bf16[16,16384]{1,0:T(8,128)(2,1)S(1)}, bf16[16,16384]{1,0:T(8,128)(2,1)S(1)}, bf16[16,16384]{1,0:T(8,128)(2,1)S(1)}) all-reduce(f32[16,16384]{1,0:T(8,128)} %get-tuple-element.27, f32[16,16384]{1,0:T(8,128)} %get-tuple-element.28, ...), channel_id=1, replica_groups=mesh['shard'=16,'task'=2] {'task'}, use_global_device_ids=true, to_apply=%region_19.20 | all-reduce | flops 1048576 | bytes 6291456 | tf_op jit(solution)/shard_map/psum | solution.py:43
  145.3 1.1 pad_maximum_fusion
  (10 shorter events, 0.2 us)
Async XLA Ops:
  0.0 43.6 %copy-start = (bf16[1,4,16,16384]{3,2,1,0:T(8,128)(2,1)S(1)}, bf16[1,4,16,16384]{3,2,1,0:T(8,128)(2,1)}, u32[]{:S(2)}) copy-start(bf16[1,4,16,16384]{3,2,1,0:T(8,128)(2,1)} %param.3) | copy-start | bytes 6291460
  0.0 42.6 %copy-start.1 = (s32[1,4,8]{2,1,0:T(4,128)S(1)}, s32[1,4,8]{2,1,0:T(4,128)}, u32[]{:S(2)}) copy-start(s32[1,4,8]{2,1,0:T(4,128)} %param.5) | copy-start | bytes 388
  3.3 40.0 %collective-permute-start.1 = (f32[16384]{0:T(1024)S(1)}, f32[16384]{0:T(1024)S(1)}, u32[]{:S(2)}, u32[]{:S(2)}) collective-permute-start(f32[16384]{0:T(1024)S(1)} %get-tuple-element.9), channel_id=1, source_target_pairs={{0,2},{2,0},{4,6},{6,4},{8,10},{10,8},{12,14},{14,12},{16,18},{18,... | collective-permute-start | bytes 196616 | tf_op jit(solution)/shard_map/ppermute | solution.py:13
  3.8 39.5 %collective-permute-start = (f32[16384]{0:T(1024)S(1)}, f32[16384]{0:T(1024)S(1)}, u32[]{:S(2)}, u32[]{:S(2)}) collective-permute-start(f32[16384]{0:T(1024)S(1)} %get-tuple-element.10), channel_id=1, source_target_pairs={{0,2},{2,0},{4,6},{6,4},{8,10},{10,8},{12,14},{14,12},{16,18},{18,... | collective-permute-start | bytes 196616 | tf_op jit(solution)/shard_map/ppermute | solution.py:13
  3.8 39.6 %collective-permute-start.3 = (f32[16384]{0:T(1024)S(1)}, f32[16384]{0:T(1024)S(1)}, u32[]{:S(2)}, u32[]{:S(2)}) collective-permute-start(f32[16384]{0:T(1024)S(1)} %get-tuple-element.11), channel_id=1, source_target_pairs={{0,2},{2,0},{4,6},{6,4},{8,10},{10,8},{12,14},{14,12},{16,18},{18,... | collective-permute-start | bytes 196616 | tf_op jit(solution)/shard_map/ppermute | solution.py:13
  4.3 39.2 %collective-permute-start.2 = (f32[16384]{0:T(1024)S(1)}, f32[16384]{0:T(1024)S(1)}, u32[]{:S(2)}, u32[]{:S(2)}) collective-permute-start(f32[16384]{0:T(1024)S(1)} %get-tuple-element.12), channel_id=1, source_target_pairs={{0,2},{2,0},{4,6},{6,4},{8,10},{10,8},{12,14},{14,12},{16,18},{18,... | collective-permute-start | bytes 196616 | tf_op jit(solution)/shard_map/ppermute | solution.py:13
where the time goes:
time: 147 us; the launch traced here: 146 us
  blocking collectives  131 us (89%)
  other arithmetic  11.8 us (8%)
  between operations  2.65 us (2%)
    psum x1, blocking collectives, on_device(): summed = lax.psum(retained, 'task')  95 us
    psum x1, blocking collectives, on_device(): grand_sum = lax.psum(jnp.sum(magnitude), 'shard')  35.8 us
    select_n x1, other arithmetic, on_device(): jnp.where(rank_scores[0, layer_at] < own_limit, change / probability[None...  6.62 us
    reduce_sum x1, other arithmetic, on_device(): grand_sum = lax.psum(jnp.sum(magnitude), 'shard')  3.31 us
  transfers between devices with their start and end apart: 4, of which 0 were waited for; matrix products, arithmetic and copies ran while one was open for 1% of the time, Pallas kernels for 0%

commit v1 on v0

v1 whole, which is shorter than its diff:
```python
import jax
import jax.numpy as jnp
from jax import lax
from jax.sharding import PartitionSpec as P

EXPERTS = 8
FF = 16384


def swapped(value, axis, bit):
    pairs = [(source, source ^ (1 << bit)) for source in range(lax.axis_size(axis))]
    return lax.ppermute(value, axis, pairs)


def shifted(value, axis, step):
    size = lax.axis_size(axis)
    return lax.ppermute(value, axis, [(source, (source + step) % size) for source in range(size)])


def inverse_probability(column_mean, grand_mean):
    return 1.0 / (0.2 + 0.7 * column_mean / (column_mean + grand_mean))


def on_device(task_deltas, rank_scores, keep_limits):
    shards, tasks = lax.axis_size("shard"), lax.axis_size("task")
    groups = shards // EXPERTS
    group_bits = groups.bit_length() - 1
    expert = lax.axis_index("shard") // groups
    task = lax.axis_index("task")
    layers, row_count, width = task_deltas.shape[1:]
    rows_whole = row_count * groups
    columns = width // tasks
    deltas, scores = task_deltas[0], rank_scores[0]
    limits = lax.dynamic_index_in_dim(keep_limits[0], expert, 1, keepdims=False)

    def own(value, step):
        return lax.dynamic_slice_in_dim(value, (task + step) % tasks * columns, columns, value.ndim - 1)

    def masked(layer, step):
        return jnp.where(own(scores[layer], step) < limits[layer], own(deltas[layer], step), jnp.bfloat16(0))

    arrived = [[shifted(masked(layer, step), "task", step) for layer in range(layers)] for step in range(1, tasks)]

    sums = jnp.sum(jnp.abs(deltas.astype(jnp.float32)), axis=1)
    for bit in range(group_bits):
        sums = sums + swapped(sums, "shard", bit)
    totals = jnp.sum(sums, axis=1)
    means = sums / rows_whole
    all_means = [own(means, 0)]
    all_totals = [totals]
    for step in range(1, tasks):
        all_means.append(shifted(own(means, step).astype(jnp.bfloat16), "task", step).astype(jnp.float32))
        all_totals.append(shifted(totals, "task", step))
    totals = jnp.stack(all_totals)
    for bit in range(group_bits, shards.bit_length() - 1):
        totals = totals + swapped(totals, "shard", bit)
    grand = totals / (EXPERTS * rows_whole * FF)

    results = []
    for layer in range(layers):
        merged = masked(layer, 0).astype(jnp.float32) * inverse_probability(all_means[0][layer], grand[0, layer])
        for step in range(1, tasks):
            scale = inverse_probability(all_means[step][layer], grand[step, layer])
            merged = merged + arrived[step - 1][layer].astype(jnp.float32) * scale
        results.append(merged.astype(jnp.bfloat16))
    return jnp.stack(results)


def solution(mesh):
    return jax.shard_map(
        on_device,
        mesh=mesh,
        in_specs=(
            P("task", None, "shard", None),
            P("task", None, "shard", None),
            P("task", None, None),
        ),
        out_specs=P(None, "shard", "task"),
        check_vma=False,
    )
```

time: 147 us -> 64.2 us (0.44)
  blocking collectives: 131 us -> 0 us
  waiting for transfers between devices: 0.01 us -> 17.8 us
  starting transfers between devices: 1.02 us -> 14.5 us
  other arithmetic: 11.8 us -> 24.5 us
  local copies, waits for them, and re-layouts: 0.1 us -> 6.84 us
  between operations: 2.65 us -> 0.16 us
    psum x2 -> x0, blocking collectives: 131 us -> none  [the longest x1 95 us: on_device(): summed = lax.psum(retained, 'task')]
    ppermute x0 -> x6, waiting for transfers between devices: none -> 11.8 us  [shifted(): lax.ppermute(value, axis, [(source, (source + step) % size) for source in...]
    ppermute x0 -> x6, starting transfers between devices: none -> 8.55 us  [shifted(): lax.ppermute(value, axis, [(source, (source + step) % size) for source in...]
    another operation x1 -> x5, other arithmetic: 1.1 us -> 8.36 us  [on_device(): return jnp.stack(results)]
    slice x0 -> x4, local copies, waits for them, and re-layouts: none -> 6.71 us  [the longest x1 4.07 us: masked(): scores[layer]]
    ppermute x4, waiting for transfers between devices: 0.01 us -> 5.97 us  [swapped(): return lax.ppermute(value, axis, pairs)]
    div x0 -> x3, other arithmetic: none -> 5.73 us  [the longest x2 5.72 us: inverse_probability(): return 1.0 / (0.2 + 0.7 * column_mean / (column_mean + grand_mean))]
    ppermute x4, starting transfers between devices: 1.02 us -> 5.92 us  [swapped(): return lax.ppermute(value, axis, pairs)]
  transfers between devices with their start and end apart: 4 -> 10, of which waited for: 0 -> 4; matrix products, arithmetic and copies ran while one was open for 1% -> 31% of each run, Pallas kernels for 0% -> 0%
where the time goes in v1:
time: 64.2 us; the launch traced here: 63.7 us
  other arithmetic  24.5 us (38%)
  waiting for transfers between devices  17.8 us (28%)
  starting transfers between devices  14.5 us (23%)
  local copies, waits for them, and re-layouts  6.84 us (11%)
    ppermute x6, waiting for transfers between devices, shifted(): lax.ppermute(value, axis, [(source, (source + step) % size) for source in...  11.8 us
    ppermute x6, starting transfers between devices, shifted(): lax.ppermute(value, axis, [(source, (source + step) % size) for source in...  8.55 us
    another operation x5, other arithmetic, on_device(): return jnp.stack(results)  8.36 us
    select_n x4, other arithmetic, masked(): jnp.where(own(scores[layer], step) < limits[layer], own(deltas[layer], st...  8.16 us
    ppermute x4, waiting for transfers between devices, swapped(): return lax.ppermute(value, axis, pairs)  5.97 us
    ppermute x4, starting transfers between devices, swapped(): return lax.ppermute(value, axis, pairs)  5.92 us
    div x2, other arithmetic, inverse_probability(): return 1.0 / (0.2 + 0.7 * column_mean / (column_mean + grand_mean))  5.72 us
    slice x1, local copies, waits for them, and re-layouts, masked(): scores[layer]  4.07 us
  transfers between devices with their start and end apart: 10, of which 4 were waited for; matrix products, arithmetic and copies ran while one was open for 31% of the time, Pallas kernels for 0%

profile of v1, /device:TPU:0, one launch (start us, length us, event | category | flops | bytes accessed | tf_op | source)
XLA Modules:
  0.0 63.7 jit_solution(8436243994335110369)
XLA Ops:
  0.0 4.1 %fusion.29 = (s32[1,1,16,16384]{3,2,1,0:T(8,128)S(1)}, s32[1,1,16,16384]{3,2,1,0:T(8,128)}, s32[1,1,16,16384]{3,2,1,0:T(8,128)}, s32[1,1,16,16384]{3,2,1,0:T(8,128)}) fusion(s32[1,4,16,16384]{3,2,1,0:T(8,128)} %param.4), kind=kLoop, calls=%fused_computation.65 | loop fusion | bytes 8388608 | tf_op jit(solution)/shard_map/slice | solution.py:40
  4.1 1.4 %fusion.30 = (bf16[1,1,16,16384]{3,2,1,0:T(8,128)(2,1)}, bf16[1,1,16,16384]{3,2,1,0:T(8,128)(2,1)}, bf16[1,1,16,16384]{3,2,1,0:T(8,128)(2,1)}, bf16[1,1,16,16384]{3,2,1,0:T(8,128)(2,1)}) fusion(bf16[1,4,16,16384]{3,2,1,0:T(8,128)(2,1)S(1)} %copy-done.1), kind=kLoop, calls=%fused_computation.66 | loop fusion | bytes 4194304 | tf_op jit(solution)/shard_map/slice | solution.py:40
  6.1 2.7 %fusion.16 = bf16[16,8192]{1,0:T(8,128)(2,1)} fusion(s32[1,1,16,16384]{3,2,1,0:T(8,128)} %get-tuple-element.7, s32[]{:T(128)S(6)} %select_n.120, bf16[1,1,16,16384]{3,2,1,0:T(8,128)(2,1)} %get-tuple-element.11, s32[]{:T(128)} %bitcast.26), kind=kLoop, calls=%fused_computation.30 | loop fusion | flops 262144 | bytes 1048584 | tf_op jit(solution)/shard_map/jit(_where)/select_n | solution.py:40
  8.8 3.0 %collective-permute-start.9 = (bf16[16,8192]{1,0:T(8,128)(2,1)}, bf16[16,8192]{1,0:T(8,128)(2,1)}, u32[]{:S(2)}, u32[]{:S(2)}) collective-permute-start(bf16[16,8192]{1,0:T(8,128)(2,1)} %fusion.16), channel_id=1, source_target_pairs={{0,1},{1,0},{2,3},{3,2},{4,5},{5,4},{6,7},{7,6},{8,9},{9,8},{10,11... | collective-permute-start | bytes 786440 | tf_op jit(solution)/shard_map/ppermute | solution.py:17
  12.8 2.6 %fusion.18 = bf16[16,8192]{1,0:T(8,128)(2,1)} fusion(s32[1,1,16,16384]{3,2,1,0:T(8,128)} %get-tuple-element.8, s32[]{:T(128)S(6)} %select_n.120, bf16[1,1,16,16384]{3,2,1,0:T(8,128)(2,1)} %get-tuple-element.12, s32[]{:T(128)} %bitcast.18), kind=kLoop, calls=%fused_computation.32 | loop fusion | flops 262144 | bytes 1048584 | tf_op jit(solution)/shard_map/jit(_where)/select_n | solution.py:40
  15.4 1.4 %fusion.20 = bf16[16,8192]{1,0:T(8,128)(2,1)} fusion(s32[1,1,16,16384]{3,2,1,0:T(8,128)S(1)} %copy-done.2, s32[]{:T(128)S(6)} %select_n.120, bf16[1,1,16,16384]{3,2,1,0:T(8,128)(2,1)S(1)} %copy-done.7, s32[]{:T(128)} %bitcast.10), kind=kLoop, calls=%fused_computation.34 | loop fusion | flops 262144 | bytes 1048584 | tf_op jit(solution)/shard_map/jit(_where)/select_n | solution.py:40
  16.9 2.0 %collective-permute-start.7 = (bf16[16,8192]{1,0:T(8,128)(2,1)}, bf16[16,8192]{1,0:T(8,128)(2,1)}, u32[]{:S(2)}, u32[]{:S(2)}) collective-permute-start(bf16[16,8192]{1,0:T(8,128)(2,1)} %fusion.20), channel_id=1, source_target_pairs={{0,1},{1,0},{2,3},{3,2},{4,5},{5,4},{6,7},{7,6},{8,9},{9,8},{10,11... | collective-permute-start | bytes 786440 | tf_op jit(solution)/shard_map/ppermute | solution.py:17
  18.9 1.4 %fusion.22 = bf16[16,8192]{1,0:T(8,128)(2,1)} fusion(s32[1,1,16,16384]{3,2,1,0:T(8,128)S(1)} %get-tuple-element.5, s32[]{:T(128)S(6)} %select_n.120, bf16[1,1,16,16384]{3,2,1,0:T(8,128)(2,1)S(1)} %copy-done.5, s32[]{:T(128)} %bitcast), kind=kLoop, calls=%fused_computation.36 | loop fusion | flops 262144 | bytes 1048584 | tf_op jit(solution)/shard_map/jit(_where)/select_n | solution.py:40
  20.3 1.3 %add_reduce_fusion = (f32[4]{0:T(128)S(1)}, f32[4,16384]{1,0:T(4,128)S(1)}) fusion(f32[4,16384]{1,0:T(4,128)S(1)} %abs_reduce_fusion, f32[4,16384]{1,0:T(4,128)} %collective-permute-done), kind=kLoop, calls=%fused_computation.44 | loop fusion | flops 196604 | bytes 786448 | tf_op jit(solution)/shard_map/reduce_sum | solution.py:47
  21.7 2.1 %collective-permute-start.1 = (f32[4]{0:T(128)S(1)}, f32[4]{0:T(128)S(1)}, u32[]{:S(2)}, u32[]{:S(2)}) collective-permute-start(f32[4]{0:T(128)S(1)} %get-tuple-element.13), channel_id=1, source_target_pairs={{0,1},{1,0},{2,3},{3,2},{4,5},{5,4},{6,7},{7,6},{8,9},{9,8},{10,11... | collective-permute-start | bytes 56 | tf_op jit(solution)/shard_map/ppermute | solution.py:17
  23.7 11.8 %collective-permute-done.1 = f32[4]{0:T(128)S(1)} collective-permute-done((f32[4]{0:T(128)S(1)}, f32[4]{0:T(128)S(1)}, u32[]{:S(2)}, u32[]{:S(2)}) %collective-permute-start.1) | collective-permute-done | bytes 48 | tf_op jit(solution)/shard_map/ppermute | solution.py:17
  35.6 1.6 %collective-permute-start.2 = (f32[2,4]{1,0:T(2,128)S(1)}, f32[2,4]{1,0:T(2,128)S(1)}, u32[]{:S(2)}, u32[]{:S(2)}) collective-permute-start(f32[2,4]{1,0:T(2,128)S(1)} %pad_maximum_fusion.1), channel_id=1, source_target_pairs={{0,4},{2,6},{4,0},{6,2},{8,12},{10,14},{12,8},{14,10},{16,20},{18,... | collective-permute-start | bytes 104 | tf_op jit(solution)/shard_map/ppermute | solution.py:12
  37.1 2.1 %collective-permute-done.2 = f32[2,4]{1,0:T(2,128)S(1)} collective-permute-done((f32[2,4]{1,0:T(2,128)S(1)}, f32[2,4]{1,0:T(2,128)S(1)}, u32[]{:S(2)}, u32[]{:S(2)}) %collective-permute-start.2) | collective-permute-done | bytes 64 | tf_op jit(solution)/shard_map/ppermute | solution.py:12
  39.2 1.6 %collective-permute-start.3 = (f32[2,4]{1,0:T(2,128)S(1)}, f32[2,4]{1,0:T(2,128)S(1)}, u32[]{:S(2)}, u32[]{:S(2)}) collective-permute-start(f32[2,4]{1,0:T(2,128)S(1)} %fusion.28), channel_id=1, source_target_pairs={{0,8},{2,10},{4,12},{6,14},{8,0},{10,2},{12,4},{14,6},{16,24},{18,... | collective-permute-start | bytes 104 | tf_op jit(solution)/shard_map/ppermute | solution.py:12
  40.8 2.0 %collective-permute-done.3 = f32[2,4]{1,0:T(2,128)S(1)} collective-permute-done((f32[2,4]{1,0:T(2,128)S(1)}, f32[2,4]{1,0:T(2,128)S(1)}, u32[]{:S(2)}, u32[]{:S(2)}) %collective-permute-start.3) | collective-permute-done | bytes 64 | tf_op jit(solution)/shard_map/ppermute | solution.py:12
  42.9 2.7 %collective-permute-start.4 = (f32[2,4]{1,0:T(2,128)S(1)}, f32[2,4]{1,0:T(2,128)S(1)}, u32[]{:S(2)}, u32[]{:S(2)}) collective-permute-start(f32[2,4]{1,0:T(2,128)S(1)} %fusion.33), channel_id=1, source_target_pairs={{0,16},{2,18},{4,20},{6,22},{8,24},{10,26},{12,28},{14,30},{16,0},... | collective-permute-start | bytes 104 | tf_op jit(solution)/shard_map/ppermute | solution.py:12
  45.5 1.9 %collective-permute-done.4 = f32[2,4]{1,0:T(2,128)S(1)} collective-permute-done((f32[2,4]{1,0:T(2,128)S(1)}, f32[2,4]{1,0:T(2,128)S(1)}, u32[]{:S(2)}, u32[]{:S(2)}) %collective-permute-start.4) | collective-permute-done | bytes 64 | tf_op jit(solution)/shard_map/ppermute | solution.py:12
  47.4 1.4 %collective-permute-start.6 = (bf16[4,8192]{1,0:T(4,128)(2,1)S(1)}, bf16[4,8192]{1,0:T(4,128)(2,1)S(1)}, u32[]{:S(2)}, u32[]{:S(2)}) collective-permute-start(bf16[4,8192]{1,0:T(4,128)(2,1)S(1)} %dynamic-slice_convert_fusion), channel_id=1, source_target_pairs={{0,1},{1,0},{2,3},{3,2},{4,5},{5,4},{6,7},{7,6},{8,9},{9,8},{10,11... | collective-permute-start | bytes 196616 | tf_op jit(solution)/shard_map/ppermute | solution.py:17
  49.5 3.0 %add_divide_fusion.14 = (f32[1,8192]{1,0:T(1,128)S(1)}, f32[1,8192]{1,0:T(1,128)S(1)}, f32[1,8192]{1,0:T(1,128)S(1)}, f32[1,8192]{1,0:T(1,128)S(1)}) fusion(f32[4,16384]{1,0:T(4,128)S(1)} %get-tuple-element.14, s32[]{:T(128)S(6)} %select_n.115, f32[]{:T(128)} %bitcast.4, f32[]{:T(128)} %bitcast.20, s32[]{:T(128)S(6)} %add.212, f32[]{:T(128)} %bitcast.12, ...), kind=kLoop, calls=%fused_computation.59 | loop fusion | flops 163840 | bytes 262176 | tf_op jit(solution)/shard_map/div | solution.py:21
  52.6 2.7 %add_divide_fusion.12 = (f32[1,8192]{1,0:T(1,128)S(1)}, f32[1,8192]{1,0:T(1,128)S(1)}, f32[1,8192]{1,0:T(1,128)S(1)}, f32[1,8192]{1,0:T(1,128)S(1)}) fusion(f32[4,8192]{1,0:T(4,128)S(1)} %convert_element_type.63, f32[]{:T(128)} %bitcast.7, f32[]{:T(128)} %bitcast.31, f32[]{:T(128)} %bitcast.23, f32[]{:T(128)} %bitcast.15), kind=kLoop, calls=%fused_computation.57 | loop fusion | flops 163840 | bytes 262160 | tf_op jit(solution)/shard_map/div | solution.py:21
  55.3 1.8 %fusion.27 = bf16[1,16,8192]{2,1,0:T(8,128)(2,1)S(1)} fusion(bf16[16,8192]{1,0:T(8,128)(2,1)} %collective-permute-done.9, s32[1,1,16,16384]{3,2,1,0:T(8,128)S(1)} %copy-done.4, s32[]{:T(128)S(6)} %select_n.115, f32[8192]{0:T(1024)S(1)} %bitcast.73, f32[8192]{0:T(1024)S(1)} %bitcast.71, bf16[1,1,16,16384]{3,2,1,0:T(8,128)(2,1)} %get-tuple-element.11, s32[]{:T(128)} %bitcast.26), kind=kLoop, calls=%fused_computation.41 | loop fusion | flops 1048576 | bytes 1376264 | tf_op jit(solution)/shard_map/stack | solution.py:66
  57.1 2.0 %fusion.26 = bf16[1,16,8192]{2,1,0:T(8,128)(2,1)S(1)} fusion(bf16[16,8192]{1,0:T(8,128)(2,1)} %collective-permute-done.8, s32[1,1,16,16384]{3,2,1,0:T(8,128)} %get-tuple-element.8, s32[]{:T(128)S(6)} %select_n.115, f32[8192]{0:T(1024)S(1)} %bitcast.72, f32[8192]{0:T(1024)S(1)} %bitcast.69, bf16[1,1,16,16384]{3,2,1,0:T(8,128)(2,1)} %get-tuple-element.12, ...), kind=kLoop, calls=%fused_computation.40 | loop fusion | flops 1048576 | bytes 1376264 | tf_op jit(solution)/shard_map/stack | solution.py:66
  59.1 1.8 %fusion.25 = bf16[1,16,8192]{2,1,0:T(8,128)(2,1)S(1)} fusion(bf16[16,8192]{1,0:T(8,128)(2,1)} %collective-permute-done.7, s32[1,1,16,16384]{3,2,1,0:T(8,128)S(1)} %copy-done.3, s32[]{:T(128)S(6)} %select_n.115, f32[8192]{0:T(1024)S(1)} %bitcast.70, f32[8192]{0:T(1024)S(1)} %bitcast.67, bf16[1,1,16,16384]{3,2,1,0:T(8,128)(2,1)S(1)} %copy-done.8, s32[]{:T(128)} %bitcast.10), kind=kLoop, calls=%fused_computation.39 | loop fusion | flops 1048576 | bytes 1376264 | tf_op jit(solution)/shard_map/stack | solution.py:66
  60.9 1.7 %fusion.24 = bf16[1,16,8192]{2,1,0:T(8,128)(2,1)S(1)} fusion(bf16[16,8192]{1,0:T(8,128)(2,1)} %collective-permute-done.5, s32[1,1,16,16384]{3,2,1,0:T(8,128)S(1)} %get-tuple-element.5, s32[]{:T(128)S(6)} %select_n.115, f32[8192]{0:T(1024)S(1)} %bitcast.68, f32[8192]{0:T(1024)S(1)} %bitcast.66, bf16[1,1,16,16384]{3,2,1,0:T(8,128)(2,1)S(1)} %copy-done.6, s32[]{:T(128)} %bitcast), kind=kLoop, calls=%fused_computation.38 | loop fusion | flops 1048576 | bytes 1376264 | tf_op jit(solution)/shard_map/stack | solution.py:66
  (38 shorter events, 3.6 us)
Async XLA Ops:
  0.0 5.4 %copy-start = (s32[1,4,8]{2,1,0:T(4,128)S(1)}, s32[1,4,8]{2,1,0:T(4,128)}, u32[]{:S(2)}) copy-start(s32[1,4,8]{2,1,0:T(4,128)} %param.5) | copy-start | bytes 388
  0.0 4.1 %copy-start.1 = (bf16[1,4,16,16384]{3,2,1,0:T(8,128)(2,1)S(1)}, bf16[1,4,16,16384]{3,2,1,0:T(8,128)(2,1)}, u32[]{:S(2)}) copy-start(bf16[1,4,16,16384]{3,2,1,0:T(8,128)(2,1)} %param.3) | copy-start | bytes 6291460
  6.1 9.3 %copy-start.2 = (s32[1,1,16,16384]{3,2,1,0:T(8,128)S(1)}, s32[1,1,16,16384]{3,2,1,0:T(8,128)}, u32[]{:S(2)}) copy-start(s32[1,1,16,16384]{3,2,1,0:T(8,128)} %get-tuple-element.6) | copy-start | bytes 3145732
  6.1 9.3 %copy-start.7 = (bf16[1,1,16,16384]{3,2,1,0:T(8,128)(2,1)S(1)}, bf16[1,1,16,16384]{3,2,1,0:T(8,128)(2,1)}, u32[]{:S(2)}) copy-start(bf16[1,1,16,16384]{3,2,1,0:T(8,128)(2,1)} %get-tuple-element.10) | copy-start | bytes 1572868
  6.1 12.8 %copy-start.5 = (bf16[1,1,16,16384]{3,2,1,0:T(8,128)(2,1)S(1)}, bf16[1,1,16,16384]{3,2,1,0:T(8,128)(2,1)}, u32[]{:S(2)}) copy-start(bf16[1,1,16,16384]{3,2,1,0:T(8,128)(2,1)} %get-tuple-element.9) | copy-start | bytes 1572868
  8.8 46.5 %collective-permute-start.9 = (bf16[16,8192]{1,0:T(8,128)(2,1)}, bf16[16,8192]{1,0:T(8,128)(2,1)}, u32[]{:S(2)}, u32[]{:S(2)}) collective-permute-start(bf16[16,8192]{1,0:T(8,128)(2,1)} %fusion.16), channel_id=1, source_target_pairs={{0,1},{1,0},{2,3},{3,2},{4,5},{5,4},{6,7},{7,6},{8,9},{9,8},{10,11... | collective-permute-start | bytes 786440 | tf_op jit(solution)/shard_map/ppermute | solution.py:17
  12.7 42.6 %copy-start.4 = (s32[1,1,16,16384]{3,2,1,0:T(8,128)S(1)}, s32[1,1,16,16384]{3,2,1,0:T(8,128)}, u32[]{:S(2)}) copy-start(s32[1,1,16,16384]{3,2,1,0:T(8,128)} %get-tuple-element.7) | copy-start | bytes 3145732
  12.7 46.4 %copy-start.3 = (s32[1,1,16,16384]{3,2,1,0:T(8,128)S(1)}, s32[1,1,16,16384]{3,2,1,0:T(8,128)}, u32[]{:S(2)}) copy-start(s32[1,1,16,16384]{3,2,1,0:T(8,128)} %get-tuple-element.6) | copy-start | bytes 3145732
  12.7 7.6 %collective-permute-start = (f32[4,16384]{1,0:T(4,128)S(1)}, f32[4,16384]{1,0:T(4,128)}, u32[]{:S(2)}, u32[]{:S(2)}) collective-permute-start(f32[4,16384]{1,0:T(4,128)S(1)} %abs_reduce_fusion), channel_id=1, source_target_pairs={{0,2},{2,0},{4,6},{6,4},{8,10},{10,8},{12,14},{14,12},{16,18},{18,... | collective-permute-start | bytes 786440 | tf_op jit(solution)/shard_map/ppermute | solution.py:12
  15.4 41.7 %collective-permute-start.8 = (bf16[16,8192]{1,0:T(8,128)(2,1)}, bf16[16,8192]{1,0:T(8,128)(2,1)}, u32[]{:S(2)}, u32[]{:S(2)}) collective-permute-start(bf16[16,8192]{1,0:T(8,128)(2,1)} %fusion.18), channel_id=1, source_target_pairs={{0,1},{1,0},{2,3},{3,2},{4,5},{5,4},{6,7},{7,6},{8,9},{9,8},{10,11... | collective-permute-start | bytes 786440 | tf_op jit(solution)/shard_map/ppermute | solution.py:17
  16.9 42.2 %collective-permute-start.7 = (bf16[16,8192]{1,0:T(8,128)(2,1)}, bf16[16,8192]{1,0:T(8,128)(2,1)}, u32[]{:S(2)}, u32[]{:S(2)}) collective-permute-start(bf16[16,8192]{1,0:T(8,128)(2,1)} %fusion.20), channel_id=1, source_target_pairs={{0,1},{1,0},{2,3},{3,2},{4,5},{5,4},{6,7},{7,6},{8,9},{9,8},{10,11... | collective-permute-start | bytes 786440 | tf_op jit(solution)/shard_map/ppermute | solution.py:17
  20.3 40.6 %collective-permute-start.5 = (bf16[16,8192]{1,0:T(8,128)(2,1)}, bf16[16,8192]{1,0:T(8,128)(2,1)}, u32[]{:S(2)}, u32[]{:S(2)}) collective-permute-start(bf16[16,8192]{1,0:T(8,128)(2,1)} %fusion.22), channel_id=1, source_target_pairs={{0,1},{1,0},{2,3},{3,2},{4,5},{5,4},{6,7},{7,6},{8,9},{9,8},{10,11... | collective-permute-start | bytes 786440 | tf_op jit(solution)/shard_map/ppermute | solution.py:17
  20.3 38.8 %copy-start.8 = (bf16[1,1,16,16384]{3,2,1,0:T(8,128)(2,1)S(1)}, bf16[1,1,16,16384]{3,2,1,0:T(8,128)(2,1)}, u32[]{:S(2)}) copy-start(bf16[1,1,16,16384]{3,2,1,0:T(8,128)(2,1)} %get-tuple-element.10) | copy-start | bytes 1572868
  20.3 40.6 %copy-start.6 = (bf16[1,1,16,16384]{3,2,1,0:T(8,128)(2,1)S(1)}, bf16[1,1,16,16384]{3,2,1,0:T(8,128)(2,1)}, u32[]{:S(2)}) copy-start(bf16[1,1,16,16384]{3,2,1,0:T(8,128)(2,1)} %get-tuple-element.9) | copy-start | bytes 1572868
  21.7 13.9 %collective-permute-start.1 = (f32[4]{0:T(128)S(1)}, f32[4]{0:T(128)S(1)}, u32[]{:S(2)}, u32[]{:S(2)}) collective-permute-start(f32[4]{0:T(128)S(1)} %get-tuple-element.13), channel_id=1, source_target_pairs={{0,1},{1,0},{2,3},{3,2},{4,5},{5,4},{6,7},{7,6},{8,9},{9,8},{10,11... | collective-permute-start | bytes 56 | tf_op jit(solution)/shard_map/ppermute | solution.py:17
  35.6 3.6 %collective-permute-start.2 = (f32[2,4]{1,0:T(2,128)S(1)}, f32[2,4]{1,0:T(2,128)S(1)}, u32[]{:S(2)}, u32[]{:S(2)}) collective-permute-start(f32[2,4]{1,0:T(2,128)S(1)} %pad_maximum_fusion.1), channel_id=1, source_target_pairs={{0,4},{2,6},{4,0},{6,2},{8,12},{10,14},{12,8},{14,10},{16,20},{18,... | collective-permute-start | bytes 104 | tf_op jit(solution)/shard_map/ppermute | solution.py:12
  39.2 3.6 %collective-permute-start.3 = (f32[2,4]{1,0:T(2,128)S(1)}, f32[2,4]{1,0:T(2,128)S(1)}, u32[]{:S(2)}, u32[]{:S(2)}) collective-permute-start(f32[2,4]{1,0:T(2,128)S(1)} %fusion.28), channel_id=1, source_target_pairs={{0,8},{2,10},{4,12},{6,14},{8,0},{10,2},{12,4},{14,6},{16,24},{18,... | collective-permute-start | bytes 104 | tf_op jit(solution)/shard_map/ppermute | solution.py:12
  42.9 4.5 %collective-permute-start.4 = (f32[2,4]{1,0:T(2,128)S(1)}, f32[2,4]{1,0:T(2,128)S(1)}, u32[]{:S(2)}, u32[]{:S(2)}) collective-permute-start(f32[2,4]{1,0:T(2,128)S(1)} %fusion.33), channel_id=1, source_target_pairs={{0,16},{2,18},{4,20},{6,22},{8,24},{10,26},{12,28},{14,30},{16,0},... | collective-permute-start | bytes 104 | tf_op jit(solution)/shard_map/ppermute | solution.py:12
  47.4 5.1 %collective-permute-start.6 = (bf16[4,8192]{1,0:T(4,128)(2,1)S(1)}, bf16[4,8192]{1,0:T(4,128)(2,1)S(1)}, u32[]{:S(2)}, u32[]{:S(2)}) collective-permute-start(bf16[4,8192]{1,0:T(4,128)(2,1)S(1)} %dynamic-slice_convert_fusion), channel_id=1, source_target_pairs={{0,1},{1,0},{2,3},{3,2},{4,5},{5,4},{6,7},{7,6},{8,9},{9,8},{10,11... | collective-permute-start | bytes 196616 | tf_op jit(solution)/shard_map/ppermute | solution.py:17

commit v2 on v1

v2 whole, which is shorter than its diff:
```python
import functools

import jax
import jax.numpy as jnp
from jax import lax
from jax.experimental import pallas as pl
from jax.experimental.pallas import tpu as pltpu
from jax.sharding import PartitionSpec as P


EXPERTS = 8
FF = 16384
LANES = 128
BLOCK = 1024

ANY = pl.BlockSpec(memory_space=pl.ANY)
VMEM = pl.BlockSpec(memory_space=pltpu.VMEM)


def crossed(value, axis, mask):
    return lax.ppermute(value, axis, [(source, source ^ mask) for source in range(lax.axis_size(axis))])


def swapped(value, axis, bit):
    return crossed(value, axis, 1 << bit)


def shifted(value, axis, step):
    size = lax.axis_size(axis)
    return lax.ppermute(value, axis, [(source, (source + step) % size) for source in range(size)])


def column_start(step, columns):
    tasks = lax.axis_size("task")
    return lax.rem(lax.axis_index("task") + step, tasks) * columns


def own_expert():
    return lax.axis_index("shard") // (lax.axis_size("shard") // EXPERTS)


def blocks(width, body):
    block = min(BLOCK, width)

    @pl.loop(0, width // block)
    def _(at):
        body(pl.multiple_of(at * block, block), block)


def mask_block(deltas, scores, limit):
    return jnp.where(scores < limit, deltas.astype(jnp.float32), 0.0).astype(jnp.bfloat16)


def first_kernel(limits, deltas, scores, *refs):
    tasks = lax.axis_size("task")
    outs = refs[: tasks - 1]
    limit_buf, delta_buf, score_buf, sems = refs[tasks - 1 :]
    columns = outs[0].shape[1]
    copies = [pltpu.make_async_copy(limits, limit_buf, sems.at[0])]
    for step in range(1, tasks):
        source = pl.ds(pl.multiple_of(column_start(step, columns), LANES), columns)
        copies.append(pltpu.make_async_copy(scores.at[0, 0, :, source], score_buf.at[step - 1], sems.at[2 * step - 1]))
        copies.append(pltpu.make_async_copy(deltas.at[0, 0, :, source], delta_buf.at[step - 1], sems.at[2 * step]))
    for copy in copies:
        copy.start()
    copies[0].wait()
    limit = limit_buf[0, 0, own_expert()]
    for step in range(1, tasks):
        copies[2 * step - 1].wait()
        copies[2 * step].wait()
        out = outs[step - 1]

        def body(at, block):
            where = pl.ds(at, block)
            out[:, where] = mask_block(delta_buf[step - 1, :, where], score_buf[step - 1, :, where], limit)

        blocks(columns, body)


def rest_kernel(limits, deltas, scores, *refs):
    tasks = lax.axis_size("task")
    layers, rows, width = deltas.shape[1:]
    columns = width // tasks
    half = columns // 2
    block = min(BLOCK, half)
    places = half // block
    folded = 2 * layers
    groups = lax.axis_size("shard") // EXPERTS
    sent = [refs[(layer - 1) * (tasks - 1) : layer * (tasks - 1)] for layer in range(1, layers)]
    refs = refs[(layers - 1) * (tasks - 1) :]
    packs, refs = refs[:tasks], refs[tasks:]
    own, limit_buf, delta_buf, score_buf, sems = refs
    limit_copy = pltpu.make_async_copy(limits, limit_buf, sems.at[0])
    limit_copy.start()
    work = [(step, place) for step in [*range(1, tasks), 0] for place in range(places)]
    copies = []
    for step, place in work:
        start = column_start(step, columns)
        pending = []
        for part in range(2):
            source = pl.ds(pl.multiple_of(start + part * half + place * block, LANES), block)
            skip = 1 if step else 0
            at = 1 + 4 * len(copies) + 2 * part
            pending.append(pltpu.make_async_copy(
                deltas.at[0, :, :, source], delta_buf.at[len(copies), part], sems.at[at]))
            pending.append(pltpu.make_async_copy(
                scores.at[0, skip:, :, source], score_buf.at[len(copies), part, skip:], sems.at[at + 1]))
        for copy in pending:
            copy.start()
        copies.append(pending)
    shape = (folded, folded * rows)
    taken = lax.broadcasted_iota(jnp.int32, shape, 1) // rows == lax.broadcasted_iota(jnp.int32, shape, 0)
    selector = jnp.where(taken, 1.0, 0.0).astype(jnp.bfloat16)
    totals = jnp.zeros((folded, LANES), jnp.float32)
    limit_copy.wait()
    chosen = [limit_buf[0, layer, own_expert()] for layer in range(layers)]
    for at, (step, place) in enumerate(work):
        for copy in copies[at]:
            copy.wait()
        change = delta_buf[at].reshape(folded * rows, block)
        sums = jnp.dot(selector, jnp.abs(change), preferred_element_type=jnp.float32)
        means = sums * (1.0 / (rows * groups))
        packs[step][:, place * block : (place + 1) * block] = means.astype(jnp.bfloat16)
        for tile in range(0, block, LANES):
            totals = totals + means[:, tile : tile + LANES]
        for part in range(2):
            target = pl.ds(part * half + place * block, block)
            for layer in range(layers):
                if step and not layer:
                    continue
                kept = mask_block(delta_buf[at, part, layer], score_buf[at, part, layer], chosen[layer])
                if step:
                    sent[layer - 1][step - 1][:, target] = kept
                else:
                    own[layer, :, target] = kept
    high = totals.astype(jnp.bfloat16)
    low = (totals - high.astype(jnp.float32)).astype(jnp.bfloat16)
    for step in range(tasks):
        packs[step][:, half : half + LANES] = high
        packs[step][:, half + LANES :] = low


def join_kernel(*refs):
    tasks = lax.axis_size("task")
    means, totals = refs[2 * tasks :]
    half = means.shape[2]
    for step in range(tasks):
        mine = refs[2 * step][...].astype(jnp.float32)
        theirs = refs[2 * step + 1][...].astype(jnp.float32)
        both = mine + theirs
        means[step] = both[:, :half]
        totals[step] = both[:, half : half + LANES] + both[:, half + LANES :]


def scale_kernel(means, totals, scales):
    tasks, folded, _ = means.shape
    for step in range(tasks):
        total = jnp.sum(totals[step], axis=1, keepdims=True)
        total = total + jnp.concatenate([total[folded // 2 :], total[: folded // 2]], axis=0)
        grand = total * (1.0 / (EXPERTS * FF))
        mean = means[step]
        rounded = (0.2 + 0.7 * mean / (mean + grand)).astype(jnp.bfloat16)
        scales[step] = 1.0 / rounded.astype(jnp.float32)


def merge_layers(picked, tasks, aliased, scales, own, *refs):
    half = scales.shape[2]
    layers = own.shape[0]
    arrived = refs[: len(picked) * (tasks - 1)]
    refs = refs[len(arrived) + aliased :]
    out, buf, sems = refs
    copies = []
    for place, layer in enumerate(picked):
        for part in range(2):
            row = part * layers + layer

            def body(at, block):
                narrow = pl.ds(at, block)
                where = pl.ds(pl.multiple_of(part * half + at, LANES), block)
                merged = own[layer, :, where].astype(jnp.float32) * scales[0, row : row + 1, narrow]
                for step in range(1, tasks):
                    other = arrived[place * (tasks - 1) + step - 1][:, where].astype(jnp.float32)
                    merged = merged + other * scales[step, row : row + 1, narrow]
                buf[place, :, where] = merged.astype(jnp.bfloat16)

            blocks(half, body)
        copies.append(pltpu.make_async_copy(buf.at[place], out.at[layer], sems.at[place]))
        copies[-1].start()
    for copy in copies:
        copy.wait()


def cost(flops, moved):
    return pl.CostEstimate(flops=flops, bytes_accessed=moved, transcendentals=0)


def on_chip(value):
    return pltpu.with_memory_space_constraint(value, pltpu.VMEM)


def merge_all(task_deltas, rank_scores, keep_limits):
    shards, tasks = lax.axis_size("shard"), lax.axis_size("task")
    groups = shards // EXPERTS
    group_bits = groups.bit_length() - 1
    layers, rows, width = task_deltas.shape[1:]
    columns = width // tasks
    half = columns // 2
    block = min(BLOCK, half)
    bf16, f32 = jnp.bfloat16, jnp.float32
    slab = pltpu.VMEM((rows, columns), bf16)

    first = pl.pallas_call(
        first_kernel,
        out_shape=[slab] * (tasks - 1),
        in_specs=[ANY] * 3,
        out_specs=[VMEM] * (tasks - 1),
        scratch_shapes=[
            pltpu.SMEM(keep_limits.shape, jnp.int32),
            pltpu.VMEM((tasks - 1, rows, columns), bf16),
            pltpu.VMEM((tasks - 1, rows, columns), jnp.int32),
            pltpu.SemaphoreType.DMA((2 * tasks - 1,)),
        ],
        cost_estimate=cost(10**6, 6 * rows * columns),
        name="first",
    )(keep_limits, task_deltas, rank_scores)
    arrived = [[shifted(first[step - 1], "task", step) for step in range(1, tasks)]]

    rest = pl.pallas_call(
        rest_kernel,
        out_shape=[slab] * ((layers - 1) * (tasks - 1))
        + [pltpu.VMEM((2 * layers, half + 2 * LANES), bf16)] * tasks
        + [pltpu.VMEM((layers, rows, columns), bf16)],
        in_specs=[ANY] * 3,
        out_specs=[VMEM] * ((layers - 1) * (tasks - 1) + tasks + 1),
        scratch_shapes=[
            pltpu.SMEM(keep_limits.shape, jnp.int32),
            pltpu.VMEM((tasks * half // block, 2, layers, rows, block), bf16),
            pltpu.VMEM((tasks * half // block, 2, layers, rows, block), jnp.int32),
            pltpu.SemaphoreType.DMA((4 * tasks * half // block + 1,)),
        ],
        cost_estimate=cost(10**7, 6 * layers * rows * width),
        name="rest",
    )(keep_limits, task_deltas, rank_scores)
    sent, packs, own = rest[: (layers - 1) * (tasks - 1)], rest[-tasks - 1 : -1], rest[-1]

    pairs = [packs[0], swapped(packs[0], "shard", 0)]
    for step in range(1, tasks):
        arrival = shifted(packs[step], "task", step)
        pairs += [arrival, swapped(arrival, "shard", 0)]
    for layer in range(1, layers):
        at = (layer - 1) * (tasks - 1)
        arrived.append([shifted(sent[at + step - 1], "task", step) for step in range(1, tasks)])

    means, totals = pl.pallas_call(
        join_kernel,
        out_shape=[pltpu.VMEM((tasks, 2 * layers, half), f32), pltpu.VMEM((tasks, 2 * layers, LANES), f32)],
        in_specs=[VMEM] * (2 * tasks),
        out_specs=[VMEM] * 2,
        cost_estimate=cost(10**6, 8 * tasks * layers * half),
        name="join",
    )(*[on_chip(pair) for pair in pairs])
    for bit in range(1, group_bits):
        means = means + swapped(means, "shard", bit)
        totals = totals + swapped(totals, "shard", bit)
    bits = [*range(group_bits, shards.bit_length() - 1)]
    for turn in (bits[:1], bits[1:]):
        masks = [0]
        for bit in turn:
            masks += [mask + (1 << bit) for mask in masks]
        totals = sum([crossed(totals, "shard", mask) for mask in masks[1:]], totals)

    scales = pl.pallas_call(
        scale_kernel,
        out_shape=pltpu.VMEM((tasks, 2 * layers, half), f32),
        in_specs=[VMEM] * 2,
        out_specs=VMEM,
        cost_estimate=cost(10**6, 8 * tasks * layers * half),
        name="scale",
    )(on_chip(means), on_chip(totals))

    out = None
    for picked in ([*range(layers - 1)], [layers - 1]):
        extra = [] if out is None else [out]
        arrivals = [on_chip(arrived[layer][step]) for layer in picked for step in range(tasks - 1)]
        out = pl.pallas_call(
            functools.partial(merge_layers, picked, tasks, len(extra)),
            out_shape=jax.ShapeDtypeStruct((layers, rows, columns), bf16),
            in_specs=[VMEM] * (2 + len(arrivals)) + [ANY] * len(extra),
            out_specs=ANY,
            scratch_shapes=[pltpu.VMEM((len(picked), rows, columns), bf16), pltpu.SemaphoreType.DMA((len(picked),))],
            input_output_aliases={2 + len(arrivals): 0} if extra else {},
            cost_estimate=cost(10**6, 6 * len(picked) * rows * columns),
            name="merge" if out is None else "merge_last",
        )(on_chip(scales), on_chip(own), *arrivals, *extra)
    return out


def solution(mesh):
    return jax.shard_map(
        merge_all,
        mesh=mesh,
        in_specs=(
            P("task", None, "shard", None),
            P("task", None, "shard", None),
            P("task", None, None),
        ),
        out_specs=P(None, "shard", "task"),
        check_vma=False,
    )
```

time: 64.2 us -> 37.5 us (0.58)
  other arithmetic: 24.5 us -> 0.01 us
  Pallas kernels: 0 us -> 7.54 us
  local copies, waits for them, and re-layouts: 6.84 us -> 0 us
  waiting for transfers between devices: 17.8 us -> 14 us
  starting transfers between devices: 14.5 us -> 15.7 us
    another operation x6 -> x0, other arithmetic: 8.37 us -> none  [the longest x5 8.36 us: on_device(): return jnp.stack(results)]
    select_n x4 -> x0, other arithmetic: 8.16 us -> none  [masked(): jnp.where(own(scores[layer], step) < limits[layer], own(deltas[layer], st...]
    pallas_call x0 -> x6, Pallas kernels: none -> 7.54 us  [the longest x1 3.93 us: merge_all(): pl.pallas_call(rest_kernel, out_shape=[slab] * ((layers - 1) * (tasks - 1...]
    ppermute x6 -> x5, waiting for transfers between devices: 11.8 us -> 4.87 us  [shifted(): lax.ppermute(value, axis, [(source, (source + step) % size) for source in...]
    slice x4 -> x0, local copies, waits for them, and re-layouts: 6.71 us -> none  [the longest x1 4.07 us: masked(): scores[layer]]
    div x3 -> x0, other arithmetic: 5.73 us -> none  [the longest x2 5.72 us: inverse_probability(): return 1.0 / (0.2 + 0.7 * column_mean / (column_mean + grand_mean))]
    ppermute x4 -> x6, waiting for transfers between devices: 5.97 us -> 9.09 us  [crossed(): lax.ppermute(value, axis, [(source, source ^ mask) for source in range(la...]
    ppermute x4 -> x6, starting transfers between devices: 5.92 us -> 8.49 us  [crossed(): lax.ppermute(value, axis, [(source, source ^ mask) for source in range(la...]
  transfers between devices with their start and end apart: 10 -> 11, of which waited for: 4 -> 6; matrix products, arithmetic and copies ran while one was open for 31% -> 0% of each run, Pallas kernels for 0% -> 7%
where the time goes in v2:
time: 37.5 us; the launch traced here: 37.3 us
  starting transfers between devices  15.7 us (42%)
  waiting for transfers between devices  14 us (37%)
  Pallas kernels  7.54 us (20%)
    ppermute x6, waiting for transfers between devices, crossed(): lax.ppermute(value, axis, [(source, source ^ mask) for source in range(la...  9.09 us
    ppermute x6, starting transfers between devices, crossed(): lax.ppermute(value, axis, [(source, source ^ mask) for source in range(la...  8.49 us
    ppermute x5, starting transfers between devices, shifted(): lax.ppermute(value, axis, [(source, (source + step) % size) for source in...  7.25 us
    ppermute x5, waiting for transfers between devices, shifted(): lax.ppermute(value, axis, [(source, (source + step) % size) for source in...  4.87 us
    pallas_call x1, Pallas kernels, merge_all(): pl.pallas_call(rest_kernel, out_shape=[slab] * ((layers - 1) * (tasks - 1...  3.93 us
    pallas_call x2, Pallas kernels, merge_all(): pl.pallas_call(functools.partial(merge_layers, picked, tasks, len(extra))...  2.1 us
    pallas_call x1, Pallas kernels, merge_all(): pl.pallas_call(first_kernel, out_shape=[slab] * (tasks - 1), in_specs=[AN...  1.23 us
  transfers between devices with their start and end apart: 11, of which 6 were waited for; matrix products, arithmetic and copies ran while one was open for 0% of the time, Pallas kernels for 7%

profile of v2, /device:TPU:0, one launch (start us, length us, event | category | flops | bytes accessed | tf_op | source)
XLA Modules:
  0.0 37.3 jit_solution(15822144424701173705)
XLA Ops:
  0.0 3.9 %rest.1 = (bf16[16,8192]{1,0:T(8,128)(2,1)}, bf16[16,8192]{1,0:T(8,128)(2,1)}, bf16[16,8192]{1,0:T(8,128)(2,1)}, bf16[8,4352]{1,0:T(8,128)(2,1)S(1)}, bf16[8,435...) custom-call(s32[1,4,8]{2,1,0:T(4,128)} %limits.3, bf16[1,4,16,16384]{3,2,1,0:T(8,128)(2,1)} %deltas.3, ...), custom_call_target="tpu_custom_call" | custom-call | flops 10000000 | bytes 6291456 | tf_op jit(solution)/shard_map/rest/pallas_call | solution.py:228
  3.9 3.1 %collective-permute-start.1 = (bf16[8,4352]{1,0:T(8,128)(2,1)S(1)}, bf16[8,4352]{1,0:T(8,128)(2,1)S(1)}, u32[]{:S(2)}, u32[]{:S(2)}) collective-permute-start(bf16[8,4352]{1,0:T(8,128)(2,1)S(1)} %get-tuple-element.14), channel_id=1, source_target_pairs={{0,1},{1,0},{2,3},{3,2},{4,5},{5,4},{6,7},{7,6},{8,9},{9,8},{10,11... | collective-permute-start | bytes 208904 | tf_op jit(solution)/shard_map/ppermute | solution.py:30
  7.0 0.0 collective-permute-start
  7.0 2.3 %collective-permute-done.1.refs_2_ = bf16[8,4352]{1,0:T(8,128)(2,1)S(1)} collective-permute-done((bf16[8,4352]{1,0:T(8,128)(2,1)S(1)}, bf16[8,4352]{1,0:T(8,128)(2,1)S(1)}, u32[]{:S(2)}, u32[]{:S(2)}) %collective-permute-start.1) | collective-permute-done | bytes 69664 | tf_op jit(solution)/shard_map/ppermute | solution.py:30
  9.3 1.2 %first.1 = bf16[16,8192]{1,0:T(8,128)(2,1)S(1)} custom-call(s32[1,4,8]{2,1,0:T(4,128)} %limits.3, bf16[1,4,16,16384]{3,2,1,0:T(8,128)(2,1)} %deltas.3, s32[1,4,16,16384]{3,2,1,0:T(8,128)} %scores.3), custom_call_target="tpu_custom_call" | custom-call | flops 1000000 | bytes 786432 | tf_op jit(solution)/shard_map/first/pallas_call | solution.py:212
  10.5 2.1 %collective-permute-start.8 = (bf16[16,8192]{1,0:T(8,128)(2,1)S(1)}, bf16[16,8192]{1,0:T(8,128)(2,1)S(1)}, u32[]{:S(2)}, u32[]{:S(2)}) collective-permute-start(bf16[16,8192]{1,0:T(8,128)(2,1)S(1)} %first.1), channel_id=1, source_target_pairs={{0,1},{1,0},{2,3},{3,2},{4,5},{5,4},{6,7},{7,6},{8,9},{9,8},{10,11... | collective-permute-start | bytes 786440 | tf_op jit(solution)/shard_map/ppermute | solution.py:30
  12.6 0.1 collective-permute-start.9
  12.7 1.9 %collective-permute-start.10 = (bf16[16,8192]{1,0:T(8,128)(2,1)}, bf16[16,8192]{1,0:T(8,128)(2,1)S(1)}, u32[]{:S(2)}, u32[]{:S(2)}) collective-permute-start(bf16[16,8192]{1,0:T(8,128)(2,1)} %get-tuple-element.20), channel_id=1, source_target_pairs={{0,1},{1,0},{2,3},{3,2},{4,5},{5,4},{6,7},{7,6},{8,9},{9,8},{10,11... | collective-permute-start | bytes 786440 | tf_op jit(solution)/shard_map/ppermute | solution.py:30
  14.6 0.0 collective-permute-done.refs_1_
  14.6 0.1 collective-permute-start.7
  14.8 2.0 %collective-permute-start.3 = (f32[2,8,128]{2,1,0:T(8,128)S(1)}, f32[2,8,128]{2,1,0:T(8,128)S(1)}, u32[]{:S(2)}, u32[]{:S(2)}) collective-permute-start(f32[2,8,128]{2,1,0:T(8,128)S(1)} %get-tuple-element.16), channel_id=1, source_target_pairs={{0,4},{2,6},{4,0},{6,2},{8,12},{10,14},{12,8},{14,10},{16,20},{18,... | collective-permute-start | bytes 24584 | tf_op jit(solution)/shard_map/ppermute | solution.py:21
  16.8 1.7 %collective-permute-done.3 = f32[2,8,128]{2,1,0:T(8,128)S(1)} collective-permute-done((f32[2,8,128]{2,1,0:T(8,128)S(1)}, f32[2,8,128]{2,1,0:T(8,128)S(1)}, u32[]{:S(2)}, u32[]{:S(2)}) %collective-permute-start.3) | collective-permute-done | bytes 8224 | tf_op jit(solution)/shard_map/ppermute | solution.py:21
  18.5 4.0 %collective-permute-start.6 = (f32[2,8,128]{2,1,0:T(8,128)S(1)}, f32[2,8,128]{2,1,0:T(8,128)S(1)}, u32[]{:S(2)}, u32[]{:S(2)}) collective-permute-start(f32[2,8,128]{2,1,0:T(8,128)S(1)} %add.12), channel_id=1, source_target_pairs={{0,24},{2,26},{4,28},{6,30},{8,16},{10,18},{12,20},{14,22},{16,8},... | collective-permute-start | bytes 24584 | tf_op jit(solution)/shard_map/ppermute | solution.py:21
  22.5 1.6 %collective-permute-done.6 = f32[2,8,128]{2,1,0:T(8,128)S(1)} collective-permute-done((f32[2,8,128]{2,1,0:T(8,128)S(1)}, f32[2,8,128]{2,1,0:T(8,128)S(1)}, u32[]{:S(2)}, u32[]{:S(2)}) %collective-permute-start.6) | collective-permute-done | bytes 8224 | tf_op jit(solution)/shard_map/ppermute | solution.py:21
  24.1 1.0 %collective-permute-start.5 = (f32[2,8,128]{2,1,0:T(8,128)S(1)}, f32[2,8,128]{2,1,0:T(8,128)S(1)}, u32[]{:S(2)}, u32[]{:S(2)}) collective-permute-start(f32[2,8,128]{2,1,0:T(8,128)S(1)} %add.12), channel_id=1, source_target_pairs={{0,16},{2,18},{4,20},{6,22},{8,24},{10,26},{12,28},{14,30},{16,0},... | collective-permute-start | bytes 24584 | tf_op jit(solution)/shard_map/ppermute | solution.py:21
  25.2 3.5 %collective-permute-done.5 = f32[2,8,128]{2,1,0:T(8,128)S(1)} collective-permute-done((f32[2,8,128]{2,1,0:T(8,128)S(1)}, f32[2,8,128]{2,1,0:T(8,128)S(1)}, u32[]{:S(2)}, u32[]{:S(2)}) %collective-permute-start.5) | collective-permute-done | bytes 8224 | tf_op jit(solution)/shard_map/ppermute | solution.py:21
  28.7 1.5 %collective-permute-start.4 = (f32[2,8,128]{2,1,0:T(8,128)S(1)}, f32[2,8,128]{2,1,0:T(8,128)S(1)}, u32[]{:S(2)}, u32[]{:S(2)}) collective-permute-start(f32[2,8,128]{2,1,0:T(8,128)S(1)} %add.12), channel_id=1, source_target_pairs={{0,8},{2,10},{4,12},{6,14},{8,0},{10,2},{12,4},{14,6},{16,24},{18,... | collective-permute-start | bytes 24584 | tf_op jit(solution)/shard_map/ppermute | solution.py:21
  30.2 2.2 %collective-permute-done.4 = f32[2,8,128]{2,1,0:T(8,128)S(1)} collective-permute-done((f32[2,8,128]{2,1,0:T(8,128)S(1)}, f32[2,8,128]{2,1,0:T(8,128)S(1)}, u32[]{:S(2)}, u32[]{:S(2)}) %collective-permute-start.4) | collective-permute-done | bytes 8224 | tf_op jit(solution)/shard_map/ppermute | solution.py:21
  32.4 0.2 scale.1.scales
  32.6 0.0 collective-permute-done.9.refs_1_
  32.6 0.0 collective-permute-done.10.refs_2_
  32.6 1.2 %merge.1.refs_1_ = bf16[4,16,8192]{2,1,0:T(8,128)(2,1)} custom-call(f32[2,8,4096]{2,1,0:T(8,128)S(1)} %scale.1.scales, bf16[4,16,8192]{2,1,0:T(8,128)(2,1)S(1)} %get-tuple-element.17.own, bf16[16,8192]{1,0:T(8,128)(2,1)S(1)} %collective-permute-done.8.refs_0_, bf16[16,8192]{1,0:T(8,128)(2,1)S(1)} %collective-permute-done.9.refs_1_, ...), custom_call_target="tpu_custom_call" | custom-call | flops 1000000 | bytes 2359296 | tf_op jit(solution)/shard_map/merge/pallas_call | solution.py:285
  33.9 2.6 %collective-permute-done.7.refs_0_ = bf16[16,8192]{1,0:T(8,128)(2,1)S(1)} collective-permute-done((bf16[16,8192]{1,0:T(8,128)(2,1)}, bf16[16,8192]{1,0:T(8,128)(2,1)S(1)}, u32[]{:S(2)}, u32[]{:S(2)}) %collective-permute-start.7) | collective-permute-done | bytes 262176 | tf_op jit(solution)/shard_map/ppermute | solution.py:30
  36.4 0.9 %merge_last.1 = bf16[4,16,8192]{2,1,0:T(8,128)(2,1)} custom-call(f32[2,8,4096]{2,1,0:T(8,128)S(1)} %scale.1.scales, bf16[4,16,8192]{2,1,0:T(8,128)(2,1)S(1)} %get-tuple-element.17.own, bf16[16,8192]{1,0:T(8,128)(2,1)S(1)} %collective-permute-done.7.refs_0_, bf16[4,16,8192]{2,1,0:T(8,128)(2,1)} %merge.1.refs_1_), custom_call_target="tpu_custom_call", output_to_operand_aliasing={{}: (3, {})} | custom-call | flops 1000000 | bytes 786432 | tf_op jit(solution)/shard_map/merge_last/pallas_call | solution.py:285
  (6 shorter events, 0.1 us)
Async XLA Ops:
  3.9 5.4 %collective-permute-start.1 = (bf16[8,4352]{1,0:T(8,128)(2,1)S(1)}, bf16[8,4352]{1,0:T(8,128)(2,1)S(1)}, u32[]{:S(2)}, u32[]{:S(2)}) collective-permute-start(bf16[8,4352]{1,0:T(8,128)(2,1)S(1)} %get-tuple-element.14), channel_id=1, source_target_pairs={{0,1},{1,0},{2,3},{3,2},{4,5},{5,4},{6,7},{7,6},{8,9},{9,8},{10,11... | collective-permute-start | bytes 208904 | tf_op jit(solution)/shard_map/ppermute | solution.py:30
  7.0 7.6 %collective-permute-start = (bf16[8,4352]{1,0:T(8,128)(2,1)S(1)}, bf16[8,4352]{1,0:T(8,128)(2,1)S(1)}, u32[]{:S(2)}, u32[]{:S(2)}) collective-permute-start(bf16[8,4352]{1,0:T(8,128)(2,1)S(1)} %get-tuple-element.13.refs_0_), channel_id=1, source_target_pairs={{0,2},{2,0},{4,6},{6,4},{8,10},{10,8},{12,14},{14,12},{16,18},{18,... | collective-permute-start | bytes 208904 | tf_op jit(solution)/shard_map/ppermute | solution.py:21
  9.3 5.4 %collective-permute-start.2 = (bf16[8,4352]{1,0:T(8,128)(2,1)S(1)}, bf16[8,4352]{1,0:T(8,128)(2,1)S(1)}, u32[]{:S(2)}, u32[]{:S(2)}) collective-permute-start(bf16[8,4352]{1,0:T(8,128)(2,1)S(1)} %collective-permute-done.1.refs_2_), channel_id=1, source_target_pairs={{0,2},{2,0},{4,6},{6,4},{8,10},{10,8},{12,14},{14,12},{16,18},{18,... | collective-permute-start | bytes 208904 | tf_op jit(solution)/shard_map/ppermute | solution.py:21
  10.5 22.1 %collective-permute-start.8 = (bf16[16,8192]{1,0:T(8,128)(2,1)S(1)}, bf16[16,8192]{1,0:T(8,128)(2,1)S(1)}, u32[]{:S(2)}, u32[]{:S(2)}) collective-permute-start(bf16[16,8192]{1,0:T(8,128)(2,1)S(1)} %first.1), channel_id=1, source_target_pairs={{0,1},{1,0},{2,3},{3,2},{4,5},{5,4},{6,7},{7,6},{8,9},{9,8},{10,11... | collective-permute-start | bytes 786440 | tf_op jit(solution)/shard_map/ppermute | solution.py:30
  12.6 20.0 %collective-permute-start.9 = (bf16[16,8192]{1,0:T(8,128)(2,1)}, bf16[16,8192]{1,0:T(8,128)(2,1)S(1)}, u32[]{:S(2)}, u32[]{:S(2)}) collective-permute-start(bf16[16,8192]{1,0:T(8,128)(2,1)} %get-tuple-element.19), channel_id=1, source_target_pairs={{0,1},{1,0},{2,3},{3,2},{4,5},{5,4},{6,7},{7,6},{8,9},{9,8},{10,11... | collective-permute-start | bytes 786440 | tf_op jit(solution)/shard_map/ppermute | solution.py:30
  12.7 19.9 %collective-permute-start.10 = (bf16[16,8192]{1,0:T(8,128)(2,1)}, bf16[16,8192]{1,0:T(8,128)(2,1)S(1)}, u32[]{:S(2)}, u32[]{:S(2)}) collective-permute-start(bf16[16,8192]{1,0:T(8,128)(2,1)} %get-tuple-element.20), channel_id=1, source_target_pairs={{0,1},{1,0},{2,3},{3,2},{4,5},{5,4},{6,7},{7,6},{8,9},{9,8},{10,11... | collective-permute-start | bytes 786440 | tf_op jit(solution)/shard_map/ppermute | solution.py:30
  14.6 21.8 %collective-permute-start.7 = (bf16[16,8192]{1,0:T(8,128)(2,1)}, bf16[16,8192]{1,0:T(8,128)(2,1)S(1)}, u32[]{:S(2)}, u32[]{:S(2)}) collective-permute-start(bf16[16,8192]{1,0:T(8,128)(2,1)} %get-tuple-element.18), channel_id=1, source_target_pairs={{0,1},{1,0},{2,3},{3,2},{4,5},{5,4},{6,7},{7,6},{8,9},{9,8},{10,11... | collective-permute-start | bytes 786440 | tf_op jit(solution)/shard_map/ppermute | solution.py:30
  14.8 3.7 %collective-permute-start.3 = (f32[2,8,128]{2,1,0:T(8,128)S(1)}, f32[2,8,128]{2,1,0:T(8,128)S(1)}, u32[]{:S(2)}, u32[]{:S(2)}) collective-permute-start(f32[2,8,128]{2,1,0:T(8,128)S(1)} %get-tuple-element.16), channel_id=1, source_target_pairs={{0,4},{2,6},{4,0},{6,2},{8,12},{10,14},{12,8},{14,10},{16,20},{18,... | collective-permute-start | bytes 24584 | tf_op jit(solution)/shard_map/ppermute | solution.py:21
  18.5 5.7 %collective-permute-start.6 = (f32[2,8,128]{2,1,0:T(8,128)S(1)}, f32[2,8,128]{2,1,0:T(8,128)S(1)}, u32[]{:S(2)}, u32[]{:S(2)}) collective-permute-start(f32[2,8,128]{2,1,0:T(8,128)S(1)} %add.12), channel_id=1, source_target_pairs={{0,24},{2,26},{4,28},{6,30},{8,16},{10,18},{12,20},{14,22},{16,8},... | collective-permute-start | bytes 24584 | tf_op jit(solution)/shard_map/ppermute | solution.py:21
  24.1 4.5 %collective-permute-start.5 = (f32[2,8,128]{2,1,0:T(8,128)S(1)}, f32[2,8,128]{2,1,0:T(8,128)S(1)}, u32[]{:S(2)}, u32[]{:S(2)}) collective-permute-start(f32[2,8,128]{2,1,0:T(8,128)S(1)} %add.12), channel_id=1, source_target_pairs={{0,16},{2,18},{4,20},{6,22},{8,24},{10,26},{12,28},{14,30},{16,0},... | collective-permute-start | bytes 24584 | tf_op jit(solution)/shard_map/ppermute | solution.py:21
  28.7 3.7 %collective-permute-start.4 = (f32[2,8,128]{2,1,0:T(8,128)S(1)}, f32[2,8,128]{2,1,0:T(8,128)S(1)}, u32[]{:S(2)}, u32[]{:S(2)}) collective-permute-start(f32[2,8,128]{2,1,0:T(8,128)S(1)} %add.12), channel_id=1, source_target_pairs={{0,8},{2,10},{4,12},{6,14},{8,0},{10,2},{12,4},{14,6},{16,24},{18,... | collective-permute-start | bytes 24584 | tf_op jit(solution)/shard_map/ppermute | solution.py:21

commit v3 on v2

v3 whole, which is shorter than its diff:
```python
import functools
import math

import jax
import jax.numpy as jnp
from jax import lax
from jax.experimental import pallas as pl
from jax.experimental.pallas import tpu as pltpu
from jax.sharding import PartitionSpec as P


EXPERTS = 8
FF = 16384
LANES = 128
BLOCK = 1024
PIECES = 4
GRANT = 16 * 2**20

ANY = pl.BlockSpec(memory_space=pl.ANY)
HBM = pl.BlockSpec(memory_space=pltpu.HBM)
VMEM = pl.BlockSpec(memory_space=pltpu.VMEM)


def crossed(value, axis, mask):
    return lax.ppermute(value, axis, [(source, source ^ mask) for source in range(lax.axis_size(axis))])


def swapped(value, axis, bit):
    return crossed(value, axis, 1 << bit)


def shifted(value, step):
    size = lax.axis_size("task")
    return lax.ppermute(value, "task", [(source, (source + step) % size) for source in range(size)])


def column_start(step, columns):
    tasks = lax.axis_size("task")
    return lax.rem(lax.axis_index("task") + step, tasks) * columns


def own_expert():
    return lax.axis_index("shard") // (lax.axis_size("shard") // EXPERTS)


def blocks(width, body):
    block = math.gcd(BLOCK, width)

    @pl.loop(0, width // block)
    def _(at):
        body(pl.multiple_of(at * block, block), block)


def chunk_plan(layers):
    last = layers - 1
    return [[(0, 0, 4)], [(layer, 0, 4) for layer in range(1, last)], [(last, 0, 3)], [(last, 3, 4)]]


def chunk_width(chunk, columns):
    return sum(end - begin for _, begin, end in chunk) * columns // 4


def mask_block(deltas, scores, limit):
    return jnp.where(scores < limit, deltas.astype(jnp.float32), 0.0).astype(jnp.bfloat16)


def first_kernel(limits, deltas, scores, *refs):
    tasks = lax.axis_size("task")
    outs = refs[: tasks - 1]
    limit_buf, delta_buf, score_buf, sems = refs[tasks - 1 :]
    columns = outs[0].shape[1]
    block = columns // PIECES
    limit_copy = pltpu.make_async_copy(limits, limit_buf, sems.at[0])
    limit_copy.start()
    work = [(step, piece) for step in range(1, tasks) for piece in range(PIECES)]
    copies = []
    for at, (step, piece) in enumerate(work):
        source = pl.ds(pl.multiple_of(column_start(step, columns) + piece * block, LANES), block)
        target = pl.ds(piece * block, block)
        copies.append([
            pltpu.make_async_copy(scores.at[0, 0, :, source], score_buf.at[step - 1, :, target], sems.at[2 * at + 1]),
            pltpu.make_async_copy(deltas.at[0, 0, :, source], delta_buf.at[step - 1, :, target], sems.at[2 * at + 2]),
        ])
        for copy in copies[-1]:
            copy.start()
    limit_copy.wait()
    limit = limit_buf[0, 0, own_expert()]
    for at, (step, piece) in enumerate(work):
        for copy in copies[at]:
            copy.wait()
        where = pl.ds(piece * block, block)
        outs[step - 1][:, where] = mask_block(delta_buf[step - 1, :, where], score_buf[step - 1, :, where], limit)


def row_sums(changes):
    values = [change.astype(jnp.float32) for change in changes]
    values = [sum(value[at : at + 8] for at in range(8, value.shape[0], 8)) + value[:8] for value in values]
    if len(values) != 8:
        return jnp.concatenate([jnp.sum(value, axis=0, keepdims=True) for value in values], axis=0)
    lane = lax.broadcasted_iota(jnp.int32, values[0].shape, 0)
    for shift in (4, 2, 1):
        low = lane % (2 * shift) < shift
        values = [
            jnp.where(low, one + pltpu.roll(one, 8 - shift, 0), two + pltpu.roll(two, shift, 0))
            for one, two in zip(values[:shift], values[shift:])
        ]
    return values[0]


def sums_kernel(deltas, copied, packs, sems):
    tasks, folded, packed = packs.shape
    half = packed - 2 * LANES
    layers, rows, _ = copied.shape
    columns = 2 * half
    block = min(BLOCK, half)
    places = half // block
    groups = lax.axis_size("shard") // EXPERTS
    work = [(step, place) for step in range(tasks) for place in range(places)]
    copies = []
    sources = []
    for step, place in work:
        start = column_start(step, columns) + place * block
        sources.append([pl.ds(pl.multiple_of(start + part * half, LANES), block) for part in range(2)])
        copies.append([
            pltpu.make_async_copy(deltas.at[0, :, :, source], copied.at[:, :, source], sems.at[2 * len(copies) + part])
            for part, source in enumerate(sources[-1])
        ])
        for copy in copies[-1]:
            copy.start()
    totals = jnp.zeros((folded, LANES), jnp.float32)
    for at, (step, place) in enumerate(work):
        for copy in copies[at]:
            copy.wait()
        sums = row_sums([jnp.abs(copied[layer, :, source]) for source in sources[at] for layer in range(layers)])
        means = sums * (1.0 / (rows * groups))
        packs[step, :, place * block : (place + 1) * block] = means.astype(jnp.bfloat16)
        for tile in range(0, block, LANES):
            totals = totals + means[:, tile : tile + LANES]
    for step in range(tasks):
        store_split(packs.at[step], totals)


def store_split(pack, totals):
    half = pack.shape[1] - 2 * LANES
    high = totals.astype(jnp.bfloat16)
    pack[:, half : half + LANES] = high
    pack[:, half + LANES :] = (totals - high.astype(jnp.float32)).astype(jnp.bfloat16)


def mask_kernel(chunks, own_layers, limits, scores, copied, *refs):
    tasks = lax.axis_size("task")
    _, _, width = copied.shape
    columns = width // tasks
    count = len(chunks) * (tasks - 1)
    sent, refs = refs[:count], refs[count:]
    if own_layers:
        own, refs = refs[0], refs[1:]
    limit_buf, score_buf, sems = refs
    limit_copy = pltpu.make_async_copy(limits, limit_buf, sems.at[0])
    limit_copy.start()
    work = []
    for at, chunk in enumerate(chunks):
        for step in range(1, tasks):
            offset = 0
            for layer, begin, end in chunk:
                size = (end - begin) * columns // 4
                work.append((sent[at * (tasks - 1) + step - 1], offset, layer, step, begin * columns // 4, size))
                offset += size
    work += [(own.at[layer], 0, layer, 0, 0, columns) for layer in own_layers]
    copies = []
    for at, (_, _, layer, step, begin, size) in enumerate(work):
        source = pl.ds(pl.multiple_of(column_start(step, columns) + begin, LANES), size)
        copies.append(pltpu.make_async_copy(scores.at[0, layer, :, source], score_buf.at[at, :, :size], sems.at[at + 1]))
        copies[-1].start()
    limit_copy.wait()
    for at, (target, offset, layer, step, begin, size) in enumerate(work):
        start = column_start(step, columns) + begin
        limit = limit_buf[0, layer, own_expert()]
        copies[at].wait()

        def body(place, block):
            change = copied[layer, :, pl.ds(pl.multiple_of(start + place, LANES), block)]
            kept = mask_block(change, score_buf[at, :, pl.ds(place, block)], limit)
            target[:, pl.ds(pl.multiple_of(offset + place, LANES), block)] = kept

        blocks(size, body)


def slot_lanes(width):
    return pl.ds(pl.multiple_of(lax.rem(lax.axis_index("shard"), 2) * width, LANES), width)


def pair_kernel(mine, theirs, means, totals, *refs):
    packs, both_buf = refs[:-1], refs[-1]
    tasks, _, packed = mine.shape
    half = packed - 2 * LANES
    both = mine[...].astype(jnp.float32) + theirs[...].astype(jnp.float32)
    both_buf[...] = both
    means[...] = both[0, :, :half]
    total = both[0, :, half : half + LANES] + both[0, :, half + LANES :]
    totals[...] = total
    for step in range(1, tasks):
        packs[step - 1][:, : half // 2] = both_buf[step, :, slot_lanes(half // 2)].astype(jnp.bfloat16)
        store_split(packs[step - 1], total)


def join_kernel(own_means, own_totals, *refs):
    tasks = lax.axis_size("task")
    means, totals = refs[2 * tasks - 2 :]
    half = means.shape[2]
    quarter = half // 2
    means[0] = own_means[...]
    totals[0] = own_totals[...]
    other = lax.rem(lax.axis_index("shard") + 1, 2) * quarter
    for step in range(1, tasks):
        mine, theirs = refs[2 * step - 2 : 2 * step]
        means[step, :, slot_lanes(quarter)] = mine[:, :quarter].astype(jnp.float32)
        means[step, :, pl.ds(pl.multiple_of(other, LANES), quarter)] = theirs[:, :quarter].astype(jnp.float32)
        both = mine[:, quarter:].astype(jnp.float32)
        totals[step] = both[:, :LANES] + both[:, LANES:]


def scale_kernel(means, totals, scales):
    tasks, folded, _ = means.shape
    for step in range(tasks):
        total = jnp.sum(totals[step], axis=1, keepdims=True)
        total = total + jnp.concatenate([total[folded // 2 :], total[: folded // 2]], axis=0)
        grand = total * (1.0 / (EXPERTS * FF))
        mean = means[step]
        rounded = (0.2 + 0.7 * mean / (mean + grand)).astype(jnp.bfloat16)
        scales[step] = 1.0 / rounded.astype(jnp.float32)


def merge_kernel(chunk, tasks, aliased, scales, own, *refs):
    half = scales.shape[2]
    layers = own.shape[0]
    columns = 2 * half
    arrived = refs[: tasks - 1]
    out, buf, sems = refs[tasks - 1 + aliased :]
    pieces = []
    offset = 0
    for layer, begin, end in chunk:
        for part in range(2):
            low, high = [min(max(at * columns // 4 - part * half, 0), half) for at in (begin, end)]
            if high > low:
                pieces.append((layer, part, low, high - low, offset))
                offset += high - low
    copies = []
    for at, (layer, part, low, size, offset) in enumerate(pieces):
        row = part * layers + layer

        def body(place, block):
            narrow = pl.ds(pl.multiple_of(low + place, LANES), block)
            source = pl.ds(pl.multiple_of(part * half + low + place, LANES), block)
            target = pl.ds(pl.multiple_of(offset + place, LANES), block)
            merged = own[layer, :, source].astype(jnp.float32) * scales[0, row : row + 1, narrow]
            for step in range(1, tasks):
                other = arrived[step - 1][:, target].astype(jnp.float32)
                merged = merged + other * scales[step, row : row + 1, narrow]
            buf[:, target] = merged.astype(jnp.bfloat16)

        blocks(size, body)
        copies.append(pltpu.make_async_copy(
            buf.at[:, pl.ds(offset, size)], out.at[layer, :, pl.ds(part * half + low, size)], sems.at[at]))
        copies[-1].start()
    for copy in copies:
        copy.wait()


def cost(flops, moved):
    return pl.CostEstimate(flops=flops, bytes_accessed=moved, transcendentals=0)


def on_chip(value):
    return pltpu.with_memory_space_constraint(value, pltpu.VMEM)


def merge_all(task_deltas, rank_scores, keep_limits):
    shards, tasks = lax.axis_size("shard"), lax.axis_size("task")
    groups = shards // EXPERTS
    group_bits = groups.bit_length() - 1
    layers, rows, width = task_deltas.shape[1:]
    columns = width // tasks
    half = columns // 2
    block = min(BLOCK, half)
    bf16, f32 = jnp.bfloat16, jnp.float32
    plan = chunk_plan(layers)
    slabs = [pltpu.VMEM((rows, chunk_width(chunk, columns)), bf16) for chunk in plan]

    task_deltas, rank_scores, keep_limits = [
        pltpu.with_memory_space_constraint(value, pltpu.HBM) for value in (task_deltas, rank_scores, keep_limits)
    ]
    first = pl.pallas_call(
        first_kernel,
        out_shape=[slabs[0]] * (tasks - 1),
        in_specs=[HBM] * 3,
        out_specs=[VMEM] * (tasks - 1),
        scratch_shapes=[
            pltpu.SMEM(keep_limits.shape, jnp.int32),
            pltpu.VMEM((tasks - 1, rows, columns), bf16),
            pltpu.VMEM((tasks - 1, rows, columns), jnp.int32),
            pltpu.SemaphoreType.DMA((2 * PIECES * (tasks - 1) + 1,)),
        ],
        compiler_params=pltpu.CompilerParams(vmem_limit_bytes=GRANT),
        cost_estimate=cost(10**6, 6 * rows * columns),
        name="first",
    )(keep_limits, task_deltas, rank_scores)
    arrived = [[shifted(first[step - 1], step) for step in range(1, tasks)]]

    pack = (2 * layers, half + 2 * LANES)
    copied, packs = pl.pallas_call(
        sums_kernel,
        out_shape=[pltpu.VMEM((layers, rows, width), bf16), pltpu.VMEM((tasks, *pack), bf16)],
        in_specs=[HBM],
        out_specs=[VMEM] * 2,
        scratch_shapes=[pltpu.SemaphoreType.DMA((2 * tasks * half // block,))],
        compiler_params=pltpu.CompilerParams(vmem_limit_bytes=GRANT),
        cost_estimate=cost(10**7, 2 * layers * rows * width),
        name="sums",
    )(task_deltas)

    def masks(places, own_layers):
        chunks = [plan[place] for place in places]
        shapes = [slabs[place] for place in places for _ in range(1, tasks)]
        shapes += [pltpu.VMEM((layers, rows, columns), bf16)] * bool(own_layers)
        pieces = sum(len(chunk) for chunk in chunks) * (tasks - 1) + len(own_layers)
        return pl.pallas_call(
            functools.partial(mask_kernel, chunks, own_layers),
            out_shape=shapes,
            in_specs=[HBM] * 2 + [VMEM],
            out_specs=[VMEM] * len(shapes),
            scratch_shapes=[
                pltpu.SMEM(keep_limits.shape, jnp.int32),
                pltpu.VMEM((pieces, rows, columns), jnp.int32),
                pltpu.SemaphoreType.DMA((pieces + 1,)),
            ],
            compiler_params=pltpu.CompilerParams(vmem_limit_bytes=GRANT),
            cost_estimate=cost(10**7, 6 * pieces * rows * columns),
            name="masks",
        )(keep_limits, rank_scores, on_chip(copied))

    for bit in range(1, group_bits):
        packs = packs.astype(f32) + swapped(packs, "shard", bit).astype(f32)
    theirs = swapped(packs, "shard", 0)
    sent = [*masks([1], [])]
    means, totals, *packs = pl.pallas_call(
        pair_kernel,
        out_shape=[pltpu.VMEM((2 * layers, half), f32), pltpu.VMEM((2 * layers, LANES), f32)]
        + [pltpu.VMEM((2 * layers, half // 2 + 2 * LANES), bf16)] * (tasks - 1),
        in_specs=[VMEM] * 2,
        out_specs=[VMEM] * (tasks + 1),
        scratch_shapes=[pltpu.VMEM((tasks, *pack), f32)],
        compiler_params=pltpu.CompilerParams(vmem_limit_bytes=GRANT),
        cost_estimate=cost(10**6, 8 * tasks * layers * half),
        name="pair",
    )(on_chip(packs), on_chip(theirs))
    arrivals = [shifted(packs[step - 1], step) for step in range(1, tasks)]
    arrived.append([shifted(sent[step - 1], step) for step in range(1, tasks)])
    sent += masks([*range(2, len(plan))], [])
    (own,) = masks([], [*range(layers)])
    pairs = []
    for arrival in arrivals:
        pairs += [arrival, swapped(arrival, "shard", 0)]
    for place in range(2, len(plan)):
        at = (place - 1) * (tasks - 1)
        arrived.append([shifted(sent[at + step - 1], step) for step in range(1, tasks)])

    means, totals = pl.pallas_call(
        join_kernel,
        out_shape=[pltpu.VMEM((tasks, 2 * layers, half), f32), pltpu.VMEM((tasks, 2 * layers, LANES), f32)],
        in_specs=[VMEM] * (2 * tasks),
        out_specs=[VMEM] * 2,
        compiler_params=pltpu.CompilerParams(vmem_limit_bytes=GRANT),
        cost_estimate=cost(10**6, 8 * tasks * layers * half),
        name="join",
    )(on_chip(means), on_chip(totals), *[on_chip(value) for value in pairs])
    for bit in range(group_bits, shards.bit_length() - 1):
        totals = totals + swapped(totals, "shard", bit)

    scales = pl.pallas_call(
        scale_kernel,
        out_shape=pltpu.VMEM((tasks, 2 * layers, half), f32),
        in_specs=[VMEM] * 2,
        out_specs=VMEM,
        compiler_params=pltpu.CompilerParams(vmem_limit_bytes=GRANT),
        cost_estimate=cost(10**6, 8 * tasks * layers * half),
        name="scale",
    )(on_chip(means), on_chip(totals))

    out = None
    for chunk, pieces in zip(plan, arrived):
        extra = [] if out is None else [out]
        out = pl.pallas_call(
            functools.partial(merge_kernel, chunk, tasks, len(extra)),
            out_shape=jax.ShapeDtypeStruct((layers, rows, columns), bf16),
            in_specs=[VMEM] * (1 + tasks) + [ANY] * len(extra),
            out_specs=ANY,
            scratch_shapes=[
                pltpu.VMEM((rows, chunk_width(chunk, columns)), bf16),
                pltpu.SemaphoreType.DMA((2 * len(chunk),)),
            ],
            input_output_aliases={1 + tasks: 0} if extra else {},
            compiler_params=pltpu.CompilerParams(vmem_limit_bytes=GRANT),
            cost_estimate=cost(10**6, 6 * rows * chunk_width(chunk, columns)),
            name="merge",
        )(on_chip(scales), on_chip(own), *[on_chip(piece) for piece in pieces], *extra)
    return out


def solution(mesh):
    return jax.shard_map(
        merge_all,
        mesh=mesh,
        in_specs=(
            P("task", None, "shard", None),
            P("task", None, "shard", None),
            P("task", None, None),
        ),
        out_specs=P(None, "shard", "task"),
        check_vma=False,
    )
```

time: 37.5 us -> 46.6 us (1.24)
  waiting for transfers between devices: 14 us -> 21.6 us
  Pallas kernels: 7.54 us -> 10.9 us
  starting transfers between devices: 15.7 us -> 13.7 us
    ppermute x5, waiting for transfers between devices: 4.87 us -> 16.5 us  [shifted(): lax.ppermute(value, 'task', [(source, (source + step) % size) for source...]
    ppermute x6 -> x5, waiting for transfers between devices: 9.09 us -> 5.09 us  [crossed(): lax.ppermute(value, axis, [(source, source ^ mask) for source in range(la...]
    pallas_call x4 -> x10, Pallas kernels: 7.26 us -> 10.6 us  [the longest x3 4.11 us: masks(): pl.pallas_call(functools.partial(mask_kernel, chunks, own_layers), out_sh...]
    ppermute x6 -> x5, starting transfers between devices: 8.49 us -> 6.44 us  [crossed(): lax.ppermute(value, axis, [(source, source ^ mask) for source in range(la...]
  transfers between devices with their start and end apart: 11 -> 10, of which waited for: 6 -> 5; matrix products, arithmetic and copies ran while one was open for 0% -> 0% of each run, Pallas kernels for 7% -> 15%
where the time goes in v3:
time: 46.6 us; the launch traced here: 46.3 us
  waiting for transfers between devices  21.6 us (46%)
  starting transfers between devices  13.7 us (29%)
  Pallas kernels  10.9 us (23%)
    ppermute x5, waiting for transfers between devices, shifted(): lax.ppermute(value, 'task', [(source, (source + step) % size) for source...  16.5 us
    ppermute x5, starting transfers between devices, shifted(): lax.ppermute(value, 'task', [(source, (source + step) % size) for source...  7.23 us
    ppermute x5, starting transfers between devices, crossed(): lax.ppermute(value, axis, [(source, source ^ mask) for source in range(la...  6.44 us
    ppermute x5, waiting for transfers between devices, crossed(): lax.ppermute(value, axis, [(source, source ^ mask) for source in range(la...  5.09 us
    pallas_call x3, Pallas kernels, masks(): pl.pallas_call(functools.partial(mask_kernel, chunks, own_layers), out_sh...  4.11 us
    pallas_call x4, Pallas kernels, merge_all(): pl.pallas_call(functools.partial(merge_kernel, chunk, tasks, len(extra)),...  3.34 us
    pallas_call x1, Pallas kernels, merge_all(): pl.pallas_call(sums_kernel, out_shape=[pltpu.VMEM((layers, rows, width),...  1.84 us
    pallas_call x1, Pallas kernels, merge_all(): pl.pallas_call(first_kernel, out_shape=[slabs[0]] * (tasks - 1), in_specs...  1.28 us
  transfers between devices with their start and end apart: 10, of which 5 were waited for; matrix products, arithmetic and copies ran while one was open for 0% of the time, Pallas kernels for 15%

profile of v3, /device:TPU:0, one launch (start us, length us, event | category | flops | bytes accessed | tf_op | source)
XLA Modules:
  0.0 46.3 jit_solution(9992622493047178793)
XLA Ops:
  0.0 1.8 %sums.1 = (bf16[4,16,16384]{2,1,0:T(8,128)(2,1)S(1)}, bf16[2,8,4352]{2,1,0:T(8,128)(2,1)S(1)}) custom-call(bf16[1,4,16,16384]{3,2,1,0:T(8,128)(2,1)} %deltas.3), custom_call_target="tpu_custom_call" | custom-call | flops 10000000 | bytes 2097152 | tf_op jit(solution)/shard_map/sums/pallas_call | solution.py:311
  1.8 1.3 %masks.5 = bf16[16,16384]{1,0:T(8,128)(2,1)S(1)} custom-call(s32[1,4,8]{2,1,0:T(4,128)} %limits.7, s32[1,4,16,16384]{3,2,1,0:T(8,128)} %scores.7, bf16[4,16,16384]{2,1,0:T(8,128)(2,1)S(1)} %get-tuple-element.20.copied), custom_call_target="tpu_custom_call" | custom-call | flops 10000000 | bytes 1572864 | tf_op jit(solution)/shard_map/masks/pallas_call | solution.py:327
  3.2 3.1 %collective-permute-start.8 = (bf16[16,16384]{1,0:T(8,128)(2,1)S(1)}, bf16[16,16384]{1,0:T(8,128)(2,1)S(1)}, u32[]{:S(2)}, u32[]{:S(2)}) collective-permute-start(bf16[16,16384]{1,0:T(8,128)(2,1)S(1)} %masks.5), channel_id=1, source_target_pairs={{0,1},{1,0},{2,3},{3,2},{4,5},{5,4},{6,7},{7,6},{8,9},{9,8},{10,11... | collective-permute-start | bytes 1572872 | tf_op jit(solution)/shard_map/ppermute | solution.py:34
  6.2 1.3 %first.1 = bf16[16,8192]{1,0:T(8,128)(2,1)S(1)} custom-call(s32[1,4,8]{2,1,0:T(4,128)} %limits.7, bf16[1,4,16,16384]{3,2,1,0:T(8,128)(2,1)} %deltas.3, s32[1,4,16,16384]{3,2,1,0:T(8,128)} %scores.7), custom_call_target="tpu_custom_call" | custom-call | flops 1000000 | bytes 786432 | tf_op jit(solution)/shard_map/first/pallas_call | solution.py:293
  7.5 0.1 collective-permute-start.9
  7.6 0.1 collective-permute-start
  7.7 1.1 %masks.4 = (bf16[16,6144]{1,0:T(8,128)(2,1)S(1)}, bf16[16,2048]{1,0:T(8,128)(2,1)S(1)}) custom-call(s32[1,4,8]{2,1,0:T(4,128)} %limits.7, s32[1,4,16,16384]{3,2,1,0:T(8,128)} %scores.7, bf16[4,16,16384]{2,1,0:T(8,128)(2,1)S(1)} %get-tuple-element.20.copied), custom_call_target="tpu_custom_call" | custom-call | flops 10000000 | bytes 1572864 | tf_op jit(solution)/shard_map/masks/pallas_call | solution.py:327
  8.8 2.0 %collective-permute-start.7 = (bf16[16,6144]{1,0:T(8,128)(2,1)S(1)}, bf16[16,6144]{1,0:T(8,128)(2,1)S(1)}, u32[]{:S(2)}, u32[]{:S(2)}) collective-permute-start(bf16[16,6144]{1,0:T(8,128)(2,1)S(1)} %get-tuple-element.22), channel_id=1, source_target_pairs={{0,1},{1,0},{2,3},{3,2},{4,5},{5,4},{6,7},{7,6},{8,9},{9,8},{10,11... | collective-permute-start | bytes 589832 | tf_op jit(solution)/shard_map/ppermute | solution.py:34
  10.9 0.2 collective-permute-start.1
  11.1 1.9 %collective-permute-start.6 = (bf16[16,2048]{1,0:T(8,128)(2,1)S(1)}, bf16[16,2048]{1,0:T(8,128)(2,1)S(1)}, u32[]{:S(2)}, u32[]{:S(2)}) collective-permute-start(bf16[16,2048]{1,0:T(8,128)(2,1)S(1)} %get-tuple-element.21), channel_id=1, source_target_pairs={{0,1},{1,0},{2,3},{3,2},{4,5},{5,4},{6,7},{7,6},{8,9},{9,8},{10,11... | collective-permute-start | bytes 196616 | tf_op jit(solution)/shard_map/ppermute | solution.py:34
  13.0 16.5 %collective-permute-done.1.refs_0_ = bf16[8,2304]{1,0:T(8,128)(2,1)S(1)} collective-permute-done((bf16[8,2304]{1,0:T(8,128)(2,1)S(1)}, bf16[8,2304]{1,0:T(8,128)(2,1)S(1)}, u32[]{:S(2)}, u32[]{:S(2)}) %collective-permute-start.1) | collective-permute-done | bytes 36896 | tf_op jit(solution)/shard_map/ppermute | solution.py:34
  29.5 1.2 %collective-permute-done.2.refs_1_ = bf16[8,2304]{1,0:T(8,128)(2,1)S(1)} collective-permute-done((bf16[8,2304]{1,0:T(8,128)(2,1)S(1)}, bf16[8,2304]{1,0:T(8,128)(2,1)S(1)}, u32[]{:S(2)}, u32[]{:S(2)}) %collective-permute-start.2) | collective-permute-done | bytes 36896 | tf_op jit(solution)/shard_map/ppermute | solution.py:25
  30.7 1.8 %collective-permute-start.3 = (f32[2,8,128]{2,1,0:T(8,128)S(1)}, f32[2,8,128]{2,1,0:T(8,128)S(1)}, u32[]{:S(2)}, u32[]{:S(2)}) collective-permute-start(f32[2,8,128]{2,1,0:T(8,128)S(1)} %get-tuple-element.19), channel_id=1, source_target_pairs={{0,4},{2,6},{4,0},{6,2},{8,12},{10,14},{12,8},{14,10},{16,20},{18,... | collective-permute-start | bytes 24584 | tf_op jit(solution)/shard_map/ppermute | solution.py:25
  32.5 1.9 %collective-permute-done.3 = f32[2,8,128]{2,1,0:T(8,128)S(1)} collective-permute-done((f32[2,8,128]{2,1,0:T(8,128)S(1)}, f32[2,8,128]{2,1,0:T(8,128)S(1)}, u32[]{:S(2)}, u32[]{:S(2)}) %collective-permute-start.3) | collective-permute-done | bytes 8224 | tf_op jit(solution)/shard_map/ppermute | solution.py:25
  34.5 1.8 %collective-permute-start.4 = (f32[2,8,128]{2,1,0:T(8,128)S(1)}, f32[2,8,128]{2,1,0:T(8,128)S(1)}, u32[]{:S(2)}, u32[]{:S(2)}) collective-permute-start(f32[2,8,128]{2,1,0:T(8,128)S(1)} %add.9), channel_id=1, source_target_pairs={{0,8},{2,10},{4,12},{6,14},{8,0},{10,2},{12,4},{14,6},{16,24},{18,... | collective-permute-start | bytes 24584 | tf_op jit(solution)/shard_map/ppermute | solution.py:25
  36.3 1.9 %collective-permute-done.4 = f32[2,8,128]{2,1,0:T(8,128)S(1)} collective-permute-done((f32[2,8,128]{2,1,0:T(8,128)S(1)}, f32[2,8,128]{2,1,0:T(8,128)S(1)}, u32[]{:S(2)}, u32[]{:S(2)}) %collective-permute-start.4) | collective-permute-done | bytes 8224 | tf_op jit(solution)/shard_map/ppermute | solution.py:25
  38.1 2.8 %collective-permute-start.5 = (f32[2,8,128]{2,1,0:T(8,128)S(1)}, f32[2,8,128]{2,1,0:T(8,128)S(1)}, u32[]{:S(2)}, u32[]{:S(2)}) collective-permute-start(f32[2,8,128]{2,1,0:T(8,128)S(1)} %add.10), channel_id=1, source_target_pairs={{0,16},{2,18},{4,20},{6,22},{8,24},{10,26},{12,28},{14,30},{16,0},... | collective-permute-start | bytes 24584 | tf_op jit(solution)/shard_map/ppermute | solution.py:25
  40.9 1.6 %masks.3.own = bf16[4,16,8192]{2,1,0:T(8,128)(2,1)S(1)} custom-call(s32[1,4,8]{2,1,0:T(4,128)} %limits.7, s32[1,4,16,16384]{3,2,1,0:T(8,128)} %scores.7, bf16[4,16,16384]{2,1,0:T(8,128)(2,1)S(1)} %get-tuple-element.20.copied), custom_call_target="tpu_custom_call" | custom-call | flops 10000000 | bytes 3145728 | tf_op jit(solution)/shard_map/masks/pallas_call | solution.py:327
  42.6 0.1 collective-permute-done.5
  42.7 0.2 scale.1.scales
  42.9 0.8 %merge.4.refs_1_ = bf16[4,16,8192]{2,1,0:T(8,128)(2,1)} custom-call(f32[2,8,4096]{2,1,0:T(8,128)S(1)} %scale.1.scales, bf16[4,16,8192]{2,1,0:T(8,128)(2,1)S(1)} %masks.3.own, bf16[16,8192]{1,0:T(8,128)(2,1)S(1)} %collective-permute-done.9.refs_0_), custom_call_target="tpu_custom_call" | custom-call | flops 1000000 | bytes 786432 | tf_op jit(solution)/shard_map/merge/pallas_call | solution.py:393
  43.8 1.0 %merge.5.refs_1_ = bf16[4,16,8192]{2,1,0:T(8,128)(2,1)} custom-call(f32[2,8,4096]{2,1,0:T(8,128)S(1)} %scale.1.scales, bf16[4,16,8192]{2,1,0:T(8,128)(2,1)S(1)} %masks.3.own, bf16[16,16384]{1,0:T(8,128)(2,1)S(1)} %collective-permute-done.8.refs_0_, bf16[4,16,8192]{2,1,0:T(8,128)(2,1)} %merge.4.refs_1_), custom_call_target="tpu_custom_call", output_to_operand_aliasing={{}: (3, {})} | custom-call | flops 1000000 | bytes 1572864 | tf_op jit(solution)/shard_map/merge/pallas_call | solution.py:393
  44.8 0.8 %merge.6.refs_1_ = bf16[4,16,8192]{2,1,0:T(8,128)(2,1)} custom-call(f32[2,8,4096]{2,1,0:T(8,128)S(1)} %scale.1.scales, bf16[4,16,8192]{2,1,0:T(8,128)(2,1)S(1)} %masks.3.own, bf16[16,6144]{1,0:T(8,128)(2,1)S(1)} %collective-permute-done.7.refs_0_, bf16[4,16,8192]{2,1,0:T(8,128)(2,1)} %merge.5.refs_1_), custom_call_target="tpu_custom_call", output_to_operand_aliasing={{}: (3, {})} | custom-call | flops 1000000 | bytes 589824 | tf_op jit(solution)/shard_map/merge/pallas_call | solution.py:393
  45.6 0.7 %merge.7 = bf16[4,16,8192]{2,1,0:T(8,128)(2,1)} custom-call(f32[2,8,4096]{2,1,0:T(8,128)S(1)} %scale.1.scales, bf16[4,16,8192]{2,1,0:T(8,128)(2,1)S(1)} %masks.3.own, bf16[16,2048]{1,0:T(8,128)(2,1)S(1)} %collective-permute-done.6.refs_0_, bf16[4,16,8192]{2,1,0:T(8,128)(2,1)} %merge.6.refs_1_), custom_call_target="tpu_custom_call", output_to_operand_aliasing={{}: (3, {})} | custom-call | flops 1000000 | bytes 196608 | tf_op jit(solution)/shard_map/merge/pallas_call | solution.py:393
  (11 shorter events, 0.1 us)
Async XLA Ops:
  3.2 40.6 %collective-permute-start.8 = (bf16[16,16384]{1,0:T(8,128)(2,1)S(1)}, bf16[16,16384]{1,0:T(8,128)(2,1)S(1)}, u32[]{:S(2)}, u32[]{:S(2)}) collective-permute-start(bf16[16,16384]{1,0:T(8,128)(2,1)S(1)} %masks.5), channel_id=1, source_target_pairs={{0,1},{1,0},{2,3},{3,2},{4,5},{5,4},{6,7},{7,6},{8,9},{9,8},{10,11... | collective-permute-start | bytes 1572872 | tf_op jit(solution)/shard_map/ppermute | solution.py:34
  7.5 35.4 %collective-permute-start.9 = (bf16[16,8192]{1,0:T(8,128)(2,1)S(1)}, bf16[16,8192]{1,0:T(8,128)(2,1)S(1)}, u32[]{:S(2)}, u32[]{:S(2)}) collective-permute-start(bf16[16,8192]{1,0:T(8,128)(2,1)S(1)} %first.1), channel_id=1, source_target_pairs={{0,1},{1,0},{2,3},{3,2},{4,5},{5,4},{6,7},{7,6},{8,9},{9,8},{10,11... | collective-permute-start | bytes 786440 | tf_op jit(solution)/shard_map/ppermute | solution.py:34
  7.6 3.2 %collective-permute-start = (bf16[2,8,4352]{2,1,0:T(8,128)(2,1)S(1)}, bf16[2,8,4352]{2,1,0:T(8,128)(2,1)S(1)}, u32[]{:S(2)}, u32[]{:S(2)}) collective-permute-start(bf16[2,8,4352]{2,1,0:T(8,128)(2,1)S(1)} %get-tuple-element.14.mine), channel_id=1, source_target_pairs={{0,2},{2,0},{4,6},{6,4},{8,10},{10,8},{12,14},{14,12},{16,18},{18,... | collective-permute-start | bytes 417800 | tf_op jit(solution)/shard_map/ppermute | solution.py:25
  8.8 36.0 %collective-permute-start.7 = (bf16[16,6144]{1,0:T(8,128)(2,1)S(1)}, bf16[16,6144]{1,0:T(8,128)(2,1)S(1)}, u32[]{:S(2)}, u32[]{:S(2)}) collective-permute-start(bf16[16,6144]{1,0:T(8,128)(2,1)S(1)} %get-tuple-element.22), channel_id=1, source_target_pairs={{0,1},{1,0},{2,3},{3,2},{4,5},{5,4},{6,7},{7,6},{8,9},{9,8},{10,11... | collective-permute-start | bytes 589832 | tf_op jit(solution)/shard_map/ppermute | solution.py:34
  10.9 18.6 %collective-permute-start.1 = (bf16[8,2304]{1,0:T(8,128)(2,1)S(1)}, bf16[8,2304]{1,0:T(8,128)(2,1)S(1)}, u32[]{:S(2)}, u32[]{:S(2)}) collective-permute-start(bf16[8,2304]{1,0:T(8,128)(2,1)S(1)} %get-tuple-element.17), channel_id=1, source_target_pairs={{0,1},{1,0},{2,3},{3,2},{4,5},{5,4},{6,7},{7,6},{8,9},{9,8},{10,11... | collective-permute-start | bytes 110600 | tf_op jit(solution)/shard_map/ppermute | solution.py:34
  11.1 34.5 %collective-permute-start.6 = (bf16[16,2048]{1,0:T(8,128)(2,1)S(1)}, bf16[16,2048]{1,0:T(8,128)(2,1)S(1)}, u32[]{:S(2)}, u32[]{:S(2)}) collective-permute-start(bf16[16,2048]{1,0:T(8,128)(2,1)S(1)} %get-tuple-element.21), channel_id=1, source_target_pairs={{0,1},{1,0},{2,3},{3,2},{4,5},{5,4},{6,7},{7,6},{8,9},{9,8},{10,11... | collective-permute-start | bytes 196616 | tf_op jit(solution)/shard_map/ppermute | solution.py:34
  29.5 1.2 %collective-permute-start.2 = (bf16[8,2304]{1,0:T(8,128)(2,1)S(1)}, bf16[8,2304]{1,0:T(8,128)(2,1)S(1)}, u32[]{:S(2)}, u32[]{:S(2)}) collective-permute-start(bf16[8,2304]{1,0:T(8,128)(2,1)S(1)} %collective-permute-done.1.refs_0_), channel_id=1, source_target_pairs={{0,2},{2,0},{4,6},{6,4},{8,10},{10,8},{12,14},{14,12},{16,18},{18,... | collective-permute-start | bytes 110600 | tf_op jit(solution)/shard_map/ppermute | solution.py:25
  30.7 3.7 %collective-permute-start.3 = (f32[2,8,128]{2,1,0:T(8,128)S(1)}, f32[2,8,128]{2,1,0:T(8,128)S(1)}, u32[]{:S(2)}, u32[]{:S(2)}) collective-permute-start(f32[2,8,128]{2,1,0:T(8,128)S(1)} %get-tuple-element.19), channel_id=1, source_target_pairs={{0,4},{2,6},{4,0},{6,2},{8,12},{10,14},{12,8},{14,10},{16,20},{18,... | collective-permute-start | bytes 24584 | tf_op jit(solution)/shard_map/ppermute | solution.py:25
  34.5 3.7 %collective-permute-start.4 = (f32[2,8,128]{2,1,0:T(8,128)S(1)}, f32[2,8,128]{2,1,0:T(8,128)S(1)}, u32[]{:S(2)}, u32[]{:S(2)}) collective-permute-start(f32[2,8,128]{2,1,0:T(8,128)S(1)} %add.9), channel_id=1, source_target_pairs={{0,8},{2,10},{4,12},{6,14},{8,0},{10,2},{12,4},{14,6},{16,24},{18,... | collective-permute-start | bytes 24584 | tf_op jit(solution)/shard_map/ppermute | solution.py:25
  38.1 4.5 %collective-permute-start.5 = (f32[2,8,128]{2,1,0:T(8,128)S(1)}, f32[2,8,128]{2,1,0:T(8,128)S(1)}, u32[]{:S(2)}, u32[]{:S(2)}) collective-permute-start(f32[2,8,128]{2,1,0:T(8,128)S(1)} %add.10), channel_id=1, source_target_pairs={{0,16},{2,18},{4,20},{6,22},{8,24},{10,26},{12,28},{14,30},{16,0},... | collective-permute-start | bytes 24584 | tf_op jit(solution)/shard_map/ppermute | solution.py:25

commit v4 on v3

--- a/solution.py
+++ b/solution.py
@@ -13,7 +13,7 @@
 FF = 16384
 LANES = 128
 BLOCK = 1024
-PIECES = 4
+PIECES = 1
 GRANT = 16 * 2**20
 
 ANY = pl.BlockSpec(memory_space=pl.ANY)
@@ -231,37 +231,40 @@
         scales[step] = 1.0 / rounded.astype(jnp.float32)
 
 
-def merge_kernel(chunk, tasks, aliased, scales, own, *refs):
+def merge_kernel(chunks, tasks, aliased, scales, own, *refs):
     half = scales.shape[2]
     layers = own.shape[0]
     columns = 2 * half
-    arrived = refs[: tasks - 1]
-    out, buf, sems = refs[tasks - 1 + aliased :]
+    arrived = refs[: len(chunks) * (tasks - 1)]
+    out, buf, sems = refs[len(arrived) + aliased :]
     pieces = []
-    offset = 0
-    for layer, begin, end in chunk:
-        for part in range(2):
-            low, high = [min(max(at * columns // 4 - part * half, 0), half) for at in (begin, end)]
-            if high > low:
-                pieces.append((layer, part, low, high - low, offset))
-                offset += high - low
+    base = 0
+    for place, chunk in enumerate(chunks):
+        offset = 0
+        for layer, begin, end in chunk:
+            for part in range(2):
+                low, high = [min(max(at * columns // 4 - part * half, 0), half) for at in (begin, end)]
+                if high > low:
+                    pieces.append((place, base, layer, part, low, high - low, offset))
+                    offset += high - low
+        base += offset
     copies = []
-    for at, (layer, part, low, size, offset) in enumerate(pieces):
+    for at, (place, base, layer, part, low, size, offset) in enumerate(pieces):
         row = part * layers + layer
 
-        def body(place, block):
-            narrow = pl.ds(pl.multiple_of(low + place, LANES), block)
-            source = pl.ds(pl.multiple_of(part * half + low + place, LANES), block)
-            target = pl.ds(pl.multiple_of(offset + place, LANES), block)
-            merged = own[layer, :, source].astype(jnp.float32) * scales[0, row : row + 1, narrow]
+        def body(shift, block):
+            narrow = pl.ds(pl.multiple_of(low + shift, LANES), block)
+            mine = pl.ds(pl.multiple_of(part * half + low + shift, LANES), block)
+            source = pl.ds(pl.multiple_of(offset + shift, LANES), block)
+            merged = own[layer, :, mine].astype(jnp.float32) * scales[0, row : row + 1, narrow]
             for step in range(1, tasks):
-                other = arrived[step - 1][:, target].astype(jnp.float32)
+                other = arrived[place * (tasks - 1) + step - 1][:, source].astype(jnp.float32)
                 merged = merged + other * scales[step, row : row + 1, narrow]
-            buf[:, target] = merged.astype(jnp.bfloat16)
+            buf[:, pl.ds(pl.multiple_of(base + offset + shift, LANES), block)] = merged.astype(jnp.bfloat16)
 
         blocks(size, body)
         copies.append(pltpu.make_async_copy(
-            buf.at[:, pl.ds(offset, size)], out.at[layer, :, pl.ds(part * half + low, size)], sems.at[at]))
+            buf.at[:, pl.ds(base + offset, size)], out.at[layer, :, pl.ds(part * half + low, size)], sems.at[at]))
         copies[-1].start()
     for copy in copies:
         copy.wait()
@@ -388,20 +391,23 @@
     )(on_chip(means), on_chip(totals))
 
     out = None
-    for chunk, pieces in zip(plan, arrived):
+    for places in ([0, 1], *[[place] for place in range(2, len(plan))]):
+        chunks = [plan[place] for place in places]
+        pieces = [piece for place in places for piece in arrived[place]]
         extra = [] if out is None else [out]
+        merged_width = sum(chunk_width(chunk, columns) for chunk in chunks)
         out = pl.pallas_call(
-            functools.partial(merge_kernel, chunk, tasks, len(extra)),
+            functools.partial(merge_kernel, chunks, tasks, len(extra)),
             out_shape=jax.ShapeDtypeStruct((layers, rows, columns), bf16),
-            in_specs=[VMEM] * (1 + tasks) + [ANY] * len(extra),
+            in_specs=[VMEM] * (2 + len(pieces)) + [ANY] * len(extra),
             out_specs=ANY,
             scratch_shapes=[
-                pltpu.VMEM((rows, chunk_width(chunk, columns)), bf16),
-                pltpu.SemaphoreType.DMA((2 * len(chunk),)),
+                pltpu.VMEM((rows, merged_width), bf16),
+                pltpu.SemaphoreType.DMA((2 * sum(len(chunk) for chunk in chunks),)),
             ],
-            input_output_aliases={1 + tasks: 0} if extra else {},
+            input_output_aliases={2 + len(pieces): 0} if extra else {},
             compiler_params=pltpu.CompilerParams(vmem_limit_bytes=GRANT),
-            cost_estimate=cost(10**6, 6 * rows * chunk_width(chunk, columns)),
+            cost_estimate=cost(10**6, 6 * rows * merged_width),
             name="merge",
         )(on_chip(scales), on_chip(own), *[on_chip(piece) for piece in pieces], *extra)
     return out

time: 46.6 us -> 45.9 us (0.985)
  Pallas kernels: 10.9 us -> 10.1 us
    pallas_call x4 -> x3, Pallas kernels: 3.34 us -> 2.69 us  [merge_all(): pl.pallas_call(functools.partial(merge_kernel, chunks, tasks, len(extra))...]
  transfers between devices with their start and end apart: 10 -> 10, of which waited for: 5 -> 5; matrix products, arithmetic and copies ran while one was open for 0% -> 0% of each run, Pallas kernels for 15% -> 14%
where the time goes in v4:
time: 45.9 us; the launch traced here: 45.7 us
  waiting for transfers between devices  21.7 us (47%)
  starting transfers between devices  13.7 us (30%)
  Pallas kernels  10.1 us (22%)
    ppermute x5, waiting for transfers between devices, shifted(): lax.ppermute(value, 'task', [(source, (source + step) % size) for source...  16.6 us
    ppermute x5, starting transfers between devices, shifted(): lax.ppermute(value, 'task', [(source, (source + step) % size) for source...  7.23 us
    ppermute x5, starting transfers between devices, crossed(): lax.ppermute(value, axis, [(source, source ^ mask) for source in range(la...  6.44 us
    ppermute x5, waiting for transfers between devices, crossed(): lax.ppermute(value, axis, [(source, source ^ mask) for source in range(la...  5.09 us
    pallas_call x3, Pallas kernels, masks(): pl.pallas_call(functools.partial(mask_kernel, chunks, own_layers), out_sh...  4.11 us
    pallas_call x3, Pallas kernels, merge_all(): pl.pallas_call(functools.partial(merge_kernel, chunks, tasks, len(extra))...  2.69 us
    pallas_call x1, Pallas kernels, merge_all(): pl.pallas_call(sums_kernel, out_shape=[pltpu.VMEM((layers, rows, width),...  1.84 us
    pallas_call x1, Pallas kernels, merge_all(): pl.pallas_call(first_kernel, out_shape=[slabs[0]] * (tasks - 1), in_specs...  1.19 us
  transfers between devices with their start and end apart: 10, of which 5 were waited for; matrix products, arithmetic and copies ran while one was open for 0% of the time, Pallas kernels for 14%

profile of v4, /device:TPU:0, one launch (start us, length us, event | category | flops | bytes accessed | tf_op | source)
XLA Modules:
  0.0 45.7 jit_solution(7565107310107781500)
XLA Ops:
  0.0 1.8 %sums.1 = (bf16[4,16,16384]{2,1,0:T(8,128)(2,1)S(1)}, bf16[2,8,4352]{2,1,0:T(8,128)(2,1)S(1)}) custom-call(bf16[1,4,16,16384]{3,2,1,0:T(8,128)(2,1)} %deltas.3), custom_call_target="tpu_custom_call" | custom-call | flops 10000000 | bytes 2097152 | tf_op jit(solution)/shard_map/sums/pallas_call | solution.py:314
  1.8 1.3 %masks.5 = bf16[16,16384]{1,0:T(8,128)(2,1)S(1)} custom-call(s32[1,4,8]{2,1,0:T(4,128)} %limits.7, s32[1,4,16,16384]{3,2,1,0:T(8,128)} %scores.7, bf16[4,16,16384]{2,1,0:T(8,128)(2,1)S(1)} %get-tuple-element.20.copied), custom_call_target="tpu_custom_call" | custom-call | flops 10000000 | bytes 1572864 | tf_op jit(solution)/shard_map/masks/pallas_call | solution.py:330
  3.2 3.1 %collective-permute-start.9 = (bf16[16,16384]{1,0:T(8,128)(2,1)S(1)}, bf16[16,16384]{1,0:T(8,128)(2,1)S(1)}, u32[]{:S(2)}, u32[]{:S(2)}) collective-permute-start(bf16[16,16384]{1,0:T(8,128)(2,1)S(1)} %masks.5), channel_id=1, source_target_pairs={{0,1},{1,0},{2,3},{3,2},{4,5},{5,4},{6,7},{7,6},{8,9},{9,8},{10,11... | collective-permute-start | bytes 1572872 | tf_op jit(solution)/shard_map/ppermute | solution.py:34
  6.2 1.2 %first.1 = bf16[16,8192]{1,0:T(8,128)(2,1)S(1)} custom-call(s32[1,4,8]{2,1,0:T(4,128)} %limits.7, bf16[1,4,16,16384]{3,2,1,0:T(8,128)(2,1)} %deltas.3, s32[1,4,16,16384]{3,2,1,0:T(8,128)} %scores.7), custom_call_target="tpu_custom_call" | custom-call | flops 1000000 | bytes 786432 | tf_op jit(solution)/shard_map/first/pallas_call | solution.py:296
  7.4 0.1 collective-permute-start.8
  7.5 0.1 collective-permute-start
  7.6 1.1 %masks.4 = (bf16[16,6144]{1,0:T(8,128)(2,1)S(1)}, bf16[16,2048]{1,0:T(8,128)(2,1)S(1)}) custom-call(s32[1,4,8]{2,1,0:T(4,128)} %limits.7, s32[1,4,16,16384]{3,2,1,0:T(8,128)} %scores.7, bf16[4,16,16384]{2,1,0:T(8,128)(2,1)S(1)} %get-tuple-element.20.copied), custom_call_target="tpu_custom_call" | custom-call | flops 10000000 | bytes 1572864 | tf_op jit(solution)/shard_map/masks/pallas_call | solution.py:330
  8.7 2.0 %collective-permute-start.7 = (bf16[16,6144]{1,0:T(8,128)(2,1)S(1)}, bf16[16,6144]{1,0:T(8,128)(2,1)S(1)}, u32[]{:S(2)}, u32[]{:S(2)}) collective-permute-start(bf16[16,6144]{1,0:T(8,128)(2,1)S(1)} %get-tuple-element.22), channel_id=1, source_target_pairs={{0,1},{1,0},{2,3},{3,2},{4,5},{5,4},{6,7},{7,6},{8,9},{9,8},{10,11... | collective-permute-start | bytes 589832 | tf_op jit(solution)/shard_map/ppermute | solution.py:34
  10.7 0.0 collective-permute-done.theirs
  10.8 0.2 collective-permute-start.1
  11.0 1.9 %collective-permute-start.6 = (bf16[16,2048]{1,0:T(8,128)(2,1)S(1)}, bf16[16,2048]{1,0:T(8,128)(2,1)S(1)}, u32[]{:S(2)}, u32[]{:S(2)}) collective-permute-start(bf16[16,2048]{1,0:T(8,128)(2,1)S(1)} %get-tuple-element.21), channel_id=1, source_target_pairs={{0,1},{1,0},{2,3},{3,2},{4,5},{5,4},{6,7},{7,6},{8,9},{9,8},{10,11... | collective-permute-start | bytes 196616 | tf_op jit(solution)/shard_map/ppermute | solution.py:34
  12.9 16.6 %collective-permute-done.1.refs_0_ = bf16[8,2304]{1,0:T(8,128)(2,1)S(1)} collective-permute-done((bf16[8,2304]{1,0:T(8,128)(2,1)S(1)}, bf16[8,2304]{1,0:T(8,128)(2,1)S(1)}, u32[]{:S(2)}, u32[]{:S(2)}) %collective-permute-start.1) | collective-permute-done | bytes 36896 | tf_op jit(solution)/shard_map/ppermute | solution.py:34
  29.5 1.2 %collective-permute-done.2.refs_1_ = bf16[8,2304]{1,0:T(8,128)(2,1)S(1)} collective-permute-done((bf16[8,2304]{1,0:T(8,128)(2,1)S(1)}, bf16[8,2304]{1,0:T(8,128)(2,1)S(1)}, u32[]{:S(2)}, u32[]{:S(2)}) %collective-permute-start.2) | collective-permute-done | bytes 36896 | tf_op jit(solution)/shard_map/ppermute | solution.py:25
  30.7 1.8 %collective-permute-start.3 = (f32[2,8,128]{2,1,0:T(8,128)S(1)}, f32[2,8,128]{2,1,0:T(8,128)S(1)}, u32[]{:S(2)}, u32[]{:S(2)}) collective-permute-start(f32[2,8,128]{2,1,0:T(8,128)S(1)} %get-tuple-element.19), channel_id=1, source_target_pairs={{0,4},{2,6},{4,0},{6,2},{8,12},{10,14},{12,8},{14,10},{16,20},{18,... | collective-permute-start | bytes 24584 | tf_op jit(solution)/shard_map/ppermute | solution.py:25
  32.5 1.9 %collective-permute-done.3 = f32[2,8,128]{2,1,0:T(8,128)S(1)} collective-permute-done((f32[2,8,128]{2,1,0:T(8,128)S(1)}, f32[2,8,128]{2,1,0:T(8,128)S(1)}, u32[]{:S(2)}, u32[]{:S(2)}) %collective-permute-start.3) | collective-permute-done | bytes 8224 | tf_op jit(solution)/shard_map/ppermute | solution.py:25
  34.5 1.8 %collective-permute-start.4 = (f32[2,8,128]{2,1,0:T(8,128)S(1)}, f32[2,8,128]{2,1,0:T(8,128)S(1)}, u32[]{:S(2)}, u32[]{:S(2)}) collective-permute-start(f32[2,8,128]{2,1,0:T(8,128)S(1)} %add.9), channel_id=1, source_target_pairs={{0,8},{2,10},{4,12},{6,14},{8,0},{10,2},{12,4},{14,6},{16,24},{18,... | collective-permute-start | bytes 24584 | tf_op jit(solution)/shard_map/ppermute | solution.py:25
  36.3 1.9 %collective-permute-done.4 = f32[2,8,128]{2,1,0:T(8,128)S(1)} collective-permute-done((f32[2,8,128]{2,1,0:T(8,128)S(1)}, f32[2,8,128]{2,1,0:T(8,128)S(1)}, u32[]{:S(2)}, u32[]{:S(2)}) %collective-permute-start.4) | collective-permute-done | bytes 8224 | tf_op jit(solution)/shard_map/ppermute | solution.py:25
  38.1 2.8 %collective-permute-start.5 = (f32[2,8,128]{2,1,0:T(8,128)S(1)}, f32[2,8,128]{2,1,0:T(8,128)S(1)}, u32[]{:S(2)}, u32[]{:S(2)}) collective-permute-start(f32[2,8,128]{2,1,0:T(8,128)S(1)} %add.10), channel_id=1, source_target_pairs={{0,16},{2,18},{4,20},{6,22},{8,24},{10,26},{12,28},{14,30},{16,0},... | collective-permute-start | bytes 24584 | tf_op jit(solution)/shard_map/ppermute | solution.py:25
  40.9 1.6 %masks.3.own = bf16[4,16,8192]{2,1,0:T(8,128)(2,1)S(1)} custom-call(s32[1,4,8]{2,1,0:T(4,128)} %limits.7, s32[1,4,16,16384]{3,2,1,0:T(8,128)} %scores.7, bf16[4,16,16384]{2,1,0:T(8,128)(2,1)S(1)} %get-tuple-element.20.copied), custom_call_target="tpu_custom_call" | custom-call | flops 10000000 | bytes 3145728 | tf_op jit(solution)/shard_map/masks/pallas_call | solution.py:330
  42.6 0.1 collective-permute-done.5
  42.7 0.2 scale.1.scales
  42.9 1.2 %merge.3.refs_1_ = bf16[4,16,8192]{2,1,0:T(8,128)(2,1)} custom-call(f32[2,8,4096]{2,1,0:T(8,128)S(1)} %scale.1.scales, bf16[4,16,8192]{2,1,0:T(8,128)(2,1)S(1)} %masks.3.own, bf16[16,8192]{1,0:T(8,128)(2,1)S(1)} %collective-permute-done.8.refs_0_, bf16[16,16384]{1,0:T(8,128)(2,1)S(1)} %collective-permute-done.9.refs_1_), custom_call_target="tpu_custom_call" | custom-call | flops 1000000 | bytes 2359296 | tf_op jit(solution)/shard_map/merge/pallas_call | solution.py:399
  44.2 0.8 %merge.4.refs_1_ = bf16[4,16,8192]{2,1,0:T(8,128)(2,1)} custom-call(f32[2,8,4096]{2,1,0:T(8,128)S(1)} %scale.1.scales, bf16[4,16,8192]{2,1,0:T(8,128)(2,1)S(1)} %masks.3.own, bf16[16,6144]{1,0:T(8,128)(2,1)S(1)} %collective-permute-done.7.refs_0_, bf16[4,16,8192]{2,1,0:T(8,128)(2,1)} %merge.3.refs_1_), custom_call_target="tpu_custom_call", output_to_operand_aliasing={{}: (3, {})} | custom-call | flops 1000000 | bytes 589824 | tf_op jit(solution)/shard_map/merge/pallas_call | solution.py:399
  45.0 0.7 %merge.5 = bf16[4,16,8192]{2,1,0:T(8,128)(2,1)} custom-call(f32[2,8,4096]{2,1,0:T(8,128)S(1)} %scale.1.scales, bf16[4,16,8192]{2,1,0:T(8,128)(2,1)S(1)} %masks.3.own, bf16[16,2048]{1,0:T(8,128)(2,1)S(1)} %collective-permute-done.6.refs_0_, bf16[4,16,8192]{2,1,0:T(8,128)(2,1)} %merge.4.refs_1_), custom_call_target="tpu_custom_call", output_to_operand_aliasing={{}: (3, {})} | custom-call | flops 1000000 | bytes 196608 | tf_op jit(solution)/shard_map/merge/pallas_call | solution.py:399
  (10 shorter events, 0.1 us)
Async XLA Ops:
  3.2 39.7 %collective-permute-start.9 = (bf16[16,16384]{1,0:T(8,128)(2,1)S(1)}, bf16[16,16384]{1,0:T(8,128)(2,1)S(1)}, u32[]{:S(2)}, u32[]{:S(2)}) collective-permute-start(bf16[16,16384]{1,0:T(8,128)(2,1)S(1)} %masks.5), channel_id=1, source_target_pairs={{0,1},{1,0},{2,3},{3,2},{4,5},{5,4},{6,7},{7,6},{8,9},{9,8},{10,11... | collective-permute-start | bytes 1572872 | tf_op jit(solution)/shard_map/ppermute | solution.py:34
  7.4 35.5 %collective-permute-start.8 = (bf16[16,8192]{1,0:T(8,128)(2,1)S(1)}, bf16[16,8192]{1,0:T(8,128)(2,1)S(1)}, u32[]{:S(2)}, u32[]{:S(2)}) collective-permute-start(bf16[16,8192]{1,0:T(8,128)(2,1)S(1)} %first.1), channel_id=1, source_target_pairs={{0,1},{1,0},{2,3},{3,2},{4,5},{5,4},{6,7},{7,6},{8,9},{9,8},{10,11... | collective-permute-start | bytes 786440 | tf_op jit(solution)/shard_map/ppermute | solution.py:34
  7.5 3.2 %collective-permute-start = (bf16[2,8,4352]{2,1,0:T(8,128)(2,1)S(1)}, bf16[2,8,4352]{2,1,0:T(8,128)(2,1)S(1)}, u32[]{:S(2)}, u32[]{:S(2)}) collective-permute-start(bf16[2,8,4352]{2,1,0:T(8,128)(2,1)S(1)} %get-tuple-element.14.mine), channel_id=1, source_target_pairs={{0,2},{2,0},{4,6},{6,4},{8,10},{10,8},{12,14},{14,12},{16,18},{18,... | collective-permute-start | bytes 417800 | tf_op jit(solution)/shard_map/ppermute | solution.py:25
  8.7 35.4 %collective-permute-start.7 = (bf16[16,6144]{1,0:T(8,128)(2,1)S(1)}, bf16[16,6144]{1,0:T(8,128)(2,1)S(1)}, u32[]{:S(2)}, u32[]{:S(2)}) collective-permute-start(bf16[16,6144]{1,0:T(8,128)(2,1)S(1)} %get-tuple-element.22), channel_id=1, source_target_pairs={{0,1},{1,0},{2,3},{3,2},{4,5},{5,4},{6,7},{7,6},{8,9},{9,8},{10,11... | collective-permute-start | bytes 589832 | tf_op jit(solution)/shard_map/ppermute | solution.py:34
  10.8 18.7 %collective-permute-start.1 = (bf16[8,2304]{1,0:T(8,128)(2,1)S(1)}, bf16[8,2304]{1,0:T(8,128)(2,1)S(1)}, u32[]{:S(2)}, u32[]{:S(2)}) collective-permute-start(bf16[8,2304]{1,0:T(8,128)(2,1)S(1)} %get-tuple-element.17), channel_id=1, source_target_pairs={{0,1},{1,0},{2,3},{3,2},{4,5},{5,4},{6,7},{7,6},{8,9},{9,8},{10,11... | collective-permute-start | bytes 110600 | tf_op jit(solution)/shard_map/ppermute | solution.py:34
  11.0 33.9 %collective-permute-start.6 = (bf16[16,2048]{1,0:T(8,128)(2,1)S(1)}, bf16[16,2048]{1,0:T(8,128)(2,1)S(1)}, u32[]{:S(2)}, u32[]{:S(2)}) collective-permute-start(bf16[16,2048]{1,0:T(8,128)(2,1)S(1)} %get-tuple-element.21), channel_id=1, source_target_pairs={{0,1},{1,0},{2,3},{3,2},{4,5},{5,4},{6,7},{7,6},{8,9},{9,8},{10,11... | collective-permute-start | bytes 196616 | tf_op jit(solution)/shard_map/ppermute | solution.py:34
  29.5 1.2 %collective-permute-start.2 = (bf16[8,2304]{1,0:T(8,128)(2,1)S(1)}, bf16[8,2304]{1,0:T(8,128)(2,1)S(1)}, u32[]{:S(2)}, u32[]{:S(2)}) collective-permute-start(bf16[8,2304]{1,0:T(8,128)(2,1)S(1)} %collective-permute-done.1.refs_0_), channel_id=1, source_target_pairs={{0,2},{2,0},{4,6},{6,4},{8,10},{10,8},{12,14},{14,12},{16,18},{18,... | collective-permute-start | bytes 110600 | tf_op jit(solution)/shard_map/ppermute | solution.py:25
  30.7 3.7 %collective-permute-start.3 = (f32[2,8,128]{2,1,0:T(8,128)S(1)}, f32[2,8,128]{2,1,0:T(8,128)S(1)}, u32[]{:S(2)}, u32[]{:S(2)}) collective-permute-start(f32[2,8,128]{2,1,0:T(8,128)S(1)} %get-tuple-element.19), channel_id=1, source_target_pairs={{0,4},{2,6},{4,0},{6,2},{8,12},{10,14},{12,8},{14,10},{16,20},{18,... | collective-permute-start | bytes 24584 | tf_op jit(solution)/shard_map/ppermute | solution.py:25
  34.5 3.7 %collective-permute-start.4 = (f32[2,8,128]{2,1,0:T(8,128)S(1)}, f32[2,8,128]{2,1,0:T(8,128)S(1)}, u32[]{:S(2)}, u32[]{:S(2)}) collective-permute-start(f32[2,8,128]{2,1,0:T(8,128)S(1)} %add.9), channel_id=1, source_target_pairs={{0,8},{2,10},{4,12},{6,14},{8,0},{10,2},{12,4},{14,6},{16,24},{18,... | collective-permute-start | bytes 24584 | tf_op jit(solution)/shard_map/ppermute | solution.py:25
  38.1 4.5 %collective-permute-start.5 = (f32[2,8,128]{2,1,0:T(8,128)S(1)}, f32[2,8,128]{2,1,0:T(8,128)S(1)}, u32[]{:S(2)}, u32[]{:S(2)}) collective-permute-start(f32[2,8,128]{2,1,0:T(8,128)S(1)} %add.10), channel_id=1, source_target_pairs={{0,16},{2,18},{4,20},{6,22},{8,24},{10,26},{12,28},{14,30},{16,0},... | collective-permute-start | bytes 24584 | tf_op jit(solution)/shard_map/ppermute | solution.py:25

commit v5 on v4

--- a/solution.py
+++ b/solution.py
@@ -12,8 +12,9 @@
 EXPERTS = 8
 FF = 16384
 LANES = 128
-BLOCK = 1024
+BLOCK = 2048
 PIECES = 1
+CUT = 5
 GRANT = 16 * 2**20
 
 ANY = pl.BlockSpec(memory_space=pl.ANY)
@@ -53,11 +54,11 @@
 
 def chunk_plan(layers):
     last = layers - 1
-    return [[(0, 0, 4)], [(layer, 0, 4) for layer in range(1, last)], [(last, 0, 3)], [(last, 3, 4)]]
+    return [[(0, 0, 8)], [(layer, 0, 8) for layer in range(1, last)], [(last, 0, CUT)], [(last, CUT, 8)]]
 
 
 def chunk_width(chunk, columns):
-    return sum(end - begin for _, begin, end in chunk) * columns // 4
+    return sum(end - begin for _, begin, end in chunk) * columns // 8
 
 
 def mask_block(deltas, scores, limit):
@@ -109,7 +110,7 @@
 
 def sums_kernel(deltas, copied, packs, sems):
     tasks, folded, packed = packs.shape
-    half = packed - 2 * LANES
+    half = packed - LANES
     layers, rows, _ = copied.shape
     columns = 2 * half
     block = min(BLOCK, half)
@@ -133,11 +134,11 @@
             copy.wait()
         sums = row_sums([jnp.abs(copied[layer, :, source]) for source in sources[at] for layer in range(layers)])
         means = sums * (1.0 / (rows * groups))
-        packs[step, :, place * block : (place + 1) * block] = means.astype(jnp.bfloat16)
+        packs[step, :, place * block : (place + 1) * block] = means
         for tile in range(0, block, LANES):
             totals = totals + means[:, tile : tile + LANES]
     for step in range(tasks):
-        store_split(packs.at[step], totals)
+        packs[step, :, half:] = totals
 
 
 def store_split(pack, totals):
@@ -163,8 +164,8 @@
         for step in range(1, tasks):
             offset = 0
             for layer, begin, end in chunk:
-                size = (end - begin) * columns // 4
-                work.append((sent[at * (tasks - 1) + step - 1], offset, layer, step, begin * columns // 4, size))
+                size = (end - begin) * columns // 8
+                work.append((sent[at * (tasks - 1) + step - 1], offset, layer, step, begin * columns // 8, size))
                 offset += size
     work += [(own.at[layer], 0, layer, 0, 0, columns) for layer in own_layers]
     copies = []
@@ -190,17 +191,15 @@
     return pl.ds(pl.multiple_of(lax.rem(lax.axis_index("shard"), 2) * width, LANES), width)
 
 
-def pair_kernel(mine, theirs, means, totals, *refs):
-    packs, both_buf = refs[:-1], refs[-1]
+def pair_kernel(mine, theirs, means, totals, *packs):
     tasks, _, packed = mine.shape
-    half = packed - 2 * LANES
-    both = mine[...].astype(jnp.float32) + theirs[...].astype(jnp.float32)
-    both_buf[...] = both
-    means[...] = both[0, :, :half]
-    total = both[0, :, half : half + LANES] + both[0, :, half + LANES :]
+    half = packed - LANES
+    means[...] = mine[0, :, :half] + theirs[0, :, :half]
+    total = mine[0, :, half:] + theirs[0, :, half:]
     totals[...] = total
     for step in range(1, tasks):
-        packs[step - 1][:, : half // 2] = both_buf[step, :, slot_lanes(half // 2)].astype(jnp.bfloat16)
+        picked = mine[step, :, slot_lanes(half // 2)] + theirs[step, :, slot_lanes(half // 2)]
+        packs[step - 1][:, : half // 2] = picked.astype(jnp.bfloat16)
         store_split(packs[step - 1], total)
 
 
@@ -243,7 +242,7 @@
         offset = 0
         for layer, begin, end in chunk:
             for part in range(2):
-                low, high = [min(max(at * columns // 4 - part * half, 0), half) for at in (begin, end)]
+                low, high = [min(max(at * columns // 8 - part * half, 0), half) for at in (begin, end)]
                 if high > low:
                     pieces.append((place, base, layer, part, low, high - low, offset))
                     offset += high - low
@@ -310,10 +309,10 @@
     )(keep_limits, task_deltas, rank_scores)
     arrived = [[shifted(first[step - 1], step) for step in range(1, tasks)]]
 
-    pack = (2 * layers, half + 2 * LANES)
+    pack = (tasks, 2 * layers, half + LANES)
     copied, packs = pl.pallas_call(
         sums_kernel,
-        out_shape=[pltpu.VMEM((layers, rows, width), bf16), pltpu.VMEM((tasks, *pack), bf16)],
+        out_shape=[pltpu.VMEM((layers, rows, width), bf16), pltpu.VMEM(pack, f32)],
         in_specs=[HBM],
         out_specs=[VMEM] * 2,
         scratch_shapes=[pltpu.SemaphoreType.DMA((2 * tasks * half // block,))],
@@ -343,7 +342,7 @@
         )(keep_limits, rank_scores, on_chip(copied))
 
     for bit in range(1, group_bits):
-        packs = packs.astype(f32) + swapped(packs, "shard", bit).astype(f32)
+        packs = packs + swapped(packs, "shard", bit)
     theirs = swapped(packs, "shard", 0)
     sent = [*masks([1], [])]
     means, totals, *packs = pl.pallas_call(
@@ -352,7 +351,6 @@
         + [pltpu.VMEM((2 * layers, half // 2 + 2 * LANES), bf16)] * (tasks - 1),
         in_specs=[VMEM] * 2,
         out_specs=[VMEM] * (tasks + 1),
-        scratch_shapes=[pltpu.VMEM((tasks, *pack), f32)],
         compiler_params=pltpu.CompilerParams(vmem_limit_bytes=GRANT),
         cost_estimate=cost(10**6, 8 * tasks * layers * half),
         name="pair",

time: 45.9 us -> 45.3 us (0.987)
  waiting for transfers between devices: 21.7 us -> 20.7 us
  starting transfers between devices: 13.7 us -> 14.3 us
    ppermute x5, starting transfers between devices: 6.44 us -> 7 us  [crossed(): lax.ppermute(value, axis, [(source, source ^ mask) for source in range(la...]
    ppermute x5, waiting for transfers between devices: 16.6 us -> 16.1 us  [shifted(): lax.ppermute(value, 'task', [(source, (source + step) % size) for source...]
    ppermute x5, waiting for transfers between devices: 5.09 us -> 4.6 us  [crossed(): lax.ppermute(value, axis, [(source, source ^ mask) for source in range(la...]
  transfers between devices with their start and end apart: 10 -> 10, of which waited for: 5 -> 4; matrix products, arithmetic and copies ran while one was open for 0% -> 0% of each run, Pallas kernels for 14% -> 14%
where the time goes in v5:
time: 45.3 us; the launch traced here: 45 us
  waiting for transfers between devices  20.7 us (46%)
  starting transfers between devices  14.3 us (32%)
  Pallas kernels  9.87 us (22%)
    ppermute x5, waiting for transfers between devices, shifted(): lax.ppermute(value, 'task', [(source, (source + step) % size) for source...  16.1 us
    ppermute x5, starting transfers between devices, shifted(): lax.ppermute(value, 'task', [(source, (source + step) % size) for source...  7.31 us
    ppermute x5, starting transfers between devices, crossed(): lax.ppermute(value, axis, [(source, source ^ mask) for source in range(la...  7 us
    ppermute x5, waiting for transfers between devices, crossed(): lax.ppermute(value, axis, [(source, source ^ mask) for source in range(la...  4.6 us
    pallas_call x3, Pallas kernels, masks(): pl.pallas_call(functools.partial(mask_kernel, chunks, own_layers), out_sh...  4.03 us
    pallas_call x3, Pallas kernels, merge_all(): pl.pallas_call(functools.partial(merge_kernel, chunks, tasks, len(extra))...  2.61 us
    pallas_call x1, Pallas kernels, merge_all(): pl.pallas_call(sums_kernel, out_shape=[pltpu.VMEM((layers, rows, width),...  1.74 us
    pallas_call x1, Pallas kernels, merge_all(): pl.pallas_call(first_kernel, out_shape=[slabs[0]] * (tasks - 1), in_specs...  1.2 us
  transfers between devices with their start and end apart: 10, of which 4 were waited for; matrix products, arithmetic and copies ran while one was open for 0% of the time, Pallas kernels for 14%

profile of v5, /device:TPU:0, one launch (start us, length us, event | category | flops | bytes accessed | tf_op | source)
XLA Modules:
  0.0 45.0 jit_solution(2865442713181350836)
XLA Ops:
  0.0 1.7 %sums.1 = (bf16[4,16,16384]{2,1,0:T(8,128)(2,1)S(1)}, f32[2,8,4224]{2,1,0:T(8,128)S(1)}) custom-call(bf16[1,4,16,16384]{3,2,1,0:T(8,128)(2,1)} %deltas.3), custom_call_target="tpu_custom_call" | custom-call | flops 10000000 | bytes 2097152 | tf_op jit(solution)/shard_map/sums/pallas_call | solution.py:313
  1.7 1.3 %masks.5 = bf16[16,16384]{1,0:T(8,128)(2,1)S(1)} custom-call(s32[1,4,8]{2,1,0:T(4,128)} %limits.7, s32[1,4,16,16384]{3,2,1,0:T(8,128)} %scores.7, bf16[4,16,16384]{2,1,0:T(8,128)(2,1)S(1)} %get-tuple-element.20.copied), custom_call_target="tpu_custom_call" | custom-call | flops 10000000 | bytes 1572864 | tf_op jit(solution)/shard_map/masks/pallas_call | solution.py:329
  3.1 3.1 %collective-permute-start.9 = (bf16[16,16384]{1,0:T(8,128)(2,1)S(1)}, bf16[16,16384]{1,0:T(8,128)(2,1)S(1)}, u32[]{:S(2)}, u32[]{:S(2)}) collective-permute-start(bf16[16,16384]{1,0:T(8,128)(2,1)S(1)} %masks.5), channel_id=1, source_target_pairs={{0,1},{1,0},{2,3},{3,2},{4,5},{5,4},{6,7},{7,6},{8,9},{9,8},{10,11... | collective-permute-start | bytes 1572872 | tf_op jit(solution)/shard_map/ppermute | solution.py:35
  6.1 1.2 %first.1 = bf16[16,8192]{1,0:T(8,128)(2,1)S(1)} custom-call(s32[1,4,8]{2,1,0:T(4,128)} %limits.7, bf16[1,4,16,16384]{3,2,1,0:T(8,128)(2,1)} %deltas.3, s32[1,4,16,16384]{3,2,1,0:T(8,128)} %scores.7), custom_call_target="tpu_custom_call" | custom-call | flops 1000000 | bytes 786432 | tf_op jit(solution)/shard_map/first/pallas_call | solution.py:295
  7.3 0.2 collective-permute-start.8
  7.5 1.1 %masks.4 = (bf16[16,5120]{1,0:T(8,128)(2,1)S(1)}, bf16[16,3072]{1,0:T(8,128)(2,1)S(1)}) custom-call(s32[1,4,8]{2,1,0:T(4,128)} %limits.7, s32[1,4,16,16384]{3,2,1,0:T(8,128)} %scores.7, bf16[4,16,16384]{2,1,0:T(8,128)(2,1)S(1)} %get-tuple-element.20.copied), custom_call_target="tpu_custom_call" | custom-call | flops 10000000 | bytes 1572864 | tf_op jit(solution)/shard_map/masks/pallas_call | solution.py:329
  8.6 2.0 %collective-permute-start.7 = (bf16[16,5120]{1,0:T(8,128)(2,1)S(1)}, bf16[16,5120]{1,0:T(8,128)(2,1)S(1)}, u32[]{:S(2)}, u32[]{:S(2)}) collective-permute-start(bf16[16,5120]{1,0:T(8,128)(2,1)S(1)} %get-tuple-element.22), channel_id=1, source_target_pairs={{0,1},{1,0},{2,3},{3,2},{4,5},{5,4},{6,7},{7,6},{8,9},{9,8},{10,11... | collective-permute-start | bytes 491528 | tf_op jit(solution)/shard_map/ppermute | solution.py:35
  10.6 0.0 collective-permute-done.theirs
  10.6 0.2 collective-permute-start.1
  10.8 1.9 %collective-permute-start.6 = (bf16[16,3072]{1,0:T(8,128)(2,1)S(1)}, bf16[16,3072]{1,0:T(8,128)(2,1)S(1)}, u32[]{:S(2)}, u32[]{:S(2)}) collective-permute-start(bf16[16,3072]{1,0:T(8,128)(2,1)S(1)} %get-tuple-element.21), channel_id=1, source_target_pairs={{0,1},{1,0},{2,3},{3,2},{4,5},{5,4},{6,7},{7,6},{8,9},{9,8},{10,11... | collective-permute-start | bytes 294920 | tf_op jit(solution)/shard_map/ppermute | solution.py:35
  12.7 16.1 %collective-permute-done.1.refs_0_ = bf16[8,2304]{1,0:T(8,128)(2,1)S(1)} collective-permute-done((bf16[8,2304]{1,0:T(8,128)(2,1)S(1)}, bf16[8,2304]{1,0:T(8,128)(2,1)S(1)}, u32[]{:S(2)}, u32[]{:S(2)}) %collective-permute-start.1) | collective-permute-done | bytes 36896 | tf_op jit(solution)/shard_map/ppermute | solution.py:35
  28.8 0.0 collective-permute-start.2
  28.8 1.2 %collective-permute-done.2.refs_1_ = bf16[8,2304]{1,0:T(8,128)(2,1)S(1)} collective-permute-done((bf16[8,2304]{1,0:T(8,128)(2,1)S(1)}, bf16[8,2304]{1,0:T(8,128)(2,1)S(1)}, u32[]{:S(2)}, u32[]{:S(2)}) %collective-permute-start.2) | collective-permute-done | bytes 36896 | tf_op jit(solution)/shard_map/ppermute | solution.py:26
  30.1 2.0 %collective-permute-start.3 = (f32[2,8,128]{2,1,0:T(8,128)S(1)}, f32[2,8,128]{2,1,0:T(8,128)S(1)}, u32[]{:S(2)}, u32[]{:S(2)}) collective-permute-start(f32[2,8,128]{2,1,0:T(8,128)S(1)} %get-tuple-element.19), channel_id=1, source_target_pairs={{0,4},{2,6},{4,0},{6,2},{8,12},{10,14},{12,8},{14,10},{16,20},{18,... | collective-permute-start | bytes 24584 | tf_op jit(solution)/shard_map/ppermute | solution.py:26
  32.0 1.7 %collective-permute-done.3 = f32[2,8,128]{2,1,0:T(8,128)S(1)} collective-permute-done((f32[2,8,128]{2,1,0:T(8,128)S(1)}, f32[2,8,128]{2,1,0:T(8,128)S(1)}, u32[]{:S(2)}, u32[]{:S(2)}) %collective-permute-start.3) | collective-permute-done | bytes 8224 | tf_op jit(solution)/shard_map/ppermute | solution.py:26
  33.8 2.0 %collective-permute-start.4 = (f32[2,8,128]{2,1,0:T(8,128)S(1)}, f32[2,8,128]{2,1,0:T(8,128)S(1)}, u32[]{:S(2)}, u32[]{:S(2)}) collective-permute-start(f32[2,8,128]{2,1,0:T(8,128)S(1)} %add.9), channel_id=1, source_target_pairs={{0,8},{2,10},{4,12},{6,14},{8,0},{10,2},{12,4},{14,6},{16,24},{18,... | collective-permute-start | bytes 24584 | tf_op jit(solution)/shard_map/ppermute | solution.py:26
  35.8 1.7 %collective-permute-done.4 = f32[2,8,128]{2,1,0:T(8,128)S(1)} collective-permute-done((f32[2,8,128]{2,1,0:T(8,128)S(1)}, f32[2,8,128]{2,1,0:T(8,128)S(1)}, u32[]{:S(2)}, u32[]{:S(2)}) %collective-permute-start.4) | collective-permute-done | bytes 8224 | tf_op jit(solution)/shard_map/ppermute | solution.py:26
  37.4 3.0 %collective-permute-start.5 = (f32[2,8,128]{2,1,0:T(8,128)S(1)}, f32[2,8,128]{2,1,0:T(8,128)S(1)}, u32[]{:S(2)}, u32[]{:S(2)}) collective-permute-start(f32[2,8,128]{2,1,0:T(8,128)S(1)} %add.10), channel_id=1, source_target_pairs={{0,16},{2,18},{4,20},{6,22},{8,24},{10,26},{12,28},{14,30},{16,0},... | collective-permute-start | bytes 24584 | tf_op jit(solution)/shard_map/ppermute | solution.py:26
  40.5 1.6 %masks.3.own = bf16[4,16,8192]{2,1,0:T(8,128)(2,1)S(1)} custom-call(s32[1,4,8]{2,1,0:T(4,128)} %limits.7, s32[1,4,16,16384]{3,2,1,0:T(8,128)} %scores.7, bf16[4,16,16384]{2,1,0:T(8,128)(2,1)S(1)} %get-tuple-element.20.copied), custom_call_target="tpu_custom_call" | custom-call | flops 10000000 | bytes 3145728 | tf_op jit(solution)/shard_map/masks/pallas_call | solution.py:329
  42.1 0.2 scale.1.scales
  42.4 0.0 collective-permute-done.9.refs_1_
  42.4 1.1 %merge.3.refs_1_ = bf16[4,16,8192]{2,1,0:T(8,128)(2,1)} custom-call(f32[2,8,4096]{2,1,0:T(8,128)S(1)} %scale.1.scales, bf16[4,16,8192]{2,1,0:T(8,128)(2,1)S(1)} %masks.3.own, bf16[16,8192]{1,0:T(8,128)(2,1)S(1)} %collective-permute-done.8.refs_0_, bf16[16,16384]{1,0:T(8,128)(2,1)S(1)} %collective-permute-done.9.refs_1_), custom_call_target="tpu_custom_call" | custom-call | flops 1000000 | bytes 2359296 | tf_op jit(solution)/shard_map/merge/pallas_call | solution.py:397
  43.5 0.7 %merge.4.refs_1_ = bf16[4,16,8192]{2,1,0:T(8,128)(2,1)} custom-call(f32[2,8,4096]{2,1,0:T(8,128)S(1)} %scale.1.scales, bf16[4,16,8192]{2,1,0:T(8,128)(2,1)S(1)} %masks.3.own, bf16[16,5120]{1,0:T(8,128)(2,1)S(1)} %collective-permute-done.7.refs_0_, bf16[4,16,8192]{2,1,0:T(8,128)(2,1)} %merge.3.refs_1_), custom_call_target="tpu_custom_call", output_to_operand_aliasing={{}: (3, {})} | custom-call | flops 1000000 | bytes 491520 | tf_op jit(solution)/shard_map/merge/pallas_call | solution.py:397
  44.3 0.7 %merge.5 = bf16[4,16,8192]{2,1,0:T(8,128)(2,1)} custom-call(f32[2,8,4096]{2,1,0:T(8,128)S(1)} %scale.1.scales, bf16[4,16,8192]{2,1,0:T(8,128)(2,1)S(1)} %masks.3.own, bf16[16,3072]{1,0:T(8,128)(2,1)S(1)} %collective-permute-done.6.refs_0_, bf16[4,16,8192]{2,1,0:T(8,128)(2,1)} %merge.4.refs_1_), custom_call_target="tpu_custom_call", output_to_operand_aliasing={{}: (3, {})} | custom-call | flops 1000000 | bytes 294912 | tf_op jit(solution)/shard_map/merge/pallas_call | solution.py:397
  (10 shorter events, 0.1 us)
Async XLA Ops:
  3.1 39.3 %collective-permute-start.9 = (bf16[16,16384]{1,0:T(8,128)(2,1)S(1)}, bf16[16,16384]{1,0:T(8,128)(2,1)S(1)}, u32[]{:S(2)}, u32[]{:S(2)}) collective-permute-start(bf16[16,16384]{1,0:T(8,128)(2,1)S(1)} %masks.5), channel_id=1, source_target_pairs={{0,1},{1,0},{2,3},{3,2},{4,5},{5,4},{6,7},{7,6},{8,9},{9,8},{10,11... | collective-permute-start | bytes 1572872 | tf_op jit(solution)/shard_map/ppermute | solution.py:35
  6.1 4.5 %collective-permute-start = (f32[2,8,4224]{2,1,0:T(8,128)S(1)}, f32[2,8,4224]{2,1,0:T(8,128)S(1)}, u32[]{:S(2)}, u32[]{:S(2)}) collective-permute-start(f32[2,8,4224]{2,1,0:T(8,128)S(1)} %get-tuple-element.14.mine), channel_id=1, source_target_pairs={{0,2},{2,0},{4,6},{6,4},{8,10},{10,8},{12,14},{14,12},{16,18},{18,... | collective-permute-start | bytes 811016 | tf_op jit(solution)/shard_map/ppermute | solution.py:26
  7.3 35.0 %collective-permute-start.8 = (bf16[16,8192]{1,0:T(8,128)(2,1)S(1)}, bf16[16,8192]{1,0:T(8,128)(2,1)S(1)}, u32[]{:S(2)}, u32[]{:S(2)}) collective-permute-start(bf16[16,8192]{1,0:T(8,128)(2,1)S(1)} %first.1), channel_id=1, source_target_pairs={{0,1},{1,0},{2,3},{3,2},{4,5},{5,4},{6,7},{7,6},{8,9},{9,8},{10,11... | collective-permute-start | bytes 786440 | tf_op jit(solution)/shard_map/ppermute | solution.py:35
  8.6 34.9 %collective-permute-start.7 = (bf16[16,5120]{1,0:T(8,128)(2,1)S(1)}, bf16[16,5120]{1,0:T(8,128)(2,1)S(1)}, u32[]{:S(2)}, u32[]{:S(2)}) collective-permute-start(bf16[16,5120]{1,0:T(8,128)(2,1)S(1)} %get-tuple-element.22), channel_id=1, source_target_pairs={{0,1},{1,0},{2,3},{3,2},{4,5},{5,4},{6,7},{7,6},{8,9},{9,8},{10,11... | collective-permute-start | bytes 491528 | tf_op jit(solution)/shard_map/ppermute | solution.py:35
  10.6 18.2 %collective-permute-start.1 = (bf16[8,2304]{1,0:T(8,128)(2,1)S(1)}, bf16[8,2304]{1,0:T(8,128)(2,1)S(1)}, u32[]{:S(2)}, u32[]{:S(2)}) collective-permute-start(bf16[8,2304]{1,0:T(8,128)(2,1)S(1)} %get-tuple-element.17), channel_id=1, source_target_pairs={{0,1},{1,0},{2,3},{3,2},{4,5},{5,4},{6,7},{7,6},{8,9},{9,8},{10,11... | collective-permute-start | bytes 110600 | tf_op jit(solution)/shard_map/ppermute | solution.py:35
  10.8 33.5 %collective-permute-start.6 = (bf16[16,3072]{1,0:T(8,128)(2,1)S(1)}, bf16[16,3072]{1,0:T(8,128)(2,1)S(1)}, u32[]{:S(2)}, u32[]{:S(2)}) collective-permute-start(bf16[16,3072]{1,0:T(8,128)(2,1)S(1)} %get-tuple-element.21), channel_id=1, source_target_pairs={{0,1},{1,0},{2,3},{3,2},{4,5},{5,4},{6,7},{7,6},{8,9},{9,8},{10,11... | collective-permute-start | bytes 294920 | tf_op jit(solution)/shard_map/ppermute | solution.py:35
  28.8 1.2 %collective-permute-start.2 = (bf16[8,2304]{1,0:T(8,128)(2,1)S(1)}, bf16[8,2304]{1,0:T(8,128)(2,1)S(1)}, u32[]{:S(2)}, u32[]{:S(2)}) collective-permute-start(bf16[8,2304]{1,0:T(8,128)(2,1)S(1)} %collective-permute-done.1.refs_0_), channel_id=1, source_target_pairs={{0,2},{2,0},{4,6},{6,4},{8,10},{10,8},{12,14},{14,12},{16,18},{18,... | collective-permute-start | bytes 110600 | tf_op jit(solution)/shard_map/ppermute | solution.py:26
  30.1 3.7 %collective-permute-start.3 = (f32[2,8,128]{2,1,0:T(8,128)S(1)}, f32[2,8,128]{2,1,0:T(8,128)S(1)}, u32[]{:S(2)}, u32[]{:S(2)}) collective-permute-start(f32[2,8,128]{2,1,0:T(8,128)S(1)} %get-tuple-element.19), channel_id=1, source_target_pairs={{0,4},{2,6},{4,0},{6,2},{8,12},{10,14},{12,8},{14,10},{16,20},{18,... | collective-permute-start | bytes 24584 | tf_op jit(solution)/shard_map/ppermute | solution.py:26
  33.8 3.7 %collective-permute-start.4 = (f32[2,8,128]{2,1,0:T(8,128)S(1)}, f32[2,8,128]{2,1,0:T(8,128)S(1)}, u32[]{:S(2)}, u32[]{:S(2)}) collective-permute-start(f32[2,8,128]{2,1,0:T(8,128)S(1)} %add.9), channel_id=1, source_target_pairs={{0,8},{2,10},{4,12},{6,14},{8,0},{10,2},{12,4},{14,6},{16,24},{18,... | collective-permute-start | bytes 24584 | tf_op jit(solution)/shard_map/ppermute | solution.py:26
  37.4 4.7 %collective-permute-start.5 = (f32[2,8,128]{2,1,0:T(8,128)S(1)}, f32[2,8,128]{2,1,0:T(8,128)S(1)}, u32[]{:S(2)}, u32[]{:S(2)}) collective-permute-start(f32[2,8,128]{2,1,0:T(8,128)S(1)} %add.10), channel_id=1, source_target_pairs={{0,16},{2,18},{4,20},{6,22},{8,24},{10,26},{12,28},{14,30},{16,0},... | collective-permute-start | bytes 24584 | tf_op jit(solution)/shard_map/ppermute | solution.py:26

commit v6 on v5

--- a/solution.py
+++ b/solution.py
@@ -33,6 +33,16 @@
 def shifted(value, step):
     size = lax.axis_size("task")
     return lax.ppermute(value, "task", [(source, (source + step) % size) for source in range(size)])
+
+
+def shifted_across(value, step):
+    tasks = lax.axis_size("task")
+    pairs = [
+        (shard * tasks + source, (shard ^ 1) * tasks + (source + step) % tasks)
+        for shard in range(lax.axis_size("shard"))
+        for source in range(tasks)
+    ]
+    return lax.ppermute(value, ("shard", "task"), pairs)
 
 
 def column_start(step, columns):
@@ -362,9 +372,12 @@
     pairs = []
     for arrival in arrivals:
         pairs += [arrival, swapped(arrival, "shard", 0)]
-    for place in range(2, len(plan)):
+    last = len(plan) - 1
+    for place in range(2, last):
         at = (place - 1) * (tasks - 1)
         arrived.append([shifted(sent[at + step - 1], step) for step in range(1, tasks)])
+    exchanged = [swapped(sent[(last - 1) * (tasks - 1) + step - 1], "shard", 0) for step in range(1, tasks)]
+    arrived.append([shifted_across(exchanged[step - 1], step) for step in range(1, tasks)])
 
     means, totals = pl.pallas_call(
         join_kernel,

time: 45.3 us -> 45.3 us (level)
  waiting for transfers between devices: 20.7 us -> 21.2 us
    ppermute x5 -> x4, starting transfers between devices: 7.31 us -> 5.32 us  [shifted(): lax.ppermute(value, 'task', [(source, (source + step) % size) for source...]
    ppermute x0 -> x1, starting transfers between devices: none -> 1.05 us  [shifted_across(): return lax.ppermute(value, ('shard', 'task'), pairs)]
    ppermute x5 -> x6, starting transfers between devices: 7 us -> 7.5 us  [crossed(): lax.ppermute(value, axis, [(source, source ^ mask) for source in range(la...]
    ppermute x5 -> x4, waiting for transfers between devices: 16.1 us -> 16.6 us  [shifted(): lax.ppermute(value, 'task', [(source, (source + step) % size) for source...]
    ppermute x5 -> x6, waiting for transfers between devices: 4.6 us -> 4.6 us  [crossed(): lax.ppermute(value, axis, [(source, source ^ mask) for source in range(la...]
  transfers between devices with their start and end apart: 10 -> 11, of which waited for: 4 -> 4; matrix products, arithmetic and copies ran while one was open for 0% -> 0% of each run, Pallas kernels for 14% -> 14%
where the time goes in v6:
time: 45.3 us; the launch traced here: 45 us
  waiting for transfers between devices  21.2 us (47%)
  starting transfers between devices  13.9 us (31%)
  Pallas kernels  9.87 us (22%)
    ppermute x4, waiting for transfers between devices, shifted(): lax.ppermute(value, 'task', [(source, (source + step) % size) for source...  16.6 us
    ppermute x6, starting transfers between devices, crossed(): lax.ppermute(value, axis, [(source, source ^ mask) for source in range(la...  7.5 us
    ppermute x4, starting transfers between devices, shifted(): lax.ppermute(value, 'task', [(source, (source + step) % size) for source...  5.32 us
    ppermute x6, waiting for transfers between devices, crossed(): lax.ppermute(value, axis, [(source, source ^ mask) for source in range(la...  4.6 us
    pallas_call x3, Pallas kernels, masks(): pl.pallas_call(functools.partial(mask_kernel, chunks, own_layers), out_sh...  4.03 us
    pallas_call x3, Pallas kernels, merge_all(): pl.pallas_call(functools.partial(merge_kernel, chunks, tasks, len(extra))...  2.61 us
    pallas_call x1, Pallas kernels, merge_all(): pl.pallas_call(sums_kernel, out_shape=[pltpu.VMEM((layers, rows, width),...  1.74 us
    pallas_call x1, Pallas kernels, merge_all(): pl.pallas_call(first_kernel, out_shape=[slabs[0]] * (tasks - 1), in_specs...  1.2 us
  transfers between devices with their start and end apart: 11, of which 4 were waited for; matrix products, arithmetic and copies ran while one was open for 0% of the time, Pallas kernels for 14%

profile of v6, /device:TPU:0, one launch (start us, length us, event | category | flops | bytes accessed | tf_op | source)
XLA Modules:
  0.0 45.0 jit_solution(7187868008584248957)
XLA Ops:
  0.0 1.7 %sums.1 = (bf16[4,16,16384]{2,1,0:T(8,128)(2,1)S(1)}, f32[2,8,4224]{2,1,0:T(8,128)S(1)}) custom-call(bf16[1,4,16,16384]{3,2,1,0:T(8,128)(2,1)} %deltas.3), custom_call_target="tpu_custom_call" | custom-call | flops 10000000 | bytes 2097152 | tf_op jit(solution)/shard_map/sums/pallas_call | solution.py:323
  1.7 1.3 %masks.5 = bf16[16,16384]{1,0:T(8,128)(2,1)S(1)} custom-call(s32[1,4,8]{2,1,0:T(4,128)} %limits.7, s32[1,4,16,16384]{3,2,1,0:T(8,128)} %scores.7, bf16[4,16,16384]{2,1,0:T(8,128)(2,1)S(1)} %get-tuple-element.20.copied), custom_call_target="tpu_custom_call" | custom-call | flops 10000000 | bytes 1572864 | tf_op jit(solution)/shard_map/masks/pallas_call | solution.py:339
  3.1 3.1 %collective-permute-start.10 = (bf16[16,16384]{1,0:T(8,128)(2,1)S(1)}, bf16[16,16384]{1,0:T(8,128)(2,1)S(1)}, u32[]{:S(2)}, u32[]{:S(2)}) collective-permute-start(bf16[16,16384]{1,0:T(8,128)(2,1)S(1)} %masks.5), channel_id=1, source_target_pairs={{0,1},{1,0},{2,3},{3,2},{4,5},{5,4},{6,7},{7,6},{8,9},{9,8},{10,11... | collective-permute-start | bytes 1572872 | tf_op jit(solution)/shard_map/ppermute | solution.py:35
  6.1 1.2 %first.1 = bf16[16,8192]{1,0:T(8,128)(2,1)S(1)} custom-call(s32[1,4,8]{2,1,0:T(4,128)} %limits.7, bf16[1,4,16,16384]{3,2,1,0:T(8,128)(2,1)} %deltas.3, s32[1,4,16,16384]{3,2,1,0:T(8,128)} %scores.7), custom_call_target="tpu_custom_call" | custom-call | flops 1000000 | bytes 786432 | tf_op jit(solution)/shard_map/first/pallas_call | solution.py:305
  7.3 0.2 collective-permute-start.9
  7.5 1.1 %masks.4 = (bf16[16,5120]{1,0:T(8,128)(2,1)S(1)}, bf16[16,3072]{1,0:T(8,128)(2,1)S(1)}) custom-call(s32[1,4,8]{2,1,0:T(4,128)} %limits.7, s32[1,4,16,16384]{3,2,1,0:T(8,128)} %scores.7, bf16[4,16,16384]{2,1,0:T(8,128)(2,1)S(1)} %get-tuple-element.20.copied), custom_call_target="tpu_custom_call" | custom-call | flops 10000000 | bytes 1572864 | tf_op jit(solution)/shard_map/masks/pallas_call | solution.py:339
  8.6 0.5 %collective-permute-start.6 = (bf16[16,3072]{1,0:T(8,128)(2,1)S(1)}, bf16[16,3072]{1,0:T(8,128)(2,1)S(1)}, u32[]{:S(2)}, u32[]{:S(2)}) collective-permute-start(bf16[16,3072]{1,0:T(8,128)(2,1)S(1)} %get-tuple-element.21), channel_id=1, source_target_pairs={{0,2},{2,0},{4,6},{6,4},{8,10},{10,8},{12,14},{14,12},{16,18},{18,... | collective-permute-start | bytes 294920 | tf_op jit(solution)/shard_map/ppermute | solution.py:26
  9.1 1.7 %collective-permute-start.8 = (bf16[16,5120]{1,0:T(8,128)(2,1)S(1)}, bf16[16,5120]{1,0:T(8,128)(2,1)S(1)}, u32[]{:S(2)}, u32[]{:S(2)}) collective-permute-start(bf16[16,5120]{1,0:T(8,128)(2,1)S(1)} %get-tuple-element.22), channel_id=1, source_target_pairs={{0,1},{1,0},{2,3},{3,2},{4,5},{5,4},{6,7},{7,6},{8,9},{9,8},{10,11... | collective-permute-start | bytes 491528 | tf_op jit(solution)/shard_map/ppermute | solution.py:35
  10.9 0.4 collective-permute-start.1
  11.2 0.0 collective-permute-done.6
  11.2 1.0 %collective-permute-start.7 = (bf16[16,3072]{1,0:T(8,128)(2,1)S(1)}, bf16[16,3072]{1,0:T(8,128)(2,1)S(1)}, u32[]{:S(2)}, u32[]{:S(2)}) collective-permute-start(bf16[16,3072]{1,0:T(8,128)(2,1)S(1)} %collective-permute-done.6), channel_id=1, source_target_pairs={{0,3},{1,2},{2,1},{3,0},{4,7},{5,6},{6,5},{7,4},{8,11},{9,10},{10,... | collective-permute-start | bytes 294920 | tf_op jit(solution)/shard_map/ppermute | solution.py:45
  12.3 16.5 %collective-permute-done.1.refs_0_ = bf16[8,2304]{1,0:T(8,128)(2,1)S(1)} collective-permute-done((bf16[8,2304]{1,0:T(8,128)(2,1)S(1)}, bf16[8,2304]{1,0:T(8,128)(2,1)S(1)}, u32[]{:S(2)}, u32[]{:S(2)}) %collective-permute-start.1) | collective-permute-done | bytes 36896 | tf_op jit(solution)/shard_map/ppermute | solution.py:35
  28.8 0.0 collective-permute-start.2
  28.8 1.2 %collective-permute-done.2.refs_1_ = bf16[8,2304]{1,0:T(8,128)(2,1)S(1)} collective-permute-done((bf16[8,2304]{1,0:T(8,128)(2,1)S(1)}, bf16[8,2304]{1,0:T(8,128)(2,1)S(1)}, u32[]{:S(2)}, u32[]{:S(2)}) %collective-permute-start.2) | collective-permute-done | bytes 36896 | tf_op jit(solution)/shard_map/ppermute | solution.py:26
  30.1 2.0 %collective-permute-start.3 = (f32[2,8,128]{2,1,0:T(8,128)S(1)}, f32[2,8,128]{2,1,0:T(8,128)S(1)}, u32[]{:S(2)}, u32[]{:S(2)}) collective-permute-start(f32[2,8,128]{2,1,0:T(8,128)S(1)} %get-tuple-element.19), channel_id=1, source_target_pairs={{0,4},{2,6},{4,0},{6,2},{8,12},{10,14},{12,8},{14,10},{16,20},{18,... | collective-permute-start | bytes 24584 | tf_op jit(solution)/shard_map/ppermute | solution.py:26
  32.0 1.7 %collective-permute-done.3 = f32[2,8,128]{2,1,0:T(8,128)S(1)} collective-permute-done((f32[2,8,128]{2,1,0:T(8,128)S(1)}, f32[2,8,128]{2,1,0:T(8,128)S(1)}, u32[]{:S(2)}, u32[]{:S(2)}) %collective-permute-start.3) | collective-permute-done | bytes 8224 | tf_op jit(solution)/shard_map/ppermute | solution.py:26
  33.8 2.0 %collective-permute-start.4 = (f32[2,8,128]{2,1,0:T(8,128)S(1)}, f32[2,8,128]{2,1,0:T(8,128)S(1)}, u32[]{:S(2)}, u32[]{:S(2)}) collective-permute-start(f32[2,8,128]{2,1,0:T(8,128)S(1)} %add.9), channel_id=1, source_target_pairs={{0,8},{2,10},{4,12},{6,14},{8,0},{10,2},{12,4},{14,6},{16,24},{18,... | collective-permute-start | bytes 24584 | tf_op jit(solution)/shard_map/ppermute | solution.py:26
  35.8 1.7 %collective-permute-done.4 = f32[2,8,128]{2,1,0:T(8,128)S(1)} collective-permute-done((f32[2,8,128]{2,1,0:T(8,128)S(1)}, f32[2,8,128]{2,1,0:T(8,128)S(1)}, u32[]{:S(2)}, u32[]{:S(2)}) %collective-permute-start.4) | collective-permute-done | bytes 8224 | tf_op jit(solution)/shard_map/ppermute | solution.py:26
  37.4 3.0 %collective-permute-start.5 = (f32[2,8,128]{2,1,0:T(8,128)S(1)}, f32[2,8,128]{2,1,0:T(8,128)S(1)}, u32[]{:S(2)}, u32[]{:S(2)}) collective-permute-start(f32[2,8,128]{2,1,0:T(8,128)S(1)} %add.10), channel_id=1, source_target_pairs={{0,16},{2,18},{4,20},{6,22},{8,24},{10,26},{12,28},{14,30},{16,0},... | collective-permute-start | bytes 24584 | tf_op jit(solution)/shard_map/ppermute | solution.py:26
  40.5 1.6 %masks.3.own = bf16[4,16,8192]{2,1,0:T(8,128)(2,1)S(1)} custom-call(s32[1,4,8]{2,1,0:T(4,128)} %limits.7, s32[1,4,16,16384]{3,2,1,0:T(8,128)} %scores.7, bf16[4,16,16384]{2,1,0:T(8,128)(2,1)S(1)} %get-tuple-element.20.copied), custom_call_target="tpu_custom_call" | custom-call | flops 10000000 | bytes 3145728 | tf_op jit(solution)/shard_map/masks/pallas_call | solution.py:339
  42.1 0.2 scale.1.scales
  42.4 1.1 %merge.3.refs_1_ = bf16[4,16,8192]{2,1,0:T(8,128)(2,1)} custom-call(f32[2,8,4096]{2,1,0:T(8,128)S(1)} %scale.1.scales, bf16[4,16,8192]{2,1,0:T(8,128)(2,1)S(1)} %masks.3.own, bf16[16,8192]{1,0:T(8,128)(2,1)S(1)} %collective-permute-done.9.refs_0_, bf16[16,16384]{1,0:T(8,128)(2,1)S(1)} %collective-permute-done.10.refs_1_), custom_call_target="tpu_custom_call" | custom-call | flops 1000000 | bytes 2359296 | tf_op jit(solution)/shard_map/merge/pallas_call | solution.py:410
  43.5 0.7 %merge.4.refs_1_ = bf16[4,16,8192]{2,1,0:T(8,128)(2,1)} custom-call(f32[2,8,4096]{2,1,0:T(8,128)S(1)} %scale.1.scales, bf16[4,16,8192]{2,1,0:T(8,128)(2,1)S(1)} %masks.3.own, bf16[16,5120]{1,0:T(8,128)(2,1)S(1)} %collective-permute-done.8.refs_0_, bf16[4,16,8192]{2,1,0:T(8,128)(2,1)} %merge.3.refs_1_), custom_call_target="tpu_custom_call", output_to_operand_aliasing={{}: (3, {})} | custom-call | flops 1000000 | bytes 491520 | tf_op jit(solution)/shard_map/merge/pallas_call | solution.py:410
  44.3 0.7 %merge.5 = bf16[4,16,8192]{2,1,0:T(8,128)(2,1)} custom-call(f32[2,8,4096]{2,1,0:T(8,128)S(1)} %scale.1.scales, bf16[4,16,8192]{2,1,0:T(8,128)(2,1)S(1)} %masks.3.own, bf16[16,3072]{1,0:T(8,128)(2,1)S(1)} %collective-permute-done.7.refs_0_, bf16[4,16,8192]{2,1,0:T(8,128)(2,1)} %merge.4.refs_1_), custom_call_target="tpu_custom_call", output_to_operand_aliasing={{}: (3, {})} | custom-call | flops 1000000 | bytes 294912 | tf_op jit(solution)/shard_map/merge/pallas_call | solution.py:410
  (12 shorter events, 0.1 us)
Async XLA Ops:
  3.1 39.3 %collective-permute-start.10 = (bf16[16,16384]{1,0:T(8,128)(2,1)S(1)}, bf16[16,16384]{1,0:T(8,128)(2,1)S(1)}, u32[]{:S(2)}, u32[]{:S(2)}) collective-permute-start(bf16[16,16384]{1,0:T(8,128)(2,1)S(1)} %masks.5), channel_id=1, source_target_pairs={{0,1},{1,0},{2,3},{3,2},{4,5},{5,4},{6,7},{7,6},{8,9},{9,8},{10,11... | collective-permute-start | bytes 1572872 | tf_op jit(solution)/shard_map/ppermute | solution.py:35
  6.1 4.7 %collective-permute-start = (f32[2,8,4224]{2,1,0:T(8,128)S(1)}, f32[2,8,4224]{2,1,0:T(8,128)S(1)}, u32[]{:S(2)}, u32[]{:S(2)}) collective-permute-start(f32[2,8,4224]{2,1,0:T(8,128)S(1)} %get-tuple-element.14.mine), channel_id=1, source_target_pairs={{0,2},{2,0},{4,6},{6,4},{8,10},{10,8},{12,14},{14,12},{16,18},{18,... | collective-permute-start | bytes 811016 | tf_op jit(solution)/shard_map/ppermute | solution.py:26
  7.3 35.0 %collective-permute-start.9 = (bf16[16,8192]{1,0:T(8,128)(2,1)S(1)}, bf16[16,8192]{1,0:T(8,128)(2,1)S(1)}, u32[]{:S(2)}, u32[]{:S(2)}) collective-permute-start(bf16[16,8192]{1,0:T(8,128)(2,1)S(1)} %first.1), channel_id=1, source_target_pairs={{0,1},{1,0},{2,3},{3,2},{4,5},{5,4},{6,7},{7,6},{8,9},{9,8},{10,11... | collective-permute-start | bytes 786440 | tf_op jit(solution)/shard_map/ppermute | solution.py:35
  8.6 2.6 %collective-permute-start.6 = (bf16[16,3072]{1,0:T(8,128)(2,1)S(1)}, bf16[16,3072]{1,0:T(8,128)(2,1)S(1)}, u32[]{:S(2)}, u32[]{:S(2)}) collective-permute-start(bf16[16,3072]{1,0:T(8,128)(2,1)S(1)} %get-tuple-element.21), channel_id=1, source_target_pairs={{0,2},{2,0},{4,6},{6,4},{8,10},{10,8},{12,14},{14,12},{16,18},{18,... | collective-permute-start | bytes 294920 | tf_op jit(solution)/shard_map/ppermute | solution.py:26
  9.1 34.4 %collective-permute-start.8 = (bf16[16,5120]{1,0:T(8,128)(2,1)S(1)}, bf16[16,5120]{1,0:T(8,128)(2,1)S(1)}, u32[]{:S(2)}, u32[]{:S(2)}) collective-permute-start(bf16[16,5120]{1,0:T(8,128)(2,1)S(1)} %get-tuple-element.22), channel_id=1, source_target_pairs={{0,1},{1,0},{2,3},{3,2},{4,5},{5,4},{6,7},{7,6},{8,9},{9,8},{10,11... | collective-permute-start | bytes 491528 | tf_op jit(solution)/shard_map/ppermute | solution.py:35
  10.9 18.0 %collective-permute-start.1 = (bf16[8,2304]{1,0:T(8,128)(2,1)S(1)}, bf16[8,2304]{1,0:T(8,128)(2,1)S(1)}, u32[]{:S(2)}, u32[]{:S(2)}) collective-permute-start(bf16[8,2304]{1,0:T(8,128)(2,1)S(1)} %get-tuple-element.17), channel_id=1, source_target_pairs={{0,1},{1,0},{2,3},{3,2},{4,5},{5,4},{6,7},{7,6},{8,9},{9,8},{10,11... | collective-permute-start | bytes 110600 | tf_op jit(solution)/shard_map/ppermute | solution.py:35
  11.2 33.1 %collective-permute-start.7 = (bf16[16,3072]{1,0:T(8,128)(2,1)S(1)}, bf16[16,3072]{1,0:T(8,128)(2,1)S(1)}, u32[]{:S(2)}, u32[]{:S(2)}) collective-permute-start(bf16[16,3072]{1,0:T(8,128)(2,1)S(1)} %collective-permute-done.6), channel_id=1, source_target_pairs={{0,3},{1,2},{2,1},{3,0},{4,7},{5,6},{6,5},{7,4},{8,11},{9,10},{10,... | collective-permute-start | bytes 294920 | tf_op jit(solution)/shard_map/ppermute | solution.py:45
  28.8 1.2 %collective-permute-start.2 = (bf16[8,2304]{1,0:T(8,128)(2,1)S(1)}, bf16[8,2304]{1,0:T(8,128)(2,1)S(1)}, u32[]{:S(2)}, u32[]{:S(2)}) collective-permute-start(bf16[8,2304]{1,0:T(8,128)(2,1)S(1)} %collective-permute-done.1.refs_0_), channel_id=1, source_target_pairs={{0,2},{2,0},{4,6},{6,4},{8,10},{10,8},{12,14},{14,12},{16,18},{18,... | collective-permute-start | bytes 110600 | tf_op jit(solution)/shard_map/ppermute | solution.py:26
  30.1 3.7 %collective-permute-start.3 = (f32[2,8,128]{2,1,0:T(8,128)S(1)}, f32[2,8,128]{2,1,0:T(8,128)S(1)}, u32[]{:S(2)}, u32[]{:S(2)}) collective-permute-start(f32[2,8,128]{2,1,0:T(8,128)S(1)} %get-tuple-element.19), channel_id=1, source_target_pairs={{0,4},{2,6},{4,0},{6,2},{8,12},{10,14},{12,8},{14,10},{16,20},{18,... | collective-permute-start | bytes 24584 | tf_op jit(solution)/shard_map/ppermute | solution.py:26
  33.8 3.7 %collective-permute-start.4 = (f32[2,8,128]{2,1,0:T(8,128)S(1)}, f32[2,8,128]{2,1,0:T(8,128)S(1)}, u32[]{:S(2)}, u32[]{:S(2)}) collective-permute-start(f32[2,8,128]{2,1,0:T(8,128)S(1)} %add.9), channel_id=1, source_target_pairs={{0,8},{2,10},{4,12},{6,14},{8,0},{10,2},{12,4},{14,6},{16,24},{18,... | collective-permute-start | bytes 24584 | tf_op jit(solution)/shard_map/ppermute | solution.py:26
  37.4 4.7 %collective-permute-start.5 = (f32[2,8,128]{2,1,0:T(8,128)S(1)}, f32[2,8,128]{2,1,0:T(8,128)S(1)}, u32[]{:S(2)}, u32[]{:S(2)}) collective-permute-start(f32[2,8,128]{2,1,0:T(8,128)S(1)} %add.10), channel_id=1, source_target_pairs={{0,16},{2,18},{4,20},{6,22},{8,24},{10,26},{12,28},{14,30},{16,0},... | collective-permute-start | bytes 24584 | tf_op jit(solution)/shard_map/ppermute | solution.py:26

commit v7 on v6

--- a/solution.py
+++ b/solution.py
@@ -13,8 +13,8 @@
 FF = 16384
 LANES = 128
 BLOCK = 2048
-PIECES = 1
-CUT = 5
+CUT = 4
+EXTRA = 0
 GRANT = 16 * 2**20
 
 ANY = pl.BlockSpec(memory_space=pl.ANY)
@@ -55,7 +55,10 @@
 
 
 def blocks(width, body):
-    block = math.gcd(BLOCK, width)
+    block = width if width <= 2 * BLOCK else math.gcd(BLOCK, width)
+    if block == width:
+        body(0, block)
+        return
 
     @pl.loop(0, width // block)
     def _(at):
@@ -64,7 +67,8 @@
 
 def chunk_plan(layers):
     last = layers - 1
-    return [[(0, 0, 8)], [(layer, 0, 8) for layer in range(1, last)], [(last, 0, CUT)], [(last, CUT, 8)]]
+    middle = [(1, EXTRA, 8), *[(layer, 0, 8) for layer in range(2, last)]]
+    return [[(0, 0, 8)], middle, [(last, 0, CUT)], [(last, CUT, 8)]]
 
 
 def chunk_width(chunk, columns):
@@ -75,32 +79,35 @@
     return jnp.where(scores < limit, deltas.astype(jnp.float32), 0.0).astype(jnp.bfloat16)
 
 
-def first_kernel(limits, deltas, scores, *refs):
+def first_kernel(chunk, limits, deltas, scores, *refs):
     tasks = lax.axis_size("task")
     outs = refs[: tasks - 1]
     limit_buf, delta_buf, score_buf, sems = refs[tasks - 1 :]
-    columns = outs[0].shape[1]
-    block = columns // PIECES
+    columns = deltas.shape[3] // tasks
     limit_copy = pltpu.make_async_copy(limits, limit_buf, sems.at[0])
     limit_copy.start()
-    work = [(step, piece) for step in range(1, tasks) for piece in range(PIECES)]
-    copies = []
-    for at, (step, piece) in enumerate(work):
-        source = pl.ds(pl.multiple_of(column_start(step, columns) + piece * block, LANES), block)
-        target = pl.ds(piece * block, block)
-        copies.append([
-            pltpu.make_async_copy(scores.at[0, 0, :, source], score_buf.at[step - 1, :, target], sems.at[2 * at + 1]),
-            pltpu.make_async_copy(deltas.at[0, 0, :, source], delta_buf.at[step - 1, :, target], sems.at[2 * at + 2]),
-        ])
-        for copy in copies[-1]:
-            copy.start()
+    work = []
+    for step in range(1, tasks):
+        offset = 0
+        for layer, begin, end in chunk:
+            size = (end - begin) * columns // 8
+            source = pl.ds(pl.multiple_of(column_start(step, columns) + begin * columns // 8, LANES), size)
+            target = pl.ds(offset, size)
+            at = 2 * len(work)
+            copies = [
+                pltpu.make_async_copy(scores.at[0, layer, :, source], score_buf.at[step - 1, :, target], sems.at[at + 1]),
+                pltpu.make_async_copy(deltas.at[0, layer, :, source], delta_buf.at[step - 1, :, target], sems.at[at + 2]),
+            ]
+            for copy in copies:
+                copy.start()
+            work.append((step, layer, target, copies))
+            offset += size
     limit_copy.wait()
-    limit = limit_buf[0, 0, own_expert()]
-    for at, (step, piece) in enumerate(work):
-        for copy in copies[at]:
+    for step, layer, target, copies in work:
+        for copy in copies:
             copy.wait()
-        where = pl.ds(piece * block, block)
-        outs[step - 1][:, where] = mask_block(delta_buf[step - 1, :, where], score_buf[step - 1, :, where], limit)
+        limit = limit_buf[0, layer, own_expert()]
+        outs[step - 1][:, target] = mask_block(delta_buf[step - 1, :, target], score_buf[step - 1, :, target], limit)
 
 
 def row_sums(changes):
@@ -213,20 +220,23 @@
         store_split(packs[step - 1], total)
 
 
-def join_kernel(own_means, own_totals, *refs):
-    tasks = lax.axis_size("task")
-    means, totals = refs[2 * tasks - 2 :]
-    half = means.shape[2]
-    quarter = half // 2
+def unpack_kernel(own_totals, *refs):
+    arrivals, totals = refs[:-1], refs[-1]
+    totals[0] = own_totals[...]
+    for step, arrival in enumerate(arrivals, 1):
+        both = arrival[:, arrival.shape[1] - 2 * LANES :].astype(jnp.float32)
+        totals[step] = both[:, :LANES] + both[:, LANES:]
+
+
+def join_kernel(own_means, *refs):
+    pairs, means = refs[:-1], refs[-1]
+    quarter = means.shape[2] // 2
     means[0] = own_means[...]
-    totals[0] = own_totals[...]
     other = lax.rem(lax.axis_index("shard") + 1, 2) * quarter
-    for step in range(1, tasks):
-        mine, theirs = refs[2 * step - 2 : 2 * step]
+    for step in range(1, means.shape[0]):
+        mine, theirs = pairs[2 * step - 2 : 2 * step]
         means[step, :, slot_lanes(quarter)] = mine[:, :quarter].astype(jnp.float32)
         means[step, :, pl.ds(pl.multiple_of(other, LANES), quarter)] = theirs[:, :quarter].astype(jnp.float32)
-        both = mine[:, quarter:].astype(jnp.float32)
-        totals[step] = both[:, :LANES] + both[:, LANES:]
 
 
 def scale_kernel(means, totals, scales):
@@ -303,15 +313,15 @@
         pltpu.with_memory_space_constraint(value, pltpu.HBM) for value in (task_deltas, rank_scores, keep_limits)
     ]
     first = pl.pallas_call(
-        first_kernel,
+        functools.partial(first_kernel, plan[0]),
         out_shape=[slabs[0]] * (tasks - 1),
         in_specs=[HBM] * 3,
         out_specs=[VMEM] * (tasks - 1),
         scratch_shapes=[
             pltpu.SMEM(keep_limits.shape, jnp.int32),
-            pltpu.VMEM((tasks - 1, rows, columns), bf16),
-            pltpu.VMEM((tasks - 1, rows, columns), jnp.int32),
-            pltpu.SemaphoreType.DMA((2 * PIECES * (tasks - 1) + 1,)),
+            pltpu.VMEM((tasks - 1, *slabs[0].shape), bf16),
+            pltpu.VMEM((tasks - 1, *slabs[0].shape), jnp.int32),
+            pltpu.SemaphoreType.DMA((2 * len(plan[0]) * (tasks - 1) + 1,)),
         ],
         compiler_params=pltpu.CompilerParams(vmem_limit_bytes=GRANT),
         cost_estimate=cost(10**6, 6 * rows * columns),
@@ -379,18 +389,27 @@
     exchanged = [swapped(sent[(last - 1) * (tasks - 1) + step - 1], "shard", 0) for step in range(1, tasks)]
     arrived.append([shifted_across(exchanged[step - 1], step) for step in range(1, tasks)])
 
-    means, totals = pl.pallas_call(
-        join_kernel,
-        out_shape=[pltpu.VMEM((tasks, 2 * layers, half), f32), pltpu.VMEM((tasks, 2 * layers, LANES), f32)],
-        in_specs=[VMEM] * (2 * tasks),
-        out_specs=[VMEM] * 2,
-        compiler_params=pltpu.CompilerParams(vmem_limit_bytes=GRANT),
-        cost_estimate=cost(10**6, 8 * tasks * layers * half),
-        name="join",
-    )(on_chip(means), on_chip(totals), *[on_chip(value) for value in pairs])
+    totals = pl.pallas_call(
+        unpack_kernel,
+        out_shape=pltpu.VMEM((tasks, 2 * layers, LANES), f32),
+        in_specs=[VMEM] * tasks,
+        out_specs=VMEM,
+        compiler_params=pltpu.CompilerParams(vmem_limit_bytes=GRANT),
+        cost_estimate=cost(10**4, 8 * tasks * layers * LANES),
+        name="unpack",
+    )(on_chip(totals), *[on_chip(value) for value in arrivals])
     for bit in range(group_bits, shards.bit_length() - 1):
         totals = totals + swapped(totals, "shard", bit)
 
+    means = pl.pallas_call(
+        join_kernel,
+        out_shape=pltpu.VMEM((tasks, 2 * layers, half), f32),
+        in_specs=[VMEM] * (2 * tasks - 1),
+        out_specs=VMEM,
+        compiler_params=pltpu.CompilerParams(vmem_limit_bytes=GRANT),
+        cost_estimate=cost(10**4, 8 * tasks * layers * half),
+        name="join",
+    )(on_chip(means), *[on_chip(value) for value in pairs])
     scales = pl.pallas_call(
         scale_kernel,
         out_shape=pltpu.VMEM((tasks, 2 * layers, half), f32),
@@ -402,7 +421,7 @@
     )(on_chip(means), on_chip(totals))
 
     out = None
-    for places in ([0, 1], *[[place] for place in range(2, len(plan))]):
+    for places in ([*range(last)], [last]):
         chunks = [plan[place] for place in places]
         pieces = [piece for place in places for piece in arrived[place]]
         extra = [] if out is None else [out]

time: 45.3 us -> 46.1 us (1.018)
  waiting for transfers between devices: 21.2 us -> 23.1 us
  Pallas kernels: 9.87 us -> 9.16 us
    ppermute x4, waiting for transfers between devices: 16.6 us -> 17.5 us  [shifted(): lax.ppermute(value, 'task', [(source, (source + step) % size) for source...]
    ppermute x6, waiting for transfers between devices: 4.6 us -> 5.54 us  [crossed(): lax.ppermute(value, axis, [(source, source ^ mask) for source in range(la...]
    pallas_call x3 -> x2, Pallas kernels: 2.61 us -> 1.89 us  [merge_all(): pl.pallas_call(functools.partial(merge_kernel, chunks, tasks, len(extra))...]
    ppermute x6, starting transfers between devices: 7.5 us -> 6.82 us  [crossed(): lax.ppermute(value, axis, [(source, source ^ mask) for source in range(la...]
    pallas_call x2 -> x3, Pallas kernels: 1.22 us -> 1.22 us  [the longest x1 1.2 us: merge_all(): pl.pallas_call(functools.partial(first_kernel, plan[0]), out_shape=[slabs...]
  transfers between devices with their start and end apart: 11 -> 11, of which waited for: 4 -> 4; matrix products, arithmetic and copies ran while one was open for 0% -> 0% of each run, Pallas kernels for 14% -> 12%
where the time goes in v7:
time: 46.1 us; the launch traced here: 45.8 us
  waiting for transfers between devices  23.1 us (50%)
  starting transfers between devices  13.5 us (29%)
  Pallas kernels  9.16 us (20%)
    ppermute x4, waiting for transfers between devices, shifted(): lax.ppermute(value, 'task', [(source, (source + step) % size) for source...  17.5 us
    ppermute x6, starting transfers between devices, crossed(): lax.ppermute(value, axis, [(source, source ^ mask) for source in range(la...  6.82 us
    ppermute x4, starting transfers between devices, shifted(): lax.ppermute(value, 'task', [(source, (source + step) % size) for source...  5.7 us
    ppermute x6, waiting for transfers between devices, crossed(): lax.ppermute(value, axis, [(source, source ^ mask) for source in range(la...  5.54 us
    pallas_call x3, Pallas kernels, masks(): pl.pallas_call(functools.partial(mask_kernel, chunks, own_layers), out_sh...  4.03 us
    pallas_call x2, Pallas kernels, merge_all(): pl.pallas_call(functools.partial(merge_kernel, chunks, tasks, len(extra))...  1.89 us
    pallas_call x1, Pallas kernels, merge_all(): pl.pallas_call(sums_kernel, out_shape=[pltpu.VMEM((layers, rows, width),...  1.74 us
    pallas_call x1, Pallas kernels, merge_all(): pl.pallas_call(functools.partial(first_kernel, plan[0]), out_shape=[slabs...  1.2 us
  transfers between devices with their start and end apart: 11, of which 4 were waited for; matrix products, arithmetic and copies ran while one was open for 0% of the time, Pallas kernels for 12%

profile of v7, /device:TPU:0, one launch (start us, length us, event | category | flops | bytes accessed | tf_op | source)
XLA Modules:
  0.0 45.8 jit_solution(14350247393356075804)
XLA Ops:
  0.0 1.7 %sums.1 = (bf16[4,16,16384]{2,1,0:T(8,128)(2,1)S(1)}, f32[2,8,4224]{2,1,0:T(8,128)S(1)}) custom-call(bf16[1,4,16,16384]{3,2,1,0:T(8,128)(2,1)} %deltas.3), custom_call_target="tpu_custom_call" | custom-call | flops 10000000 | bytes 2097152 | tf_op jit(solution)/shard_map/sums/pallas_call | solution.py:333
  1.7 1.3 %masks.5 = bf16[16,16384]{1,0:T(8,128)(2,1)S(1)} custom-call(s32[1,4,8]{2,1,0:T(4,128)} %limits.7, s32[1,4,16,16384]{3,2,1,0:T(8,128)} %scores.7, bf16[4,16,16384]{2,1,0:T(8,128)(2,1)S(1)} %get-tuple-element.16.copied), custom_call_target="tpu_custom_call" | custom-call | flops 10000000 | bytes 1572864 | tf_op jit(solution)/shard_map/masks/pallas_call | solution.py:349
  3.1 3.1 %collective-permute-start.9 = (bf16[16,16384]{1,0:T(8,128)(2,1)S(1)}, bf16[16,16384]{1,0:T(8,128)(2,1)S(1)}, u32[]{:S(2)}, u32[]{:S(2)}) collective-permute-start(bf16[16,16384]{1,0:T(8,128)(2,1)S(1)} %masks.5), channel_id=1, source_target_pairs={{0,1},{1,0},{2,3},{3,2},{4,5},{5,4},{6,7},{7,6},{8,9},{9,8},{10,11... | collective-permute-start | bytes 1572872 | tf_op jit(solution)/shard_map/ppermute | solution.py:35
  6.1 1.2 %first.1 = bf16[16,8192]{1,0:T(8,128)(2,1)S(1)} custom-call(s32[1,4,8]{2,1,0:T(4,128)} %limits.7, bf16[1,4,16,16384]{3,2,1,0:T(8,128)(2,1)} %deltas.3, s32[1,4,16,16384]{3,2,1,0:T(8,128)} %scores.7), custom_call_target="tpu_custom_call" | custom-call | flops 1000000 | bytes 786432 | tf_op jit(solution)/shard_map/first/pallas_call | solution.py:315
  7.3 0.2 collective-permute-start.8
  7.5 1.1 %masks.4 = (bf16[16,4096]{1,0:T(8,128)(2,1)S(1)}, bf16[16,4096]{1,0:T(8,128)(2,1)S(1)}) custom-call(s32[1,4,8]{2,1,0:T(4,128)} %limits.7, s32[1,4,16,16384]{3,2,1,0:T(8,128)} %scores.7, bf16[4,16,16384]{2,1,0:T(8,128)(2,1)S(1)} %get-tuple-element.16.copied), custom_call_target="tpu_custom_call" | custom-call | flops 10000000 | bytes 1572864 | tf_op jit(solution)/shard_map/masks/pallas_call | solution.py:349
  8.6 0.5 %collective-permute-start.6 = (bf16[16,4096]{1,0:T(8,128)(2,1)S(1)}, bf16[16,4096]{1,0:T(8,128)(2,1)S(1)}, u32[]{:S(2)}, u32[]{:S(2)}) collective-permute-start(bf16[16,4096]{1,0:T(8,128)(2,1)S(1)} %get-tuple-element.17), channel_id=1, source_target_pairs={{0,2},{2,0},{4,6},{6,4},{8,10},{10,8},{12,14},{14,12},{16,18},{18,... | collective-permute-start | bytes 393224 | tf_op jit(solution)/shard_map/ppermute | solution.py:26
  9.1 1.7 %collective-permute-start.10 = (bf16[16,4096]{1,0:T(8,128)(2,1)S(1)}, bf16[16,4096]{1,0:T(8,128)(2,1)S(1)}, u32[]{:S(2)}, u32[]{:S(2)}) collective-permute-start(bf16[16,4096]{1,0:T(8,128)(2,1)S(1)} %get-tuple-element.18), channel_id=1, source_target_pairs={{0,1},{1,0},{2,3},{3,2},{4,5},{5,4},{6,7},{7,6},{8,9},{9,8},{10,11... | collective-permute-start | bytes 393224 | tf_op jit(solution)/shard_map/ppermute | solution.py:35
  10.8 0.0 collective-permute-done.6
  10.8 0.9 %collective-permute-start.7 = (bf16[16,4096]{1,0:T(8,128)(2,1)S(1)}, bf16[16,4096]{1,0:T(8,128)(2,1)S(1)}, u32[]{:S(2)}, u32[]{:S(2)}) collective-permute-start(bf16[16,4096]{1,0:T(8,128)(2,1)S(1)} %collective-permute-done.6), channel_id=1, source_target_pairs={{0,3},{1,2},{2,1},{3,0},{4,7},{5,6},{6,5},{7,4},{8,11},{9,10},{10,... | collective-permute-start | bytes 393224 | tf_op jit(solution)/shard_map/ppermute | solution.py:45
  11.8 0.0 collective-permute-done.theirs
  11.8 0.8 %collective-permute-start.1 = (bf16[8,2304]{1,0:T(8,128)(2,1)S(1)}, bf16[8,2304]{1,0:T(8,128)(2,1)S(1)}, u32[]{:S(2)}, u32[]{:S(2)}) collective-permute-start(bf16[8,2304]{1,0:T(8,128)(2,1)S(1)} %get-tuple-element.14), channel_id=1, source_target_pairs={{0,1},{1,0},{2,3},{3,2},{4,5},{5,4},{6,7},{7,6},{8,9},{9,8},{10,11... | collective-permute-start | bytes 110600 | tf_op jit(solution)/shard_map/ppermute | solution.py:35
  12.6 17.5 %collective-permute-done.1.refs_0_ = bf16[8,2304]{1,0:T(8,128)(2,1)S(1)} collective-permute-done((bf16[8,2304]{1,0:T(8,128)(2,1)S(1)}, bf16[8,2304]{1,0:T(8,128)(2,1)S(1)}, u32[]{:S(2)}, u32[]{:S(2)}) %collective-permute-start.1) | collective-permute-done | bytes 36896 | tf_op jit(solution)/shard_map/ppermute | solution.py:35
  30.1 1.7 %collective-permute-start.3 = (f32[2,8,128]{2,1,0:T(8,128)S(1)}, f32[2,8,128]{2,1,0:T(8,128)S(1)}, u32[]{:S(2)}, u32[]{:S(2)}) collective-permute-start(f32[2,8,128]{2,1,0:T(8,128)S(1)} %unpack.1), channel_id=1, source_target_pairs={{0,4},{2,6},{4,0},{6,2},{8,12},{10,14},{12,8},{14,10},{16,20},{18,... | collective-permute-start | bytes 24584 | tf_op jit(solution)/shard_map/ppermute | solution.py:26
  31.8 1.9 %collective-permute-done.3 = f32[2,8,128]{2,1,0:T(8,128)S(1)} collective-permute-done((f32[2,8,128]{2,1,0:T(8,128)S(1)}, f32[2,8,128]{2,1,0:T(8,128)S(1)}, u32[]{:S(2)}, u32[]{:S(2)}) %collective-permute-start.3) | collective-permute-done | bytes 8224 | tf_op jit(solution)/shard_map/ppermute | solution.py:26
  33.7 1.8 %collective-permute-start.4 = (f32[2,8,128]{2,1,0:T(8,128)S(1)}, f32[2,8,128]{2,1,0:T(8,128)S(1)}, u32[]{:S(2)}, u32[]{:S(2)}) collective-permute-start(f32[2,8,128]{2,1,0:T(8,128)S(1)} %add.9), channel_id=1, source_target_pairs={{0,8},{2,10},{4,12},{6,14},{8,0},{10,2},{12,4},{14,6},{16,24},{18,... | collective-permute-start | bytes 24584 | tf_op jit(solution)/shard_map/ppermute | solution.py:26
  35.5 1.9 %collective-permute-done.4 = f32[2,8,128]{2,1,0:T(8,128)S(1)} collective-permute-done((f32[2,8,128]{2,1,0:T(8,128)S(1)}, f32[2,8,128]{2,1,0:T(8,128)S(1)}, u32[]{:S(2)}, u32[]{:S(2)}) %collective-permute-start.4) | collective-permute-done | bytes 8224 | tf_op jit(solution)/shard_map/ppermute | solution.py:26
  37.4 2.8 %collective-permute-start.5 = (f32[2,8,128]{2,1,0:T(8,128)S(1)}, f32[2,8,128]{2,1,0:T(8,128)S(1)}, u32[]{:S(2)}, u32[]{:S(2)}) collective-permute-start(f32[2,8,128]{2,1,0:T(8,128)S(1)} %add.10), channel_id=1, source_target_pairs={{0,16},{2,18},{4,20},{6,22},{8,24},{10,26},{12,28},{14,30},{16,0},... | collective-permute-start | bytes 24584 | tf_op jit(solution)/shard_map/ppermute | solution.py:26
  40.2 1.7 %collective-permute-done.5 = f32[2,8,128]{2,1,0:T(8,128)S(1)} collective-permute-done((f32[2,8,128]{2,1,0:T(8,128)S(1)}, f32[2,8,128]{2,1,0:T(8,128)S(1)}, u32[]{:S(2)}, u32[]{:S(2)}) %collective-permute-start.5) | collective-permute-done | bytes 8224 | tf_op jit(solution)/shard_map/ppermute | solution.py:26
  41.9 1.6 %masks.3.own = bf16[4,16,8192]{2,1,0:T(8,128)(2,1)S(1)} custom-call(s32[1,4,8]{2,1,0:T(4,128)} %limits.7, s32[1,4,16,16384]{3,2,1,0:T(8,128)} %scores.7, bf16[4,16,16384]{2,1,0:T(8,128)(2,1)S(1)} %get-tuple-element.16.copied), custom_call_target="tpu_custom_call" | custom-call | flops 10000000 | bytes 3145728 | tf_op jit(solution)/shard_map/masks/pallas_call | solution.py:349
  43.6 0.0 collective-permute-done.2.refs_1_
  43.6 0.2 scale.1.scales
  43.9 1.2 %merge.2.refs_1_ = bf16[4,16,8192]{2,1,0:T(8,128)(2,1)} custom-call(f32[2,8,4096]{2,1,0:T(8,128)S(1)} %scale.1.scales, bf16[4,16,8192]{2,1,0:T(8,128)(2,1)S(1)} %masks.3.own, bf16[16,8192]{1,0:T(8,128)(2,1)S(1)} %collective-permute-done.8.refs_0_, bf16[16,16384]{1,0:T(8,128)(2,1)S(1)} %collective-permute-done.9.refs_1_, ...), custom_call_target="tpu_custom_call" | custom-call | flops 1000000 | bytes 2752512 | tf_op jit(solution)/shard_map/merge/pallas_call | solution.py:429
  45.1 0.7 %merge.3 = bf16[4,16,8192]{2,1,0:T(8,128)(2,1)} custom-call(f32[2,8,4096]{2,1,0:T(8,128)S(1)} %scale.1.scales, bf16[4,16,8192]{2,1,0:T(8,128)(2,1)S(1)} %masks.3.own, bf16[16,4096]{1,0:T(8,128)(2,1)S(1)} %collective-permute-done.7.refs_0_, bf16[4,16,8192]{2,1,0:T(8,128)(2,1)} %merge.2.refs_1_), custom_call_target="tpu_custom_call", output_to_operand_aliasing={{}: (3, {})} | custom-call | flops 1000000 | bytes 393216 | tf_op jit(solution)/shard_map/merge/pallas_call | solution.py:429
  (12 shorter events, 0.1 us)
Async XLA Ops:
  3.1 40.8 %collective-permute-start.9 = (bf16[16,16384]{1,0:T(8,128)(2,1)S(1)}, bf16[16,16384]{1,0:T(8,128)(2,1)S(1)}, u32[]{:S(2)}, u32[]{:S(2)}) collective-permute-start(bf16[16,16384]{1,0:T(8,128)(2,1)S(1)} %masks.5), channel_id=1, source_target_pairs={{0,1},{1,0},{2,3},{3,2},{4,5},{5,4},{6,7},{7,6},{8,9},{9,8},{10,11... | collective-permute-start | bytes 1572872 | tf_op jit(solution)/shard_map/ppermute | solution.py:35
  6.1 5.6 %collective-permute-start = (f32[2,8,4224]{2,1,0:T(8,128)S(1)}, f32[2,8,4224]{2,1,0:T(8,128)S(1)}, u32[]{:S(2)}, u32[]{:S(2)}) collective-permute-start(f32[2,8,4224]{2,1,0:T(8,128)S(1)} %get-tuple-element.12.mine), channel_id=1, source_target_pairs={{0,2},{2,0},{4,6},{6,4},{8,10},{10,8},{12,14},{14,12},{16,18},{18,... | collective-permute-start | bytes 811016 | tf_op jit(solution)/shard_map/ppermute | solution.py:26
  7.3 36.6 %collective-permute-start.8 = (bf16[16,8192]{1,0:T(8,128)(2,1)S(1)}, bf16[16,8192]{1,0:T(8,128)(2,1)S(1)}, u32[]{:S(2)}, u32[]{:S(2)}) collective-permute-start(bf16[16,8192]{1,0:T(8,128)(2,1)S(1)} %first.1), channel_id=1, source_target_pairs={{0,1},{1,0},{2,3},{3,2},{4,5},{5,4},{6,7},{7,6},{8,9},{9,8},{10,11... | collective-permute-start | bytes 786440 | tf_op jit(solution)/shard_map/ppermute | solution.py:35
  8.6 2.2 %collective-permute-start.6 = (bf16[16,4096]{1,0:T(8,128)(2,1)S(1)}, bf16[16,4096]{1,0:T(8,128)(2,1)S(1)}, u32[]{:S(2)}, u32[]{:S(2)}) collective-permute-start(bf16[16,4096]{1,0:T(8,128)(2,1)S(1)} %get-tuple-element.17), channel_id=1, source_target_pairs={{0,2},{2,0},{4,6},{6,4},{8,10},{10,8},{12,14},{14,12},{16,18},{18,... | collective-permute-start | bytes 393224 | tf_op jit(solution)/shard_map/ppermute | solution.py:26
  9.1 34.8 %collective-permute-start.10 = (bf16[16,4096]{1,0:T(8,128)(2,1)S(1)}, bf16[16,4096]{1,0:T(8,128)(2,1)S(1)}, u32[]{:S(2)}, u32[]{:S(2)}) collective-permute-start(bf16[16,4096]{1,0:T(8,128)(2,1)S(1)} %get-tuple-element.18), channel_id=1, source_target_pairs={{0,1},{1,0},{2,3},{3,2},{4,5},{5,4},{6,7},{7,6},{8,9},{9,8},{10,11... | collective-permute-start | bytes 393224 | tf_op jit(solution)/shard_map/ppermute | solution.py:35
  10.8 34.3 %collective-permute-start.7 = (bf16[16,4096]{1,0:T(8,128)(2,1)S(1)}, bf16[16,4096]{1,0:T(8,128)(2,1)S(1)}, u32[]{:S(2)}, u32[]{:S(2)}) collective-permute-start(bf16[16,4096]{1,0:T(8,128)(2,1)S(1)} %collective-permute-done.6), channel_id=1, source_target_pairs={{0,3},{1,2},{2,1},{3,0},{4,7},{5,6},{6,5},{7,4},{8,11},{9,10},{10,... | collective-permute-start | bytes 393224 | tf_op jit(solution)/shard_map/ppermute | solution.py:45
  11.8 18.3 %collective-permute-start.1 = (bf16[8,2304]{1,0:T(8,128)(2,1)S(1)}, bf16[8,2304]{1,0:T(8,128)(2,1)S(1)}, u32[]{:S(2)}, u32[]{:S(2)}) collective-permute-start(bf16[8,2304]{1,0:T(8,128)(2,1)S(1)} %get-tuple-element.14), channel_id=1, source_target_pairs={{0,1},{1,0},{2,3},{3,2},{4,5},{5,4},{6,7},{7,6},{8,9},{9,8},{10,11... | collective-permute-start | bytes 110600 | tf_op jit(solution)/shard_map/ppermute | solution.py:35
  30.1 3.7 %collective-permute-start.3 = (f32[2,8,128]{2,1,0:T(8,128)S(1)}, f32[2,8,128]{2,1,0:T(8,128)S(1)}, u32[]{:S(2)}, u32[]{:S(2)}) collective-permute-start(f32[2,8,128]{2,1,0:T(8,128)S(1)} %unpack.1), channel_id=1, source_target_pairs={{0,4},{2,6},{4,0},{6,2},{8,12},{10,14},{12,8},{14,10},{16,20},{18,... | collective-permute-start | bytes 24584 | tf_op jit(solution)/shard_map/ppermute | solution.py:26
  33.7 3.7 %collective-permute-start.4 = (f32[2,8,128]{2,1,0:T(8,128)S(1)}, f32[2,8,128]{2,1,0:T(8,128)S(1)}, u32[]{:S(2)}, u32[]{:S(2)}) collective-permute-start(f32[2,8,128]{2,1,0:T(8,128)S(1)} %add.9), channel_id=1, source_target_pairs={{0,8},{2,10},{4,12},{6,14},{8,0},{10,2},{12,4},{14,6},{16,24},{18,... | collective-permute-start | bytes 24584 | tf_op jit(solution)/shard_map/ppermute | solution.py:26
  37.4 4.5 %collective-permute-start.5 = (f32[2,8,128]{2,1,0:T(8,128)S(1)}, f32[2,8,128]{2,1,0:T(8,128)S(1)}, u32[]{:S(2)}, u32[]{:S(2)}) collective-permute-start(f32[2,8,128]{2,1,0:T(8,128)S(1)} %add.10), channel_id=1, source_target_pairs={{0,16},{2,18},{4,20},{6,22},{8,24},{10,26},{12,28},{14,30},{16,0},... | collective-permute-start | bytes 24584 | tf_op jit(solution)/shard_map/ppermute | solution.py:26
  41.9 1.7 %collective-permute-start.2 = (bf16[8,2304]{1,0:T(8,128)(2,1)S(1)}, bf16[8,2304]{1,0:T(8,128)(2,1)S(1)}, u32[]{:S(2)}, u32[]{:S(2)}) collective-permute-start(bf16[8,2304]{1,0:T(8,128)(2,1)S(1)} %collective-permute-done.1.refs_0_), channel_id=1, source_target_pairs={{0,2},{2,0},{4,6},{6,4},{8,10},{10,8},{12,14},{14,12},{16,18},{18,... | collective-permute-start | bytes 110600 | tf_op jit(solution)/shard_map/ppermute | solution.py:26

commit v8 on v7

--- a/solution.py
+++ b/solution.py
@@ -159,10 +159,10 @@
 
 
 def store_split(pack, totals):
-    half = pack.shape[1] - 2 * LANES
-    high = totals.astype(jnp.bfloat16)
-    pack[:, half : half + LANES] = high
-    pack[:, half + LANES :] = (totals - high.astype(jnp.float32)).astype(jnp.bfloat16)
+    layers = totals.shape[0] // 2
+    folded = totals[:layers] + totals[layers:]
+    high = folded.astype(jnp.bfloat16).astype(jnp.float32)
+    pack[:, pack.shape[1] - LANES :] = jnp.concatenate([high, folded - high], axis=0).astype(jnp.bfloat16)
 
 
 def mask_kernel(chunks, own_layers, limits, scores, copied, *refs):
@@ -224,8 +224,7 @@
     arrivals, totals = refs[:-1], refs[-1]
     totals[0] = own_totals[...]
     for step, arrival in enumerate(arrivals, 1):
-        both = arrival[:, arrival.shape[1] - 2 * LANES :].astype(jnp.float32)
-        totals[step] = both[:, :LANES] + both[:, LANES:]
+        totals[step] = arrival[:, arrival.shape[1] - LANES :].astype(jnp.float32)
 
 
 def join_kernel(own_means, *refs):
@@ -368,7 +367,7 @@
     means, totals, *packs = pl.pallas_call(
         pair_kernel,
         out_shape=[pltpu.VMEM((2 * layers, half), f32), pltpu.VMEM((2 * layers, LANES), f32)]
-        + [pltpu.VMEM((2 * layers, half // 2 + 2 * LANES), bf16)] * (tasks - 1),
+        + [pltpu.VMEM((2 * layers, half // 2 + LANES), bf16)] * (tasks - 1),
         in_specs=[VMEM] * 2,
         out_specs=[VMEM] * (tasks + 1),
         compiler_params=pltpu.CompilerParams(vmem_limit_bytes=GRANT),

time: 46.1 us -> 46 us (level)
  no operation moved by 1% of the time
where the time goes in v8:
time: 46 us; the launch traced here: 45.8 us
  waiting for transfers between devices  23 us (50%)
  starting transfers between devices  13.5 us (29%)
  Pallas kernels  9.16 us (20%)
    ppermute x4, waiting for transfers between devices, shifted(): lax.ppermute(value, 'task', [(source, (source + step) % size) for source...  17.5 us
    ppermute x6, starting transfers between devices, crossed(): lax.ppermute(value, axis, [(source, source ^ mask) for source in range(la...  6.82 us
    ppermute x4, starting transfers between devices, shifted(): lax.ppermute(value, 'task', [(source, (source + step) % size) for source...  5.7 us
    ppermute x6, waiting for transfers between devices, crossed(): lax.ppermute(value, axis, [(source, source ^ mask) for source in range(la...  5.54 us
    pallas_call x3, Pallas kernels, masks(): pl.pallas_call(functools.partial(mask_kernel, chunks, own_layers), out_sh...  4.03 us
    pallas_call x2, Pallas kernels, merge_all(): pl.pallas_call(functools.partial(merge_kernel, chunks, tasks, len(extra))...  1.89 us
    pallas_call x1, Pallas kernels, merge_all(): pl.pallas_call(sums_kernel, out_shape=[pltpu.VMEM((layers, rows, width),...  1.74 us
    pallas_call x1, Pallas kernels, merge_all(): pl.pallas_call(functools.partial(first_kernel, plan[0]), out_shape=[slabs...  1.2 us
  transfers between devices with their start and end apart: 11, of which 4 were waited for; matrix products, arithmetic and copies ran while one was open for 0% of the time, Pallas kernels for 12%

profile of v8, /device:TPU:0, one launch (start us, length us, event | category | flops | bytes accessed | tf_op | source)
XLA Modules:
  0.0 45.8 jit_solution(8485105349342665469)
XLA Ops:
  0.0 1.7 %sums.1 = (bf16[4,16,16384]{2,1,0:T(8,128)(2,1)S(1)}, f32[2,8,4224]{2,1,0:T(8,128)S(1)}) custom-call(bf16[1,4,16,16384]{3,2,1,0:T(8,128)(2,1)} %deltas.3), custom_call_target="tpu_custom_call" | custom-call | flops 10000000 | bytes 2097152 | tf_op jit(solution)/shard_map/sums/pallas_call | solution.py:332
  1.7 1.3 %masks.5 = bf16[16,16384]{1,0:T(8,128)(2,1)S(1)} custom-call(s32[1,4,8]{2,1,0:T(4,128)} %limits.7, s32[1,4,16,16384]{3,2,1,0:T(8,128)} %scores.7, bf16[4,16,16384]{2,1,0:T(8,128)(2,1)S(1)} %get-tuple-element.16.copied), custom_call_target="tpu_custom_call" | custom-call | flops 10000000 | bytes 1572864 | tf_op jit(solution)/shard_map/masks/pallas_call | solution.py:348
  3.1 3.1 %collective-permute-start.9 = (bf16[16,16384]{1,0:T(8,128)(2,1)S(1)}, bf16[16,16384]{1,0:T(8,128)(2,1)S(1)}, u32[]{:S(2)}, u32[]{:S(2)}) collective-permute-start(bf16[16,16384]{1,0:T(8,128)(2,1)S(1)} %masks.5), channel_id=1, source_target_pairs={{0,1},{1,0},{2,3},{3,2},{4,5},{5,4},{6,7},{7,6},{8,9},{9,8},{10,11... | collective-permute-start | bytes 1572872 | tf_op jit(solution)/shard_map/ppermute | solution.py:35
  6.1 1.2 %first.1 = bf16[16,8192]{1,0:T(8,128)(2,1)S(1)} custom-call(s32[1,4,8]{2,1,0:T(4,128)} %limits.7, bf16[1,4,16,16384]{3,2,1,0:T(8,128)(2,1)} %deltas.3, s32[1,4,16,16384]{3,2,1,0:T(8,128)} %scores.7), custom_call_target="tpu_custom_call" | custom-call | flops 1000000 | bytes 786432 | tf_op jit(solution)/shard_map/first/pallas_call | solution.py:314
  7.3 0.2 collective-permute-start.8
  7.5 1.1 %masks.4 = (bf16[16,4096]{1,0:T(8,128)(2,1)S(1)}, bf16[16,4096]{1,0:T(8,128)(2,1)S(1)}) custom-call(s32[1,4,8]{2,1,0:T(4,128)} %limits.7, s32[1,4,16,16384]{3,2,1,0:T(8,128)} %scores.7, bf16[4,16,16384]{2,1,0:T(8,128)(2,1)S(1)} %get-tuple-element.16.copied), custom_call_target="tpu_custom_call" | custom-call | flops 10000000 | bytes 1572864 | tf_op jit(solution)/shard_map/masks/pallas_call | solution.py:348
  8.6 0.5 %collective-permute-start.6 = (bf16[16,4096]{1,0:T(8,128)(2,1)S(1)}, bf16[16,4096]{1,0:T(8,128)(2,1)S(1)}, u32[]{:S(2)}, u32[]{:S(2)}) collective-permute-start(bf16[16,4096]{1,0:T(8,128)(2,1)S(1)} %get-tuple-element.17), channel_id=1, source_target_pairs={{0,2},{2,0},{4,6},{6,4},{8,10},{10,8},{12,14},{14,12},{16,18},{18,... | collective-permute-start | bytes 393224 | tf_op jit(solution)/shard_map/ppermute | solution.py:26
  9.1 1.7 %collective-permute-start.10 = (bf16[16,4096]{1,0:T(8,128)(2,1)S(1)}, bf16[16,4096]{1,0:T(8,128)(2,1)S(1)}, u32[]{:S(2)}, u32[]{:S(2)}) collective-permute-start(bf16[16,4096]{1,0:T(8,128)(2,1)S(1)} %get-tuple-element.18), channel_id=1, source_target_pairs={{0,1},{1,0},{2,3},{3,2},{4,5},{5,4},{6,7},{7,6},{8,9},{9,8},{10,11... | collective-permute-start | bytes 393224 | tf_op jit(solution)/shard_map/ppermute | solution.py:35
  10.8 0.0 collective-permute-done.6
  10.8 0.9 %collective-permute-start.7 = (bf16[16,4096]{1,0:T(8,128)(2,1)S(1)}, bf16[16,4096]{1,0:T(8,128)(2,1)S(1)}, u32[]{:S(2)}, u32[]{:S(2)}) collective-permute-start(bf16[16,4096]{1,0:T(8,128)(2,1)S(1)} %collective-permute-done.6), channel_id=1, source_target_pairs={{0,3},{1,2},{2,1},{3,0},{4,7},{5,6},{6,5},{7,4},{8,11},{9,10},{10,... | collective-permute-start | bytes 393224 | tf_op jit(solution)/shard_map/ppermute | solution.py:45
  11.8 0.0 collective-permute-done.theirs
  11.8 0.7 %collective-permute-start.1 = (bf16[8,2176]{1,0:T(8,128)(2,1)S(1)}, bf16[8,2176]{1,0:T(8,128)(2,1)S(1)}, u32[]{:S(2)}, u32[]{:S(2)}) collective-permute-start(bf16[8,2176]{1,0:T(8,128)(2,1)S(1)} %get-tuple-element.14), channel_id=1, source_target_pairs={{0,1},{1,0},{2,3},{3,2},{4,5},{5,4},{6,7},{7,6},{8,9},{9,8},{10,11... | collective-permute-start | bytes 104456 | tf_op jit(solution)/shard_map/ppermute | solution.py:35
  12.6 17.5 %collective-permute-done.1.refs_0_ = bf16[8,2176]{1,0:T(8,128)(2,1)S(1)} collective-permute-done((bf16[8,2176]{1,0:T(8,128)(2,1)S(1)}, bf16[8,2176]{1,0:T(8,128)(2,1)S(1)}, u32[]{:S(2)}, u32[]{:S(2)}) %collective-permute-start.1) | collective-permute-done | bytes 34848 | tf_op jit(solution)/shard_map/ppermute | solution.py:35
  30.0 1.7 %collective-permute-start.3 = (f32[2,8,128]{2,1,0:T(8,128)S(1)}, f32[2,8,128]{2,1,0:T(8,128)S(1)}, u32[]{:S(2)}, u32[]{:S(2)}) collective-permute-start(f32[2,8,128]{2,1,0:T(8,128)S(1)} %unpack.1), channel_id=1, source_target_pairs={{0,4},{2,6},{4,0},{6,2},{8,12},{10,14},{12,8},{14,10},{16,20},{18,... | collective-permute-start | bytes 24584 | tf_op jit(solution)/shard_map/ppermute | solution.py:26
  31.7 1.9 %collective-permute-done.3 = f32[2,8,128]{2,1,0:T(8,128)S(1)} collective-permute-done((f32[2,8,128]{2,1,0:T(8,128)S(1)}, f32[2,8,128]{2,1,0:T(8,128)S(1)}, u32[]{:S(2)}, u32[]{:S(2)}) %collective-permute-start.3) | collective-permute-done | bytes 8224 | tf_op jit(solution)/shard_map/ppermute | solution.py:26
  33.7 1.8 %collective-permute-start.4 = (f32[2,8,128]{2,1,0:T(8,128)S(1)}, f32[2,8,128]{2,1,0:T(8,128)S(1)}, u32[]{:S(2)}, u32[]{:S(2)}) collective-permute-start(f32[2,8,128]{2,1,0:T(8,128)S(1)} %add.9), channel_id=1, source_target_pairs={{0,8},{2,10},{4,12},{6,14},{8,0},{10,2},{12,4},{14,6},{16,24},{18,... | collective-permute-start | bytes 24584 | tf_op jit(solution)/shard_map/ppermute | solution.py:26
  35.5 1.9 %collective-permute-done.4 = f32[2,8,128]{2,1,0:T(8,128)S(1)} collective-permute-done((f32[2,8,128]{2,1,0:T(8,128)S(1)}, f32[2,8,128]{2,1,0:T(8,128)S(1)}, u32[]{:S(2)}, u32[]{:S(2)}) %collective-permute-start.4) | collective-permute-done | bytes 8224 | tf_op jit(solution)/shard_map/ppermute | solution.py:26
  37.3 2.8 %collective-permute-start.5 = (f32[2,8,128]{2,1,0:T(8,128)S(1)}, f32[2,8,128]{2,1,0:T(8,128)S(1)}, u32[]{:S(2)}, u32[]{:S(2)}) collective-permute-start(f32[2,8,128]{2,1,0:T(8,128)S(1)} %add.10), channel_id=1, source_target_pairs={{0,16},{2,18},{4,20},{6,22},{8,24},{10,26},{12,28},{14,30},{16,0},... | collective-permute-start | bytes 24584 | tf_op jit(solution)/shard_map/ppermute | solution.py:26
  40.2 1.7 %collective-permute-done.5 = f32[2,8,128]{2,1,0:T(8,128)S(1)} collective-permute-done((f32[2,8,128]{2,1,0:T(8,128)S(1)}, f32[2,8,128]{2,1,0:T(8,128)S(1)}, u32[]{:S(2)}, u32[]{:S(2)}) %collective-permute-start.5) | collective-permute-done | bytes 8224 | tf_op jit(solution)/shard_map/ppermute | solution.py:26
  41.9 1.6 %masks.3.own = bf16[4,16,8192]{2,1,0:T(8,128)(2,1)S(1)} custom-call(s32[1,4,8]{2,1,0:T(4,128)} %limits.7, s32[1,4,16,16384]{3,2,1,0:T(8,128)} %scores.7, bf16[4,16,16384]{2,1,0:T(8,128)(2,1)S(1)} %get-tuple-element.16.copied), custom_call_target="tpu_custom_call" | custom-call | flops 10000000 | bytes 3145728 | tf_op jit(solution)/shard_map/masks/pallas_call | solution.py:348
  43.6 0.0 collective-permute-done.2.refs_1_
  43.6 0.2 scale.1.scales
  43.9 1.2 %merge.2.refs_1_ = bf16[4,16,8192]{2,1,0:T(8,128)(2,1)} custom-call(f32[2,8,4096]{2,1,0:T(8,128)S(1)} %scale.1.scales, bf16[4,16,8192]{2,1,0:T(8,128)(2,1)S(1)} %masks.3.own, bf16[16,8192]{1,0:T(8,128)(2,1)S(1)} %collective-permute-done.8.refs_0_, bf16[16,16384]{1,0:T(8,128)(2,1)S(1)} %collective-permute-done.9.refs_1_, ...), custom_call_target="tpu_custom_call" | custom-call | flops 1000000 | bytes 2752512 | tf_op jit(solution)/shard_map/merge/pallas_call | solution.py:428
  45.0 0.7 %merge.3 = bf16[4,16,8192]{2,1,0:T(8,128)(2,1)} custom-call(f32[2,8,4096]{2,1,0:T(8,128)S(1)} %scale.1.scales, bf16[4,16,8192]{2,1,0:T(8,128)(2,1)S(1)} %masks.3.own, bf16[16,4096]{1,0:T(8,128)(2,1)S(1)} %collective-permute-done.7.refs_0_, bf16[4,16,8192]{2,1,0:T(8,128)(2,1)} %merge.2.refs_1_), custom_call_target="tpu_custom_call", output_to_operand_aliasing={{}: (3, {})} | custom-call | flops 1000000 | bytes 393216 | tf_op jit(solution)/shard_map/merge/pallas_call | solution.py:428
  (12 shorter events, 0.1 us)
Async XLA Ops:
  3.1 40.8 %collective-permute-start.9 = (bf16[16,16384]{1,0:T(8,128)(2,1)S(1)}, bf16[16,16384]{1,0:T(8,128)(2,1)S(1)}, u32[]{:S(2)}, u32[]{:S(2)}) collective-permute-start(bf16[16,16384]{1,0:T(8,128)(2,1)S(1)} %masks.5), channel_id=1, source_target_pairs={{0,1},{1,0},{2,3},{3,2},{4,5},{5,4},{6,7},{7,6},{8,9},{9,8},{10,11... | collective-permute-start | bytes 1572872 | tf_op jit(solution)/shard_map/ppermute | solution.py:35
  6.1 5.6 %collective-permute-start = (f32[2,8,4224]{2,1,0:T(8,128)S(1)}, f32[2,8,4224]{2,1,0:T(8,128)S(1)}, u32[]{:S(2)}, u32[]{:S(2)}) collective-permute-start(f32[2,8,4224]{2,1,0:T(8,128)S(1)} %get-tuple-element.12.mine), channel_id=1, source_target_pairs={{0,2},{2,0},{4,6},{6,4},{8,10},{10,8},{12,14},{14,12},{16,18},{18,... | collective-permute-start | bytes 811016 | tf_op jit(solution)/shard_map/ppermute | solution.py:26
  7.3 36.5 %collective-permute-start.8 = (bf16[16,8192]{1,0:T(8,128)(2,1)S(1)}, bf16[16,8192]{1,0:T(8,128)(2,1)S(1)}, u32[]{:S(2)}, u32[]{:S(2)}) collective-permute-start(bf16[16,8192]{1,0:T(8,128)(2,1)S(1)} %first.1), channel_id=1, source_target_pairs={{0,1},{1,0},{2,3},{3,2},{4,5},{5,4},{6,7},{7,6},{8,9},{9,8},{10,11... | collective-permute-start | bytes 786440 | tf_op jit(solution)/shard_map/ppermute | solution.py:35
  8.6 2.2 %collective-permute-start.6 = (bf16[16,4096]{1,0:T(8,128)(2,1)S(1)}, bf16[16,4096]{1,0:T(8,128)(2,1)S(1)}, u32[]{:S(2)}, u32[]{:S(2)}) collective-permute-start(bf16[16,4096]{1,0:T(8,128)(2,1)S(1)} %get-tuple-element.17), channel_id=1, source_target_pairs={{0,2},{2,0},{4,6},{6,4},{8,10},{10,8},{12,14},{14,12},{16,18},{18,... | collective-permute-start | bytes 393224 | tf_op jit(solution)/shard_map/ppermute | solution.py:26
  9.1 34.7 %collective-permute-start.10 = (bf16[16,4096]{1,0:T(8,128)(2,1)S(1)}, bf16[16,4096]{1,0:T(8,128)(2,1)S(1)}, u32[]{:S(2)}, u32[]{:S(2)}) collective-permute-start(bf16[16,4096]{1,0:T(8,128)(2,1)S(1)} %get-tuple-element.18), channel_id=1, source_target_pairs={{0,1},{1,0},{2,3},{3,2},{4,5},{5,4},{6,7},{7,6},{8,9},{9,8},{10,11... | collective-permute-start | bytes 393224 | tf_op jit(solution)/shard_map/ppermute | solution.py:35
  10.8 34.2 %collective-permute-start.7 = (bf16[16,4096]{1,0:T(8,128)(2,1)S(1)}, bf16[16,4096]{1,0:T(8,128)(2,1)S(1)}, u32[]{:S(2)}, u32[]{:S(2)}) collective-permute-start(bf16[16,4096]{1,0:T(8,128)(2,1)S(1)} %collective-permute-done.6), channel_id=1, source_target_pairs={{0,3},{1,2},{2,1},{3,0},{4,7},{5,6},{6,5},{7,4},{8,11},{9,10},{10,... | collective-permute-start | bytes 393224 | tf_op jit(solution)/shard_map/ppermute | solution.py:45
  11.8 18.2 %collective-permute-start.1 = (bf16[8,2176]{1,0:T(8,128)(2,1)S(1)}, bf16[8,2176]{1,0:T(8,128)(2,1)S(1)}, u32[]{:S(2)}, u32[]{:S(2)}) collective-permute-start(bf16[8,2176]{1,0:T(8,128)(2,1)S(1)} %get-tuple-element.14), channel_id=1, source_target_pairs={{0,1},{1,0},{2,3},{3,2},{4,5},{5,4},{6,7},{7,6},{8,9},{9,8},{10,11... | collective-permute-start | bytes 104456 | tf_op jit(solution)/shard_map/ppermute | solution.py:35
  30.0 3.7 %collective-permute-start.3 = (f32[2,8,128]{2,1,0:T(8,128)S(1)}, f32[2,8,128]{2,1,0:T(8,128)S(1)}, u32[]{:S(2)}, u32[]{:S(2)}) collective-permute-start(f32[2,8,128]{2,1,0:T(8,128)S(1)} %unpack.1), channel_id=1, source_target_pairs={{0,4},{2,6},{4,0},{6,2},{8,12},{10,14},{12,8},{14,10},{16,20},{18,... | collective-permute-start | bytes 24584 | tf_op jit(solution)/shard_map/ppermute | solution.py:26
  33.7 3.7 %collective-permute-start.4 = (f32[2,8,128]{2,1,0:T(8,128)S(1)}, f32[2,8,128]{2,1,0:T(8,128)S(1)}, u32[]{:S(2)}, u32[]{:S(2)}) collective-permute-start(f32[2,8,128]{2,1,0:T(8,128)S(1)} %add.9), channel_id=1, source_target_pairs={{0,8},{2,10},{4,12},{6,14},{8,0},{10,2},{12,4},{14,6},{16,24},{18,... | collective-permute-start | bytes 24584 | tf_op jit(solution)/shard_map/ppermute | solution.py:26
  37.3 4.5 %collective-permute-start.5 = (f32[2,8,128]{2,1,0:T(8,128)S(1)}, f32[2,8,128]{2,1,0:T(8,128)S(1)}, u32[]{:S(2)}, u32[]{:S(2)}) collective-permute-start(f32[2,8,128]{2,1,0:T(8,128)S(1)} %add.10), channel_id=1, source_target_pairs={{0,16},{2,18},{4,20},{6,22},{8,24},{10,26},{12,28},{14,30},{16,0},... | collective-permute-start | bytes 24584 | tf_op jit(solution)/shard_map/ppermute | solution.py:26
  41.9 1.7 %collective-permute-start.2 = (bf16[8,2176]{1,0:T(8,128)(2,1)S(1)}, bf16[8,2176]{1,0:T(8,128)(2,1)S(1)}, u32[]{:S(2)}, u32[]{:S(2)}) collective-permute-start(bf16[8,2176]{1,0:T(8,128)(2,1)S(1)} %collective-permute-done.1.refs_0_), channel_id=1, source_target_pairs={{0,2},{2,0},{4,6},{6,4},{8,10},{10,8},{12,14},{14,12},{16,18},{18,... | collective-permute-start | bytes 104456 | tf_op jit(solution)/shard_map/ppermute | solution.py:26

commit v9 on v8

--- a/solution.py
+++ b/solution.py
@@ -262,9 +262,10 @@
         for layer, begin, end in chunk:
             for part in range(2):
                 low, high = [min(max(at * columns // 8 - part * half, 0), half) for at in (begin, end)]
-                if high > low:
-                    pieces.append((place, base, layer, part, low, high - low, offset))
-                    offset += high - low
+                size = (high - low) // (4 if len(chunks) == 1 else 1)
+                for start in range(low, high, size or 1):
+                    pieces.append((place, base, layer, part, start, size, offset))
+                    offset += size
         base += offset
     copies = []
     for at, (place, base, layer, part, low, size, offset) in enumerate(pieces):
@@ -432,7 +433,7 @@
             out_specs=ANY,
             scratch_shapes=[
                 pltpu.VMEM((rows, merged_width), bf16),
-                pltpu.SemaphoreType.DMA((2 * sum(len(chunk) for chunk in chunks),)),
+                pltpu.SemaphoreType.DMA((max(4, 2 * sum(len(chunk) for chunk in chunks)),)),
             ],
             input_output_aliases={2 + len(pieces): 0} if extra else {},
             compiler_params=pltpu.CompilerParams(vmem_limit_bytes=GRANT),

time: 46 us -> 46 us (level)
  no operation moved by 1% of the time
where the time goes in v9:
time: 46 us; the launch traced here: 45.8 us
  waiting for transfers between devices  23 us (50%)
  starting transfers between devices  13.5 us (29%)
  Pallas kernels  9.13 us (20%)
    ppermute x4, waiting for transfers between devices, shifted(): lax.ppermute(value, 'task', [(source, (source + step) % size) for source...  17.5 us
    ppermute x6, starting transfers between devices, crossed(): lax.ppermute(value, axis, [(source, source ^ mask) for source in range(la...  6.82 us
    ppermute x4, starting transfers between devices, shifted(): lax.ppermute(value, 'task', [(source, (source + step) % size) for source...  5.7 us
    ppermute x6, waiting for transfers between devices, crossed(): lax.ppermute(value, axis, [(source, source ^ mask) for source in range(la...  5.54 us
    pallas_call x3, Pallas kernels, masks(): pl.pallas_call(functools.partial(mask_kernel, chunks, own_layers), out_sh...  4.03 us
    pallas_call x2, Pallas kernels, merge_all(): pl.pallas_call(functools.partial(merge_kernel, chunks, tasks, len(extra))...  1.87 us
    pallas_call x1, Pallas kernels, merge_all(): pl.pallas_call(sums_kernel, out_shape=[pltpu.VMEM((layers, rows, width),...  1.74 us
    pallas_call x1, Pallas kernels, merge_all(): pl.pallas_call(functools.partial(first_kernel, plan[0]), out_shape=[slabs...  1.2 us
  transfers between devices with their start and end apart: 11, of which 4 were waited for; matrix products, arithmetic and copies ran while one was open for 0% of the time, Pallas kernels for 12%

profile of v9, /device:TPU:0, one launch (start us, length us, event | category | flops | bytes accessed | tf_op | source)
XLA Modules:
  0.0 45.8 jit_solution(9925356826789833191)
XLA Ops:
  0.0 1.7 %sums.1 = (bf16[4,16,16384]{2,1,0:T(8,128)(2,1)S(1)}, f32[2,8,4224]{2,1,0:T(8,128)S(1)}) custom-call(bf16[1,4,16,16384]{3,2,1,0:T(8,128)(2,1)} %deltas.3), custom_call_target="tpu_custom_call" | custom-call | flops 10000000 | bytes 2097152 | tf_op jit(solution)/shard_map/sums/pallas_call | solution.py:333
  1.7 1.3 %masks.5 = bf16[16,16384]{1,0:T(8,128)(2,1)S(1)} custom-call(s32[1,4,8]{2,1,0:T(4,128)} %limits.7, s32[1,4,16,16384]{3,2,1,0:T(8,128)} %scores.7, bf16[4,16,16384]{2,1,0:T(8,128)(2,1)S(1)} %get-tuple-element.16.copied), custom_call_target="tpu_custom_call" | custom-call | flops 10000000 | bytes 1572864 | tf_op jit(solution)/shard_map/masks/pallas_call | solution.py:349
  3.1 3.1 %collective-permute-start.9 = (bf16[16,16384]{1,0:T(8,128)(2,1)S(1)}, bf16[16,16384]{1,0:T(8,128)(2,1)S(1)}, u32[]{:S(2)}, u32[]{:S(2)}) collective-permute-start(bf16[16,16384]{1,0:T(8,128)(2,1)S(1)} %masks.5), channel_id=1, source_target_pairs={{0,1},{1,0},{2,3},{3,2},{4,5},{5,4},{6,7},{7,6},{8,9},{9,8},{10,11... | collective-permute-start | bytes 1572872 | tf_op jit(solution)/shard_map/ppermute | solution.py:35
  6.1 1.2 %first.1 = bf16[16,8192]{1,0:T(8,128)(2,1)S(1)} custom-call(s32[1,4,8]{2,1,0:T(4,128)} %limits.7, bf16[1,4,16,16384]{3,2,1,0:T(8,128)(2,1)} %deltas.3, s32[1,4,16,16384]{3,2,1,0:T(8,128)} %scores.7), custom_call_target="tpu_custom_call" | custom-call | flops 1000000 | bytes 786432 | tf_op jit(solution)/shard_map/first/pallas_call | solution.py:315
  7.3 0.2 collective-permute-start.8
  7.5 1.1 %masks.4 = (bf16[16,4096]{1,0:T(8,128)(2,1)S(1)}, bf16[16,4096]{1,0:T(8,128)(2,1)S(1)}) custom-call(s32[1,4,8]{2,1,0:T(4,128)} %limits.7, s32[1,4,16,16384]{3,2,1,0:T(8,128)} %scores.7, bf16[4,16,16384]{2,1,0:T(8,128)(2,1)S(1)} %get-tuple-element.16.copied), custom_call_target="tpu_custom_call" | custom-call | flops 10000000 | bytes 1572864 | tf_op jit(solution)/shard_map/masks/pallas_call | solution.py:349
  8.6 0.5 %collective-permute-start.6 = (bf16[16,4096]{1,0:T(8,128)(2,1)S(1)}, bf16[16,4096]{1,0:T(8,128)(2,1)S(1)}, u32[]{:S(2)}, u32[]{:S(2)}) collective-permute-start(bf16[16,4096]{1,0:T(8,128)(2,1)S(1)} %get-tuple-element.17), channel_id=1, source_target_pairs={{0,2},{2,0},{4,6},{6,4},{8,10},{10,8},{12,14},{14,12},{16,18},{18,... | collective-permute-start | bytes 393224 | tf_op jit(solution)/shard_map/ppermute | solution.py:26
  9.1 1.7 %collective-permute-start.10 = (bf16[16,4096]{1,0:T(8,128)(2,1)S(1)}, bf16[16,4096]{1,0:T(8,128)(2,1)S(1)}, u32[]{:S(2)}, u32[]{:S(2)}) collective-permute-start(bf16[16,4096]{1,0:T(8,128)(2,1)S(1)} %get-tuple-element.18), channel_id=1, source_target_pairs={{0,1},{1,0},{2,3},{3,2},{4,5},{5,4},{6,7},{7,6},{8,9},{9,8},{10,11... | collective-permute-start | bytes 393224 | tf_op jit(solution)/shard_map/ppermute | solution.py:35
  10.8 0.0 collective-permute-done.6
  10.8 0.9 %collective-permute-start.7 = (bf16[16,4096]{1,0:T(8,128)(2,1)S(1)}, bf16[16,4096]{1,0:T(8,128)(2,1)S(1)}, u32[]{:S(2)}, u32[]{:S(2)}) collective-permute-start(bf16[16,4096]{1,0:T(8,128)(2,1)S(1)} %collective-permute-done.6), channel_id=1, source_target_pairs={{0,3},{1,2},{2,1},{3,0},{4,7},{5,6},{6,5},{7,4},{8,11},{9,10},{10,... | collective-permute-start | bytes 393224 | tf_op jit(solution)/shard_map/ppermute | solution.py:45
  11.8 0.0 collective-permute-done.theirs
  11.8 0.7 %collective-permute-start.1 = (bf16[8,2176]{1,0:T(8,128)(2,1)S(1)}, bf16[8,2176]{1,0:T(8,128)(2,1)S(1)}, u32[]{:S(2)}, u32[]{:S(2)}) collective-permute-start(bf16[8,2176]{1,0:T(8,128)(2,1)S(1)} %get-tuple-element.14), channel_id=1, source_target_pairs={{0,1},{1,0},{2,3},{3,2},{4,5},{5,4},{6,7},{7,6},{8,9},{9,8},{10,11... | collective-permute-start | bytes 104456 | tf_op jit(solution)/shard_map/ppermute | solution.py:35
  12.6 17.5 %collective-permute-done.1.refs_0_ = bf16[8,2176]{1,0:T(8,128)(2,1)S(1)} collective-permute-done((bf16[8,2176]{1,0:T(8,128)(2,1)S(1)}, bf16[8,2176]{1,0:T(8,128)(2,1)S(1)}, u32[]{:S(2)}, u32[]{:S(2)}) %collective-permute-start.1) | collective-permute-done | bytes 34848 | tf_op jit(solution)/shard_map/ppermute | solution.py:35
  30.0 1.7 %collective-permute-start.3 = (f32[2,8,128]{2,1,0:T(8,128)S(1)}, f32[2,8,128]{2,1,0:T(8,128)S(1)}, u32[]{:S(2)}, u32[]{:S(2)}) collective-permute-start(f32[2,8,128]{2,1,0:T(8,128)S(1)} %unpack.1), channel_id=1, source_target_pairs={{0,4},{2,6},{4,0},{6,2},{8,12},{10,14},{12,8},{14,10},{16,20},{18,... | collective-permute-start | bytes 24584 | tf_op jit(solution)/shard_map/ppermute | solution.py:26
  31.7 1.9 %collective-permute-done.3 = f32[2,8,128]{2,1,0:T(8,128)S(1)} collective-permute-done((f32[2,8,128]{2,1,0:T(8,128)S(1)}, f32[2,8,128]{2,1,0:T(8,128)S(1)}, u32[]{:S(2)}, u32[]{:S(2)}) %collective-permute-start.3) | collective-permute-done | bytes 8224 | tf_op jit(solution)/shard_map/ppermute | solution.py:26
  33.7 1.8 %collective-permute-start.4 = (f32[2,8,128]{2,1,0:T(8,128)S(1)}, f32[2,8,128]{2,1,0:T(8,128)S(1)}, u32[]{:S(2)}, u32[]{:S(2)}) collective-permute-start(f32[2,8,128]{2,1,0:T(8,128)S(1)} %add.9), channel_id=1, source_target_pairs={{0,8},{2,10},{4,12},{6,14},{8,0},{10,2},{12,4},{14,6},{16,24},{18,... | collective-permute-start | bytes 24584 | tf_op jit(solution)/shard_map/ppermute | solution.py:26
  35.5 1.9 %collective-permute-done.4 = f32[2,8,128]{2,1,0:T(8,128)S(1)} collective-permute-done((f32[2,8,128]{2,1,0:T(8,128)S(1)}, f32[2,8,128]{2,1,0:T(8,128)S(1)}, u32[]{:S(2)}, u32[]{:S(2)}) %collective-permute-start.4) | collective-permute-done | bytes 8224 | tf_op jit(solution)/shard_map/ppermute | solution.py:26
  37.3 2.8 %collective-permute-start.5 = (f32[2,8,128]{2,1,0:T(8,128)S(1)}, f32[2,8,128]{2,1,0:T(8,128)S(1)}, u32[]{:S(2)}, u32[]{:S(2)}) collective-permute-start(f32[2,8,128]{2,1,0:T(8,128)S(1)} %add.10), channel_id=1, source_target_pairs={{0,16},{2,18},{4,20},{6,22},{8,24},{10,26},{12,28},{14,30},{16,0},... | collective-permute-start | bytes 24584 | tf_op jit(solution)/shard_map/ppermute | solution.py:26
  40.2 1.7 %collective-permute-done.5 = f32[2,8,128]{2,1,0:T(8,128)S(1)} collective-permute-done((f32[2,8,128]{2,1,0:T(8,128)S(1)}, f32[2,8,128]{2,1,0:T(8,128)S(1)}, u32[]{:S(2)}, u32[]{:S(2)}) %collective-permute-start.5) | collective-permute-done | bytes 8224 | tf_op jit(solution)/shard_map/ppermute | solution.py:26
  41.9 1.6 %masks.3.own = bf16[4,16,8192]{2,1,0:T(8,128)(2,1)S(1)} custom-call(s32[1,4,8]{2,1,0:T(4,128)} %limits.7, s32[1,4,16,16384]{3,2,1,0:T(8,128)} %scores.7, bf16[4,16,16384]{2,1,0:T(8,128)(2,1)S(1)} %get-tuple-element.16.copied), custom_call_target="tpu_custom_call" | custom-call | flops 10000000 | bytes 3145728 | tf_op jit(solution)/shard_map/masks/pallas_call | solution.py:349
  43.6 0.0 collective-permute-done.2.refs_1_
  43.6 0.2 scale.1.scales
  43.9 1.2 %merge.2.refs_1_ = bf16[4,16,8192]{2,1,0:T(8,128)(2,1)} custom-call(f32[2,8,4096]{2,1,0:T(8,128)S(1)} %scale.1.scales, bf16[4,16,8192]{2,1,0:T(8,128)(2,1)S(1)} %masks.3.own, bf16[16,8192]{1,0:T(8,128)(2,1)S(1)} %collective-permute-done.8.refs_0_, bf16[16,16384]{1,0:T(8,128)(2,1)S(1)} %collective-permute-done.9.refs_1_, ...), custom_call_target="tpu_custom_call" | custom-call | flops 1000000 | bytes 2752512 | tf_op jit(solution)/shard_map/merge/pallas_call | solution.py:429
  45.0 0.7 %merge.3 = bf16[4,16,8192]{2,1,0:T(8,128)(2,1)} custom-call(f32[2,8,4096]{2,1,0:T(8,128)S(1)} %scale.1.scales, bf16[4,16,8192]{2,1,0:T(8,128)(2,1)S(1)} %masks.3.own, bf16[16,4096]{1,0:T(8,128)(2,1)S(1)} %collective-permute-done.7.refs_0_, bf16[4,16,8192]{2,1,0:T(8,128)(2,1)} %merge.2.refs_1_), custom_call_target="tpu_custom_call", output_to_operand_aliasing={{}: (3, {})} | custom-call | flops 1000000 | bytes 393216 | tf_op jit(solution)/shard_map/merge/pallas_call | solution.py:429
  (12 shorter events, 0.1 us)
Async XLA Ops:
  3.1 40.8 %collective-permute-start.9 = (bf16[16,16384]{1,0:T(8,128)(2,1)S(1)}, bf16[16,16384]{1,0:T(8,128)(2,1)S(1)}, u32[]{:S(2)}, u32[]{:S(2)}) collective-permute-start(bf16[16,16384]{1,0:T(8,128)(2,1)S(1)} %masks.5), channel_id=1, source_target_pairs={{0,1},{1,0},{2,3},{3,2},{4,5},{5,4},{6,7},{7,6},{8,9},{9,8},{10,11... | collective-permute-start | bytes 1572872 | tf_op jit(solution)/shard_map/ppermute | solution.py:35
  6.1 5.6 %collective-permute-start = (f32[2,8,4224]{2,1,0:T(8,128)S(1)}, f32[2,8,4224]{2,1,0:T(8,128)S(1)}, u32[]{:S(2)}, u32[]{:S(2)}) collective-permute-start(f32[2,8,4224]{2,1,0:T(8,128)S(1)} %get-tuple-element.12.mine), channel_id=1, source_target_pairs={{0,2},{2,0},{4,6},{6,4},{8,10},{10,8},{12,14},{14,12},{16,18},{18,... | collective-permute-start | bytes 811016 | tf_op jit(solution)/shard_map/ppermute | solution.py:26
  7.3 36.5 %collective-permute-start.8 = (bf16[16,8192]{1,0:T(8,128)(2,1)S(1)}, bf16[16,8192]{1,0:T(8,128)(2,1)S(1)}, u32[]{:S(2)}, u32[]{:S(2)}) collective-permute-start(bf16[16,8192]{1,0:T(8,128)(2,1)S(1)} %first.1), channel_id=1, source_target_pairs={{0,1},{1,0},{2,3},{3,2},{4,5},{5,4},{6,7},{7,6},{8,9},{9,8},{10,11... | collective-permute-start | bytes 786440 | tf_op jit(solution)/shard_map/ppermute | solution.py:35
  8.6 2.2 %collective-permute-start.6 = (bf16[16,4096]{1,0:T(8,128)(2,1)S(1)}, bf16[16,4096]{1,0:T(8,128)(2,1)S(1)}, u32[]{:S(2)}, u32[]{:S(2)}) collective-permute-start(bf16[16,4096]{1,0:T(8,128)(2,1)S(1)} %get-tuple-element.17), channel_id=1, source_target_pairs={{0,2},{2,0},{4,6},{6,4},{8,10},{10,8},{12,14},{14,12},{16,18},{18,... | collective-permute-start | bytes 393224 | tf_op jit(solution)/shard_map/ppermute | solution.py:26
  9.1 34.7 %collective-permute-start.10 = (bf16[16,4096]{1,0:T(8,128)(2,1)S(1)}, bf16[16,4096]{1,0:T(8,128)(2,1)S(1)}, u32[]{:S(2)}, u32[]{:S(2)}) collective-permute-start(bf16[16,4096]{1,0:T(8,128)(2,1)S(1)} %get-tuple-element.18), channel_id=1, source_target_pairs={{0,1},{1,0},{2,3},{3,2},{4,5},{5,4},{6,7},{7,6},{8,9},{9,8},{10,11... | collective-permute-start | bytes 393224 | tf_op jit(solution)/shard_map/ppermute | solution.py:35
  10.8 34.2 %collective-permute-start.7 = (bf16[16,4096]{1,0:T(8,128)(2,1)S(1)}, bf16[16,4096]{1,0:T(8,128)(2,1)S(1)}, u32[]{:S(2)}, u32[]{:S(2)}) collective-permute-start(bf16[16,4096]{1,0:T(8,128)(2,1)S(1)} %collective-permute-done.6), channel_id=1, source_target_pairs={{0,3},{1,2},{2,1},{3,0},{4,7},{5,6},{6,5},{7,4},{8,11},{9,10},{10,... | collective-permute-start | bytes 393224 | tf_op jit(solution)/shard_map/ppermute | solution.py:45
  11.8 18.2 %collective-permute-start.1 = (bf16[8,2176]{1,0:T(8,128)(2,1)S(1)}, bf16[8,2176]{1,0:T(8,128)(2,1)S(1)}, u32[]{:S(2)}, u32[]{:S(2)}) collective-permute-start(bf16[8,2176]{1,0:T(8,128)(2,1)S(1)} %get-tuple-element.14), channel_id=1, source_target_pairs={{0,1},{1,0},{2,3},{3,2},{4,5},{5,4},{6,7},{7,6},{8,9},{9,8},{10,11... | collective-permute-start | bytes 104456 | tf_op jit(solution)/shard_map/ppermute | solution.py:35
  30.0 3.7 %collective-permute-start.3 = (f32[2,8,128]{2,1,0:T(8,128)S(1)}, f32[2,8,128]{2,1,0:T(8,128)S(1)}, u32[]{:S(2)}, u32[]{:S(2)}) collective-permute-start(f32[2,8,128]{2,1,0:T(8,128)S(1)} %unpack.1), channel_id=1, source_target_pairs={{0,4},{2,6},{4,0},{6,2},{8,12},{10,14},{12,8},{14,10},{16,20},{18,... | collective-permute-start | bytes 24584 | tf_op jit(solution)/shard_map/ppermute | solution.py:26
  33.7 3.7 %collective-permute-start.4 = (f32[2,8,128]{2,1,0:T(8,128)S(1)}, f32[2,8,128]{2,1,0:T(8,128)S(1)}, u32[]{:S(2)}, u32[]{:S(2)}) collective-permute-start(f32[2,8,128]{2,1,0:T(8,128)S(1)} %add.9), channel_id=1, source_target_pairs={{0,8},{2,10},{4,12},{6,14},{8,0},{10,2},{12,4},{14,6},{16,24},{18,... | collective-permute-start | bytes 24584 | tf_op jit(solution)/shard_map/ppermute | solution.py:26
  37.3 4.5 %collective-permute-start.5 = (f32[2,8,128]{2,1,0:T(8,128)S(1)}, f32[2,8,128]{2,1,0:T(8,128)S(1)}, u32[]{:S(2)}, u32[]{:S(2)}) collective-permute-start(f32[2,8,128]{2,1,0:T(8,128)S(1)} %add.10), channel_id=1, source_target_pairs={{0,16},{2,18},{4,20},{6,22},{8,24},{10,26},{12,28},{14,30},{16,0},... | collective-permute-start | bytes 24584 | tf_op jit(solution)/shard_map/ppermute | solution.py:26
  41.9 1.7 %collective-permute-start.2 = (bf16[8,2176]{1,0:T(8,128)(2,1)S(1)}, bf16[8,2176]{1,0:T(8,128)(2,1)S(1)}, u32[]{:S(2)}, u32[]{:S(2)}) collective-permute-start(bf16[8,2176]{1,0:T(8,128)(2,1)S(1)} %collective-permute-done.1.refs_0_), channel_id=1, source_target_pairs={{0,2},{2,0},{4,6},{6,4},{8,10},{10,8},{12,14},{14,12},{16,18},{18,... | collective-permute-start | bytes 104456 | tf_op jit(solution)/shard_map/ppermute | solution.py:26
